TPU v7x, 32 devices: a whole 2x2x4 slice. The times are simulated.
32 devices in a mesh: pair: 2 (over x), seq: 8 (over z, y), head: 2 (over core).
Axes of the slice: x: 2, y: 2, z: 4, core: 2. Of those that a mesh axis runs over, the one named last changes fastest.
Arguments:
- queries: bfloat16 [2, 512, 2, 3584], P('pair', 'seq', None, 'head'), may hold values from -6 to 6
- answer_keys: bfloat16 [2, 512, 2, 512], P('pair', 'seq', None, 'head'), may hold values from -6 to 6
- answer_values: bfloat16 [2, 512, 2, 512], P('pair', 'seq', None, 'head'), may hold values from -6 to 6
- prefix_keys: bfloat16 [768, 512], P(('pair', 'seq'), 'head'), may hold values from -8 to 8
- prefix_values: bfloat16 [768, 512], P(('pair', 'seq'), 'head'), may hold values from -6 to 6
- grad_out: bfloat16 [2, 512, 2, 3584], P('pair', 'seq', None, 'head'), may hold values from -6 to 6
- answer_length: int32 [2, 2], P('pair'), may hold values from 128 to 512
- prefix_limit: int32 [2, 2], P('pair'), may hold values from 384 to 768
Outputs:
- attention_out: bfloat16 [2, 512, 2, 3584], P('pair', 'seq', None, 'head')
- grad_queries: bfloat16 [2, 512, 2, 3584], P('pair', 'seq', None, 'head')
- grad_answer_keys: bfloat16 [2, 512, 2, 512], P('pair', 'seq', None, 'head')
- grad_answer_values: bfloat16 [2, 512, 2, 512], P('pair', 'seq', None, 'head')
- grad_prefix_keys: float32 [768, 512], P(('pair', 'seq'), 'head')
- grad_prefix_values: float32 [768, 512], P(('pair', 'seq'), 'head')
All inputs are finite; a program needn't handle non-finite values.
Results may differ from a plain program's by a relative error of at most 0.015.
Values may be sent and summed in bfloat16 or wider, within the bound.
No kernel may reach another device: no remote copies, remote signals or barrier semaphores. Data moves between devices by JAX's collectives and lax.ppermute only.
A program may use at most 64 MiB of HBM per device.

v0:
```python
import math

import jax
import jax.numpy as jnp
from jax import lax
from jax.experimental import pallas as pl
from jax.experimental.pallas import tpu as pltpu
from jax.sharding import PartitionSpec as P


HEAD_DIM = 128
NEGATIVE = -1e30
LOG2E = math.log2(math.e)

f32 = jnp.float32
bf16 = jnp.bfloat16
CHUNK = 32


def mm(a, b):
    return jnp.dot(a, b, preferred_element_type=f32)


def mm_nt(a, b):
    return lax.dot_general(a, b, (((1,), (1,)), ((), ())), preferred_element_type=f32)


def mm_tn(a, b):
    return lax.dot_general(a, b, (((0,), (0,)), ((), ())), preferred_element_type=f32)


def params(cells):
    limit = 24 if cells <= 2**20 else 60
    return pltpu.CompilerParams(
        dimension_semantics=("arbitrary",), vmem_limit_bytes=limit * 1024 * 1024
    )


def cost(flops, moved, exps):
    return pl.CostEstimate(flops=flops, bytes_accessed=moved, transcendentals=exps)


def place_prefix(refs, k_s, v_s):
    rows = refs[0].shape[-2]
    at = 0
    for ref in refs:
        for dz in range(ref.shape[0]):
            k_s[at : at + rows, :] = ref[dz, 0]
            if v_s is not None:
                v_s[at : at + rows, 0:HEAD_DIM] = ref[dz, 1]
            at += rows


def place_answer(refs, k_s, v_s):
    rows = refs[0].shape[-2]
    for t, ref in enumerate(refs):
        for b in range(ref.shape[1]):
            k_s[b, t * rows : (t + 1) * rows, :] = ref[0, b]
            v_s[b, t * rows : (t + 1) * rows, 0:HEAD_DIM] = ref[1, b]


def lanes(ref, here, update):
    for j in range(ref.shape[-1] // HEAD_DIM):
        columns = slice(j * HEAD_DIM, (j + 1) * HEAD_DIM)
        ref[0, here, columns] = update(columns)


def exponents(p_ref, s_s, m_s, first, rows):
    factor = HEAD_DIM ** (-0.5) * LOG2E

    def step(i, carry):
        here = pl.ds(pl.multiple_of(first + i * CHUNK, CHUNK), CHUNK)
        top = m_s(here)
        lanes(p_ref, here, lambda c: jnp.exp2(s_s[here, c] * factor - top).astype(bf16))
        return carry

    lax.fori_loop(0, rows // CHUNK, step, 0, unroll=7)


def blocks(total, rows, columns):
    size = total if total * columns <= 2**19 else rows
    return [slice(a, a + size) for a in range(0, total, size)]


def row_top(s):
    factor = HEAD_DIM ** (-0.5) * LOG2E
    top = jnp.max(s, axis=1, keepdims=True) * factor
    return jnp.broadcast_to(top, (s.shape[0], HEAD_DIM))


def score_grads(ds_s, p, dp, delta):
    for j in range(ds_s.shape[-1] // HEAD_DIM):
        columns = slice(j * HEAD_DIM, (j + 1) * HEAD_DIM)
        ds_s[:, columns] = (p[:, columns].astype(f32) * (dp[:, columns] - delta)).astype(bf16)


def prefix_forward_body(
    bias_ref, q_ref, pa_ref, pb_ref, pc_ref, pd_ref, p_ref, ol_ref, m_ref, k_s, v_s, s_s
):
    batch = bias_ref.shape[0]
    total = q_ref.shape[1]
    per = total // batch
    place_prefix((pa_ref, pb_ref, pc_ref, pd_ref), k_s, v_s)
    v_s[:, HEAD_DIM:] = jnp.ones((v_s.shape[0], HEAD_DIM), bf16)
    for b in range(batch):
        for part in blocks(per, 64, k_s.shape[0]):
            rows = slice(b * per + part.start, b * per + part.stop)
            s = mm_nt(q_ref[0, rows, :], k_s[...]) + bias_ref[b, 0:1, :]
            s_s[rows, :] = s
            m_ref[0, rows, :] = row_top(s)
    for b in range(batch):
        rows = slice(b * per, (b + 1) * per)
        exponents(p_ref, s_s, lambda here: m_ref[0, here, :], b * per, per)
        ol_ref[0, rows, :] = mm(p_ref[0, rows, :], v_s[...])


def middle_body(
    pieces,
    live_ref,
    bias_ref,
    q_ref,
    do_ref,
    p_ref,
    ol_ref,
    m_ref,
    *rest,
):
    prefix = rest[:4]
    answer = rest[4 : 4 + pieces]
    (
        out_ref,
        pb_ref,
        dob_ref,
        deltab_ref,
        ds_ref,
        own_ref,
        near_ref,
        far_ref,
        k_s,
        v_s,
        s_s,
        ka_s,
        va_s,
        olb_s,
        mb_s,
        doa_s,
        deltaa_s,
    ) = rest[4 + pieces :]
    scale = HEAD_DIM ** (-0.5)
    batch = ka_s.shape[0]
    keys = ka_s.shape[1]
    rows = bias_ref.shape[0]
    total = q_ref.shape[1]
    per = total // batch
    groups = per // rows
    place_answer(answer, ka_s, va_s)
    va_s[:, :, HEAD_DIM:] = jnp.ones((batch, keys, HEAD_DIM), bf16)
    place_prefix(prefix, k_s, v_s)
    for b in range(batch):
        for part in blocks(per, rows, keys):
            base = b * per + part.start
            size = part.stop - part.start
            scores = mm_nt(q_ref[0, base : base + size, :], ka_s[b])
            for g in range(size // rows):
                span = slice(base + g * rows, base + (g + 1) * rows)
                s = scores[g * rows : (g + 1) * rows, :] + bias_ref[...]
                s_s[span, :] = s
                mb_s[span, :] = row_top(s)
    for b in range(batch):
        exponents(pb_ref, s_s, lambda here: mb_s[here, :], b * per, per)
        olb_s[b * per : (b + 1) * per, :] = mm(pb_ref[0, b * per : (b + 1) * per, :], va_s[b])

    for b in range(batch):

        def combine(i, carry, b=b):
            here = pl.ds(pl.multiple_of(b * per + i * rows, rows), rows)
            live = live_ref[b]
            ma = m_ref[0, here, :]
            mb = mb_s[here, :]
            top = jnp.maximum(ma, mb)
            ea = jnp.exp2(ma - top)
            eb = jnp.exp2(mb - top)
            inverse = 1.0 / (
                ol_ref[0, here, HEAD_DIM:] * ea + olb_s[here, HEAD_DIM:] * eb
            )
            ea = ea * inverse
            eb = eb * inverse
            attended = (ol_ref[0, here, 0:HEAD_DIM] * ea + olb_s[here, 0:HEAD_DIM] * eb) * live
            out_ref[0, here, :] = attended.astype(bf16)
            douts = do_ref[0, here, :].astype(f32) * live
            da = (douts * ea).astype(bf16)
            db = (douts * eb).astype(bf16)
            doa_s[here, :] = da
            dob_ref[0, here, :] = db
            deltaa_s[here, :] = jnp.broadcast_to(
                jnp.sum(da.astype(f32) * attended, axis=1, keepdims=True), (rows, HEAD_DIM)
            )
            deltab_ref[0, here, :] = jnp.broadcast_to(
                jnp.sum(db.astype(f32) * attended, axis=1, keepdims=True), (rows, HEAD_DIM)
            )
            return carry

        lax.fori_loop(0, groups, combine, 0, unroll=groups)
    for span in blocks(total, per if per * k_s.shape[0] <= 2**19 else rows, k_s.shape[0]):
        dp = mm_nt(doa_s[span, :], v_s[...])
        score_grads(ds_ref.at[0, span], p_ref[0, span, :], dp, deltaa_s[span, :])
    half = own_ref.shape[1]
    quarter = half // 2
    value_term = jnp.transpose(mm_tn(doa_s[...], p_ref[0])).astype(bf16)
    key_term = (jnp.transpose(mm_tn(q_ref[0], ds_ref[0])) * scale).astype(bf16)
    for t, term in ((0, key_term), (1, value_term)):
        own_ref[t] = term[:half]
        near_ref[t] = term[half : half + quarter]
        far_ref[t] = term[half + quarter :]


def answer_backward_body(
    pieces, q_ref, ds_ref, pb_ref, dob_ref, deltab_ref, *rest
):
    prefix = rest[:4]
    rest = rest[4:]
    answer = rest[:pieces]
    dq_ref = rest[pieces]
    grads = rest[pieces + 1 : 2 * pieces + 1]
    k_s, ka_s, va_s, dsb_s = rest[2 * pieces + 1 :]
    scale = HEAD_DIM ** (-0.5)
    batch = ka_s.shape[0]
    total = q_ref.shape[1]
    per = total // batch
    piece_rows = answer[0].shape[-2]
    place_answer(answer, ka_s, va_s)
    place_prefix(prefix, k_s, None)
    for b in range(batch):
        for part in blocks(per, 64, ka_s.shape[1]):
            rows = slice(b * per + part.start, b * per + part.stop)
            dp = mm_nt(dob_ref[0, rows, :], va_s[b])
            score_grads(dsb_s.at[rows], pb_ref[0, rows, :], dp, deltab_ref[0, rows, :])
    for b in range(batch):
        rows = slice(b * per, (b + 1) * per)
        key_term = (jnp.transpose(mm_tn(q_ref[0, rows, :], dsb_s[rows, :])) * scale).astype(bf16)
        value_term = jnp.transpose(mm_tn(dob_ref[0, rows, :], pb_ref[0, rows, :])).astype(bf16)
        for t, ref in enumerate(grads):
            span = slice(t * piece_rows, (t + 1) * piece_rows)
            ref[0, b] = key_term[span]
            ref[1, b] = value_term[span]
    for b in range(batch):
        rows = slice(b * per, (b + 1) * per)
        dq = mm(ds_ref[0, rows, :], k_s[...]) + mm(dsb_s[rows, :], ka_s[b])
        dq_ref[0, rows, :] = (dq * scale).astype(bf16)


def on_device(
    queries,
    answer_keys,
    answer_values,
    prefix_keys,
    prefix_values,
    grad_out,
    answer_length,
    prefix_limit,
):
    size = lax.axis_size("seq")
    sides = lax.axis_size("pair")
    assert sides == 2 and size % 2 == 0
    outer = size // 2
    rows = queries.shape[1]
    batch = queries.shape[2]
    kv = answer_keys.shape[3] // HEAD_DIM
    group = queries.shape[3] // HEAD_DIM // kv
    per = group * rows
    total = batch * per
    prefix_rows = prefix_keys.shape[0]
    prefix_total = prefix_rows * size * sides
    answer_total = rows * size
    place = lax.axis_index("seq")
    side = lax.axis_index("pair")
    z, y = place // 2, place % 2

    def shift_z(x, k):
        return lax.ppermute(x, "seq", [(i, (i + 2 * k) % size) for i in range(size)])

    def swap_y(x):
        return lax.ppermute(x, "seq", [(i, i ^ 1) for i in range(size)])

    def swap_x(x):
        return lax.ppermute(x, "pair", [(0, 1), (1, 0)])

    prefix_own = jnp.stack([prefix_keys, prefix_values])
    answer_own = jnp.stack([a[0].transpose(1, 0, 2) for a in (answer_keys, answer_values)])
    prefix_z = jnp.stack([prefix_own] + [shift_z(prefix_own, k) for k in range(1, outer)])
    prefix_y = swap_y(prefix_z)
    prefix = [prefix_z, prefix_y, swap_x(prefix_z), swap_x(prefix_y)]
    near = [answer_own] + [shift_z(answer_own, k) for k in range(1, outer)]
    far = [swap_y(piece) for piece in near]
    answer = near + far
    pieces = len(answer)

    dz = jnp.arange(outer, dtype=jnp.int32)
    z_from = (z - dz) % outer
    pair_from = (side + jnp.arange(2, dtype=jnp.int32)) % 2
    y_from = (y + jnp.arange(2, dtype=jnp.int32)) % 2
    seq_from = z_from[None, :] * 2 + y_from[:, None]
    shard = pair_from[:, None, None] * size + seq_from[None]
    spots = (
        shard[..., None] * prefix_rows + jnp.arange(prefix_rows, dtype=jnp.int32)
    ).reshape(prefix_total)
    prefix_bias = jnp.where(spots[None, None, :] < prefix_limit[0][:, None, None], 0.0, NEGATIVE)
    prefix_bias = jnp.broadcast_to(prefix_bias, (batch, 8, prefix_total)).astype(f32)
    row_places = place * rows + jnp.arange(rows, dtype=jnp.int32)
    key_places = (
        seq_from[..., None] * rows + jnp.arange(rows, dtype=jnp.int32)
    ).reshape(answer_total)
    answer_bias = jnp.where(key_places[None, :] <= row_places[:, None], 0.0, NEGATIVE).astype(f32)
    live = jnp.where(row_places[None, :] < answer_length[0][:, None], 1.0, 0.0).astype(f32)
    live = jnp.broadcast_to(live[:, :, None], (batch, rows, HEAD_DIM))

    def head_major(x):
        x = x[0].reshape(rows, batch, kv, group, HEAD_DIM)
        return x.transpose(2, 1, 3, 0, 4).reshape(kv, total, HEAD_DIM)

    def row_major(x):
        x = x.reshape(kv, batch, group, rows, HEAD_DIM)
        return x.transpose(3, 1, 0, 2, 4).reshape(queries.shape)

    query_view = head_major(queries)
    grad_view = head_major(grad_out)

    def whole(shape):
        return pl.BlockSpec(shape, lambda c: (0,) * len(shape))

    def by_head(shape, axis=0):
        block = tuple(1 if a == axis else n for a, n in enumerate(shape))
        return pl.BlockSpec(block, lambda c: tuple(c if a == axis else 0 for a in range(len(shape))))

    def lane_block(shape):
        last = len(shape) - 1
        return pl.BlockSpec(shape[:-1] + (HEAD_DIM,), lambda c: (0,) * last + (c,))

    q_shape = (kv, total, HEAD_DIM)
    q_spec = by_head(q_shape)
    prefix_specs = [lane_block(prefix_z.shape)] * 4
    answer_spec = lane_block(answer_own.shape)
    pa_shape = (kv, total, prefix_total)
    pb_shape = (kv, total, answer_total)
    ol_shape = (kv, total, 2 * HEAD_DIM)
    own_shape = (2, prefix_total // 2, kv * HEAD_DIM)
    sent_shape = (2, prefix_total // 4, kv * HEAD_DIM)
    unit_a = 2 * kv * total * prefix_total * HEAD_DIM
    unit_b = 2 * kv * total * answer_total * HEAD_DIM

    probs_a, ol_a, top_a = pl.pallas_call(
        prefix_forward_body,
        grid=(kv,),
        in_specs=[whole(prefix_bias.shape), q_spec] + prefix_specs,
        out_specs=[by_head(pa_shape), by_head(ol_shape), q_spec],
        out_shape=[
            jax.ShapeDtypeStruct(pa_shape, bf16),
            jax.ShapeDtypeStruct(ol_shape, f32),
            jax.ShapeDtypeStruct(q_shape, f32),
        ],
        scratch_shapes=[
            pltpu.VMEM((prefix_total, HEAD_DIM), bf16),
            pltpu.VMEM((prefix_total, 2 * HEAD_DIM), bf16),
            pltpu.VMEM((total, prefix_total), f32),
        ],
        compiler_params=params(total * prefix_total),
        cost_estimate=cost(2 * unit_a, 8 << 20, kv * total * prefix_total),
        name="prefix_forward",
    )(prefix_bias, query_view, *prefix)

    (out_view, probs_b, grad_b, delta_b, ds_a, prefix_own_sum, prefix_near, prefix_far) = (
        pl.pallas_call(
            lambda *refs: middle_body(pieces, *refs),
            grid=(kv,),
            in_specs=[
                whole(live.shape),
                whole(answer_bias.shape),
                q_spec,
                q_spec,
                by_head(pa_shape),
                by_head(ol_shape),
                q_spec,
            ]
            + prefix_specs
            + [answer_spec] * pieces,
            out_specs=[
                q_spec,
                by_head(pb_shape),
                q_spec,
                q_spec,
                by_head(pa_shape),
                lane_block(own_shape),
                lane_block(sent_shape),
                lane_block(sent_shape),
            ],
            out_shape=[
                jax.ShapeDtypeStruct(q_shape, bf16),
                jax.ShapeDtypeStruct(pb_shape, bf16),
                jax.ShapeDtypeStruct(q_shape, bf16),
                jax.ShapeDtypeStruct(q_shape, f32),
                jax.ShapeDtypeStruct(pa_shape, bf16),
                jax.ShapeDtypeStruct(own_shape, bf16),
                jax.ShapeDtypeStruct(sent_shape, bf16),
                jax.ShapeDtypeStruct(sent_shape, bf16),
            ],
            scratch_shapes=[
                pltpu.VMEM((prefix_total, HEAD_DIM), bf16),
                pltpu.VMEM((prefix_total, HEAD_DIM), bf16),
                pltpu.VMEM((total, answer_total), f32),
                pltpu.VMEM((batch, answer_total, HEAD_DIM), bf16),
                pltpu.VMEM((batch, answer_total, 2 * HEAD_DIM), bf16),
                pltpu.VMEM((total, 2 * HEAD_DIM), f32),
                pltpu.VMEM((total, HEAD_DIM), f32),
                pltpu.VMEM((total, HEAD_DIM), bf16),
                pltpu.VMEM((total, HEAD_DIM), f32),
            ],
            compiler_params=params(total * prefix_total),
            cost_estimate=cost(2 * unit_b + 3 * unit_a, 12 << 20, kv * total * answer_total),
            name="middle",
        )(
            live,
            answer_bias,
            query_view,
            grad_view,
            probs_a,
            ol_a,
            top_a,
            *prefix,
            *answer,
        )
    )

    dq_view, *answer_grads = pl.pallas_call(
        lambda *refs: answer_backward_body(pieces, *refs),
        grid=(kv,),
        in_specs=[q_spec, by_head(pa_shape), by_head(pb_shape), q_spec, q_spec]
        + prefix_specs
        + [answer_spec] * pieces,
        out_specs=[q_spec] + [answer_spec] * pieces,
        out_shape=[jax.ShapeDtypeStruct(q_shape, bf16)]
        + [jax.ShapeDtypeStruct(answer_own.shape, bf16)] * pieces,
        scratch_shapes=[
            pltpu.VMEM((prefix_total, HEAD_DIM), bf16),
            pltpu.VMEM((batch, answer_total, HEAD_DIM), bf16),
            pltpu.VMEM((batch, answer_total, HEAD_DIM), bf16),
            pltpu.VMEM((total, answer_total), bf16),
        ],
        compiler_params=params(total * prefix_total),
        cost_estimate=cost(4 * unit_b + unit_a, 8 << 20, 0),
        name="answer_backward",
    )(query_view, ds_a, probs_b, grad_b, delta_b, *prefix, *answer)

    split = (2, outer, prefix_rows, kv * HEAD_DIM)
    half = prefix_total // 4
    far_got = swap_x(prefix_far).astype(f32) + prefix_own_sum[:, half:].astype(f32)
    y_got = swap_y(far_got.astype(bf16)).astype(f32)
    near_got = swap_x(prefix_near).astype(f32) + prefix_own_sum[:, :half].astype(f32)
    z_sum = (near_got + y_got).reshape(split)
    prefix_sum = z_sum[:, 0]
    for k in range(1, outer):
        prefix_sum = prefix_sum + shift_z(z_sum[:, k].astype(bf16), -k).astype(f32)
    answer_sum = None
    for k in reversed(range(outer)):
        got = swap_y(answer_grads[outer + k]).astype(f32)
        piece = answer_grads[k].astype(f32) + got
        if k:
            piece = shift_z(piece.astype(bf16), -k).astype(f32)
        answer_sum = piece if answer_sum is None else answer_sum + piece
    answer_sum = answer_sum.astype(bf16)

    def answer_out(x):
        return x.transpose(1, 0, 2).reshape(answer_keys.shape)

    attention_out = row_major(out_view)
    grad_queries = row_major(dq_view)
    return (
        attention_out,
        grad_queries,
        answer_out(answer_sum[0]),
        answer_out(answer_sum[1]),
        prefix_sum[0],
        prefix_sum[1],
    )


def solution(mesh):
    wide = P("pair", "seq", None, "head")
    shared = P(("pair", "seq"), "head")
    small = P("pair", None)

    return jax.shard_map(
        on_device,
        mesh=mesh,
        in_specs=(wide, wide, wide, shared, shared, wide, small, small),
        out_specs=(wide, wide, wide, wide, shared, shared),
        check_vma=False,
    )
```

profile of v0, /device:TPU:0, one launch (start us, length us, event | category | flops | bytes accessed | tf_op | source)
XLA Modules:
  0.0 79.1 jit_solution(3837968115275951219)
XLA Ops:
  0.6 0.8 %fusion.8 = (bf16[1,2,48,256]{3,2,1,0:T(8,128)(2,1)S(1)}, bf16[2,48,256]{2,1,0:T(8,128)(2,1)S(1)}) fusion(bf16[1,48,256]{2,1,0:T(8,128)(2,1)} %bitcast.85, bf16[1,48,256]{2,1,0:T(8,128)(2,1)} %bitcast.86), kind=kLoop, calls=%fused_computation.47 | loop fusion | flops 24576 | bytes 147456 | tf_op jit(solution)/shard_map/stack | solution.py:290
  1.5 4.1 %collective-permute-start.1 = (bf16[2,48,256]{2,1,0:T(8,128)(2,1)S(1)}, bf16[2,48,256]{2,1,0:T(8,128)(2,1)S(1)}, u32[]{:S(2)}, u32[]{:S(2)}) collective-permute-start(bf16[2,48,256]{2,1,0:T(8,128)(2,1)S(1)} %get-tuple-element.66), channel_id=1, source_target_pairs={{0,8},{2,10},{4,12},{6,14},{8,0},{10,2},{12,4},{14,6},{1,9},{3,11}... | collective-permute-start | bytes 147464 | tf_op jit(solution)/shard_map/ppermute | solution.py:280
  5.6 1.6 %collective-permute-start = (bf16[2,48,256]{2,1,0:T(8,128)(2,1)S(1)}, bf16[2,48,256]{2,1,0:T(8,128)(2,1)S(1)}, u32[]{:S(2)}, u32[]{:S(2)}) collective-permute-start(bf16[2,48,256]{2,1,0:T(8,128)(2,1)S(1)} %get-tuple-element.66), channel_id=1, source_target_pairs={{0,4},{2,6},{4,8},{6,10},{8,12},{10,14},{12,0},{14,2},{1,5},{3,7},... | collective-permute-start | bytes 147464 | tf_op jit(solution)/shard_map/ppermute | solution.py:280
  7.2 2.2 %collective-permute-start.2 = (bf16[2,48,256]{2,1,0:T(8,128)(2,1)S(1)}, bf16[2,48,256]{2,1,0:T(8,128)(2,1)S(1)}, u32[]{:S(2)}, u32[]{:S(2)}) collective-permute-start(bf16[2,48,256]{2,1,0:T(8,128)(2,1)S(1)} %get-tuple-element.66), channel_id=1, source_target_pairs={{0,12},{2,14},{4,0},{6,2},{8,4},{10,6},{12,8},{14,10},{1,13},{3,15... | collective-permute-start | bytes 147464 | tf_op jit(solution)/shard_map/ppermute | solution.py:280
  9.4 0.9 %copy_bitcast_fusion.2 = (bf16[1,2,64,256]{3,2,1,0:T(8,128)(2,1)S(1)}, bf16[1,2,64,256]{3,2,1,0:T(8,128)(2,1)S(1)}) fusion(bf16[1,64,2,256]{3,2,1,0:T(2,128)(2,1)} %param.10, bf16[1,64,2,256]{3,2,1,0:T(2,128)(2,1)} %param.9), kind=kLoop, calls=%fused_computation.17 | loop fusion | bytes 262144 | tf_op jit(solution)/shard_map/stack | solution.py:289
  10.4 1.2 %collective-permute-start.7 = (bf16[2,2,64,256]{3,2,1,0:T(8,128)(2,1)S(1)}, bf16[2,2,64,256]{3,2,1,0:T(8,128)(2,1)S(1)}, u32[]{:S(2)}, u32[]{:S(2)}) collective-permute-start(bf16[2,2,64,256]{3,2,1,0:T(8,128)(2,1)S(1)} %pad_maximum_fusion.1.refs_11_.refs_9_), channel_id=1, source_target_pairs={{0,8},{2,10},{4,12},{6,14},{8,0},{10,2},{12,4},{14,6},{1,9},{3,11}... | collective-permute-start | bytes 393224 | tf_op jit(solution)/shard_map/ppermute | solution.py:280
  12.2 0.8 %collective-permute-start.6 = (bf16[2,2,64,256]{3,2,1,0:T(8,128)(2,1)S(1)}, bf16[2,2,64,256]{3,2,1,0:T(8,128)(2,1)S(1)}, u32[]{:S(2)}, u32[]{:S(2)}) collective-permute-start(bf16[2,2,64,256]{3,2,1,0:T(8,128)(2,1)S(1)} %pad_maximum_fusion.1.refs_11_.refs_9_), channel_id=1, source_target_pairs={{0,4},{2,6},{4,8},{6,10},{8,12},{10,14},{12,0},{14,2},{1,5},{3,7},... | collective-permute-start | bytes 393224 | tf_op jit(solution)/shard_map/ppermute | solution.py:280
  13.1 1.6 %collective-permute-start.4 = (bf16[4,2,48,256]{3,2,1,0:T(8,128)(2,1)S(1)}, bf16[4,2,48,256]{3,2,1,0:T(8,128)(2,1)S(1)}, u32[]{:S(2)}, u32[]{:S(2)}) collective-permute-start(bf16[4,2,48,256]{3,2,1,0:T(8,128)(2,1)S(1)} %pad_maximum_fusion.pa_ref.refs_7_.refs_5_), channel_id=1, source_target_pairs={{0,16},{16,0},{1,17},{17,1},{2,18},{18,2},{3,19},{19,3},{4,20},{20... | collective-permute-start | bytes 589832 | tf_op jit(solution)/shard_map/ppermute | solution.py:286
  14.7 1.5 %collective-permute-start.3 = (bf16[4,2,48,256]{3,2,1,0:T(8,128)(2,1)S(1)}, bf16[4,2,48,256]{3,2,1,0:T(8,128)(2,1)S(1)}, u32[]{:S(2)}, u32[]{:S(2)}) collective-permute-start(bf16[4,2,48,256]{3,2,1,0:T(8,128)(2,1)S(1)} %pad_maximum_fusion.pa_ref.refs_7_.refs_5_), channel_id=1, source_target_pairs={{0,2},{2,0},{4,6},{6,4},{8,10},{10,8},{12,14},{14,12},{1,3},{3,1},... | collective-permute-start | bytes 589832 | tf_op jit(solution)/shard_map/ppermute | solution.py:283
  16.2 0.7 compare_select_fusion.1
  16.9 0.5 collective-permute-start.9
  17.4 5.4 %collective-permute-done.7.refs_13_.refs_11_ = bf16[2,2,64,256]{3,2,1,0:T(8,128)(2,1)S(1)} collective-permute-done((bf16[2,2,64,256]{3,2,1,0:T(8,128)(2,1)S(1)}, bf16[2,2,64,256]{3,2,1,0:T(8,128)(2,1)S(1)}, u32[]{:S(2)}, u32[]{:S(2)}) %collective-permute-start.7) | collective-permute-done | bytes 131104 | tf_op jit(solution)/shard_map/ppermute | solution.py:280
  22.8 1.5 %collective-permute-start.12 = (bf16[2,2,64,256]{3,2,1,0:T(8,128)(2,1)S(1)}, bf16[2,2,64,256]{3,2,1,0:T(8,128)(2,1)S(1)}, u32[]{:S(2)}, u32[]{:S(2)}) collective-permute-start(bf16[2,2,64,256]{3,2,1,0:T(8,128)(2,1)S(1)} %collective-permute-done.8.refs_14_.refs_12_), channel_id=1, source_target_pairs={{0,2},{2,0},{4,6},{6,4},{8,10},{10,8},{12,14},{14,12},{1,3},{3,1},... | collective-permute-start | bytes 393224 | tf_op jit(solution)/shard_map/ppermute | solution.py:283
  24.3 0.5 collective-permute-start.11
  24.9 1.5 %collective-permute-start.10 = (bf16[2,2,64,256]{3,2,1,0:T(8,128)(2,1)S(1)}, bf16[2,2,64,256]{3,2,1,0:T(8,128)(2,1)S(1)}, u32[]{:S(2)}, u32[]{:S(2)}) collective-permute-start(bf16[2,2,64,256]{3,2,1,0:T(8,128)(2,1)S(1)} %collective-permute-done.6.refs_12_.refs_10_), channel_id=1, source_target_pairs={{0,2},{2,0},{4,6},{6,4},{8,10},{10,8},{12,14},{14,12},{1,3},{3,1},... | collective-permute-start | bytes 393224 | tf_op jit(solution)/shard_map/ppermute | solution.py:283
  26.4 1.5 %collective-permute-start.5 = (bf16[4,2,48,256]{3,2,1,0:T(8,128)(2,1)S(1)}, bf16[4,2,48,256]{3,2,1,0:T(8,128)(2,1)S(1)}, u32[]{:S(2)}, u32[]{:S(2)}) collective-permute-start(bf16[4,2,48,256]{3,2,1,0:T(8,128)(2,1)S(1)} %collective-permute-done.3.pb_ref.refs_8_.refs_6_), channel_id=1, source_target_pairs={{0,16},{16,0},{1,17},{17,1},{2,18},{18,2},{3,19},{19,3},{4,20},{20... | collective-permute-start | bytes 589832 | tf_op jit(solution)/shard_map/ppermute | solution.py:286
  27.9 0.7 compare_select_fusion.8
  28.6 1.3 %reshape.261 = bf16[64,2,2,7,128]{4,3,2,1,0:T(8,128)(2,1)S(1)} reshape(bf16[1,64,2,1792]{3,2,1,0:T(2,128)(2,1)} %param.8) | data formatting | bytes 917504 | tf_op jit(solution)/shard_map/reshape;squeeze | solution.py:318
  30.6 1.4 %collective-permute-done.5.pd_ref.refs_10_.refs_8_ = bf16[4,2,48,256]{3,2,1,0:T(8,128)(2,1)S(1)} collective-permute-done((bf16[4,2,48,256]{3,2,1,0:T(8,128)(2,1)S(1)}, bf16[4,2,48,256]{3,2,1,0:T(8,128)(2,1)S(1)}, u32[]{:S(2)}, u32[]{:S(2)}) %collective-permute-start.5) | collective-permute-done | bytes 196640 | tf_op jit(solution)/shard_map/ppermute | solution.py:286
  32.1 4.6 %prefix_forward.1 = (bf16[2,896,768]{2,1,0:T(8,128)(2,1)S(1)}, f32[2,896,256]{2,1,0:T(8,128)S(1)}, f32[2,896,128]{2,1,0:T(8,128)S(1)}) custom-call(f32[2,8,768]{2,1,0:T(8,128)S(1)} %broadcast_in_dim.52.bias_ref, bf16[2,896,128]{2,1,0:T(8,128)(2,1)S(1)} %bitcast.70, bf16[4,2,48,256]{3,2,1,0:T(8,128)(2,1)S(1)} %pad_maximum_fusion.pa_ref.refs_7_.refs_5_, ...), custom_call_target="tpu_custom_call" | custom-call | flops 704643072 | bytes 8388608 | tf_op jit(solution)/shard_map/prefix_forward/pallas_call | solution.py:351
  36.7 6.2 %middle.1 = (bf16[2,896,128]{2,1,0:T(8,128)(2,1)S(1)}, bf16[2,896,512]{2,1,0:T(8,128)(2,1)S(1)}, bf16[2,896,128]{2,1,0:T(8,128)(2,1)S(1)}, f32[2,896,128]{2,1,0:...) custom-call(f32[2,64,128]{2,1,0:T(8,128)S(1)} %broadcast_in_dim.47.r, ...), custom_call_target="tpu_custom_call" | custom-call | flops 1526726656 | bytes 12582912 | tf_op jit(solution)/shard_map/middle/pallas_call | solution.py:372
  43.0 4.0 %answer_backward.1 = (bf16[2,896,128]{2,1,0:T(8,128)(2,1)S(1)}, bf16[2,2,64,256]{3,2,1,0:T(8,128)(2,1)S(1)}, bf16[2,2,64,256]{3,2,1,0:T(8,128)(2,1)S(1)}, bf16[2...) custom-call(bf16[2,896,128]{2,1,0:T(8,128)(2,1)S(1)} %bitcast.72, ...), custom_call_target="tpu_custom_call" | custom-call | flops 1291845632 | bytes 8388608 | tf_op jit(solution)/shard_map/answer_backward/pallas_call | solution.py:433
  47.0 0.6 collective-permute-start.13
  48.0 0.5 reshape.257
  48.5 1.2 %copy.35 = bf16[1,64,2,1792]{3,2,1,0:T(2,128)(2,1)} copy(bf16[1,64,2,1792]{3,1,2,0:T(8,128)(2,1)S(1)} %reshape.257) | data formatting | bytes 917504
  50.0 0.5 reshape.255
  50.5 1.2 %copy.34 = bf16[1,64,2,1792]{3,2,1,0:T(2,128)(2,1)} copy(bf16[1,64,2,1792]{3,1,2,0:T(8,128)(2,1)S(1)} %reshape.255) | data formatting | bytes 917504
  51.8 1.5 %collective-permute-start.15 = (bf16[2,2,64,256]{3,2,1,0:T(8,128)(2,1)S(1)}, bf16[2,2,64,256]{3,2,1,0:T(8,128)(2,1)S(1)}, u32[]{:S(2)}, u32[]{:S(2)}) collective-permute-start(bf16[2,2,64,256]{3,2,1,0:T(8,128)(2,1)S(1)} %copy-done.11), channel_id=1, source_target_pairs={{0,2},{2,0},{4,6},{6,4},{8,10},{10,8},{12,14},{14,12},{1,3},{3,1},... | collective-permute-start | bytes 393224 | tf_op jit(solution)/shard_map/ppermute | solution.py:283
  53.3 0.5 collective-permute-start.17
  53.8 1.5 %collective-permute-start.19 = (bf16[2,2,64,256]{3,2,1,0:T(8,128)(2,1)S(1)}, bf16[2,2,64,256]{3,2,1,0:T(8,128)(2,1)S(1)}, u32[]{:S(2)}, u32[]{:S(2)}) collective-permute-start(bf16[2,2,64,256]{3,2,1,0:T(8,128)(2,1)S(1)} %copy-done.7), channel_id=1, source_target_pairs={{0,2},{2,0},{4,6},{6,4},{8,10},{10,8},{12,14},{14,12},{1,3},{3,1},... | collective-permute-start | bytes 393224 | tf_op jit(solution)/shard_map/ppermute | solution.py:283
  55.3 1.5 %collective-permute-start.20 = (bf16[2,192,256]{2,1,0:T(8,128)(2,1)S(1)}, bf16[2,192,256]{2,1,0:T(8,128)(2,1)S(1)}, u32[]{:S(2)}, u32[]{:S(2)}) collective-permute-start(bf16[2,192,256]{2,1,0:T(8,128)(2,1)S(1)} %copy-done.3), channel_id=1, source_target_pairs={{0,16},{16,0},{1,17},{17,1},{2,18},{18,2},{3,19},{19,3},{4,20},{20... | collective-permute-start | bytes 589832 | tf_op jit(solution)/shard_map/ppermute | solution.py:286
  56.8 0.5 collective-permute-start.21
  57.4 0.4 collective-permute-done.15
  58.1 1.1 %collective-permute-done.17 = bf16[2,2,64,256]{3,2,1,0:T(8,128)(2,1)S(1)} collective-permute-done((bf16[2,2,64,256]{3,2,1,0:T(8,128)(2,1)S(1)}, bf16[2,2,64,256]{3,2,1,0:T(8,128)(2,1)S(1)}, u32[]{:S(2)}, u32[]{:S(2)}) %collective-permute-start.17) | collective-permute-done | bytes 131104 | tf_op jit(solution)/shard_map/ppermute | solution.py:283
  59.2 2.7 %collective-permute-start.16 = (bf16[2,2,64,256]{3,2,1,0:T(8,128)(2,1)S(1)}, bf16[2,2,64,256]{3,2,1,0:T(8,128)(2,1)S(1)}, u32[]{:S(2)}, u32[]{:S(2)}) collective-permute-start(bf16[2,2,64,256]{3,2,1,0:T(8,128)(2,1)S(1)} %add_convert_fusion.3), channel_id=1, source_target_pairs={{0,8},{2,10},{4,12},{6,14},{8,0},{10,2},{12,4},{14,6},{1,9},{3,11}... | collective-permute-start | bytes 393224 | tf_op jit(solution)/shard_map/ppermute | solution.py:280
  62.0 1.1 %collective-permute-done.21 = bf16[2,192,256]{2,1,0:T(8,128)(2,1)S(1)} collective-permute-done((bf16[2,192,256]{2,1,0:T(8,128)(2,1)S(1)}, bf16[2,192,256]{2,1,0:T(8,128)(2,1)S(1)}, u32[]{:S(2)}, u32[]{:S(2)}) %collective-permute-start.21) | collective-permute-done | bytes 196640 | tf_op jit(solution)/shard_map/ppermute | solution.py:286
  63.1 0.9 %collective-permute-start.18 = (bf16[2,2,64,256]{3,2,1,0:T(8,128)(2,1)S(1)}, bf16[2,2,64,256]{3,2,1,0:T(8,128)(2,1)S(1)}, u32[]{:S(2)}, u32[]{:S(2)}) collective-permute-start(bf16[2,2,64,256]{3,2,1,0:T(8,128)(2,1)S(1)} %add_convert_fusion.2), channel_id=1, source_target_pairs={{0,12},{2,14},{4,0},{6,2},{8,4},{10,6},{12,8},{14,10},{1,13},{3,15... | collective-permute-start | bytes 393224 | tf_op jit(solution)/shard_map/ppermute | solution.py:280
  64.1 0.7 collective-permute-start.22
  64.8 0.4 collective-permute-done.14
  65.2 3.3 %collective-permute-done.16 = bf16[2,2,64,256]{3,2,1,0:T(8,128)(2,1)S(1)} collective-permute-done((bf16[2,2,64,256]{3,2,1,0:T(8,128)(2,1)S(1)}, bf16[2,2,64,256]{3,2,1,0:T(8,128)(2,1)S(1)}, u32[]{:S(2)}, u32[]{:S(2)}) %collective-permute-start.16) | collective-permute-done | bytes 131104 | tf_op jit(solution)/shard_map/ppermute | solution.py:280
  68.5 0.4 collective-permute-done.18
  69.0 0.8 %collective-permute-done.22 = bf16[2,192,256]{2,1,0:T(8,128)(2,1)S(1)} collective-permute-done((bf16[2,192,256]{2,1,0:T(8,128)(2,1)S(1)}, bf16[2,192,256]{2,1,0:T(8,128)(2,1)S(1)}, u32[]{:S(2)}, u32[]{:S(2)}) %collective-permute-start.22) | collective-permute-done | bytes 196640 | tf_op jit(solution)/shard_map/ppermute | solution.py:283
  69.9 2.7 %collective-permute-start.23 = (bf16[2,48,256]{2,1,0:T(8,128)(2,1)S(1)}, bf16[2,48,256]{2,1,0:T(8,128)(2,1)S(1)}, u32[]{:S(2)}, u32[]{:S(2)}) collective-permute-start(bf16[2,48,256]{2,1,0:T(8,128)(2,1)S(1)} %get-tuple-element.58), channel_id=1, source_target_pairs={{0,12},{2,14},{4,0},{6,2},{8,4},{10,6},{12,8},{14,10},{1,13},{3,15... | collective-permute-start | bytes 147464 | tf_op jit(solution)/shard_map/ppermute | solution.py:280
  72.6 0.6 collective-permute-start.24
  73.2 0.7 copy.37
  73.9 0.7 copy.36
  74.6 3.8 %collective-permute-done.25 = bf16[2,48,256]{2,1,0:T(8,128)(2,1)S(1)} collective-permute-done((bf16[2,48,256]{2,1,0:T(8,128)(2,1)S(1)}, bf16[2,48,256]{2,1,0:T(8,128)(2,1)S(1)}, u32[]{:S(2)}, u32[]{:S(2)}) %collective-permute-start.25) | collective-permute-done | bytes 49184 | tf_op jit(solution)/shard_map/ppermute | solution.py:280
  78.5 0.6 slice_bitcast_fusion.3
  (74 shorter events, 2.7 us)
Async XLA Ops:
  0.6 29.5 %copy-start.12 = (bf16[1,64,2,1792]{3,2,1,0:T(2,128)(2,1)S(1)}, bf16[1,64,2,1792]{3,2,1,0:T(2,128)(2,1)}, u32[]{:S(2)}) copy-start(bf16[1,64,2,1792]{3,2,1,0:T(2,128)(2,1)} %param.13) | copy-start | bytes 1376260
  1.5 10.8 %collective-permute-start.1 = (bf16[2,48,256]{2,1,0:T(8,128)(2,1)S(1)}, bf16[2,48,256]{2,1,0:T(8,128)(2,1)S(1)}, u32[]{:S(2)}, u32[]{:S(2)}) collective-permute-start(bf16[2,48,256]{2,1,0:T(8,128)(2,1)S(1)} %get-tuple-element.66), channel_id=1, source_target_pairs={{0,8},{2,10},{4,12},{6,14},{8,0},{10,2},{12,4},{14,6},{1,9},{3,11}... | collective-permute-start | bytes 147464 | tf_op jit(solution)/shard_map/ppermute | solution.py:280
  5.6 7.5 %collective-permute-start = (bf16[2,48,256]{2,1,0:T(8,128)(2,1)S(1)}, bf16[2,48,256]{2,1,0:T(8,128)(2,1)S(1)}, u32[]{:S(2)}, u32[]{:S(2)}) collective-permute-start(bf16[2,48,256]{2,1,0:T(8,128)(2,1)S(1)} %get-tuple-element.66), channel_id=1, source_target_pairs={{0,4},{2,6},{4,8},{6,10},{8,12},{10,14},{12,0},{14,2},{1,5},{3,7},... | collective-permute-start | bytes 147464 | tf_op jit(solution)/shard_map/ppermute | solution.py:280
  7.2 5.9 %collective-permute-start.2 = (bf16[2,48,256]{2,1,0:T(8,128)(2,1)S(1)}, bf16[2,48,256]{2,1,0:T(8,128)(2,1)S(1)}, u32[]{:S(2)}, u32[]{:S(2)}) collective-permute-start(bf16[2,48,256]{2,1,0:T(8,128)(2,1)S(1)} %get-tuple-element.66), channel_id=1, source_target_pairs={{0,12},{2,14},{4,0},{6,2},{8,4},{10,6},{12,8},{14,10},{1,13},{3,15... | collective-permute-start | bytes 147464 | tf_op jit(solution)/shard_map/ppermute | solution.py:280
  10.3 6.6 %collective-permute-start.8 = (bf16[2,2,64,256]{3,2,1,0:T(8,128)(2,1)S(1)}, bf16[2,2,64,256]{3,2,1,0:T(8,128)(2,1)S(1)}, u32[]{:S(2)}, u32[]{:S(2)}) collective-permute-start(bf16[2,2,64,256]{3,2,1,0:T(8,128)(2,1)S(1)} %pad_maximum_fusion.1.refs_11_.refs_9_), channel_id=1, source_target_pairs={{0,12},{2,14},{4,0},{6,2},{8,4},{10,6},{12,8},{14,10},{1,13},{3,15... | collective-permute-start | bytes 393224 | tf_op jit(solution)/shard_map/ppermute | solution.py:280
  10.4 12.4 %collective-permute-start.7 = (bf16[2,2,64,256]{3,2,1,0:T(8,128)(2,1)S(1)}, bf16[2,2,64,256]{3,2,1,0:T(8,128)(2,1)S(1)}, u32[]{:S(2)}, u32[]{:S(2)}) collective-permute-start(bf16[2,2,64,256]{3,2,1,0:T(8,128)(2,1)S(1)} %pad_maximum_fusion.1.refs_11_.refs_9_), channel_id=1, source_target_pairs={{0,8},{2,10},{4,12},{6,14},{8,0},{10,2},{12,4},{14,6},{1,9},{3,11}... | collective-permute-start | bytes 393224 | tf_op jit(solution)/shard_map/ppermute | solution.py:280
  12.2 12.1 %collective-permute-start.6 = (bf16[2,2,64,256]{3,2,1,0:T(8,128)(2,1)S(1)}, bf16[2,2,64,256]{3,2,1,0:T(8,128)(2,1)S(1)}, u32[]{:S(2)}, u32[]{:S(2)}) collective-permute-start(bf16[2,2,64,256]{3,2,1,0:T(8,128)(2,1)S(1)} %pad_maximum_fusion.1.refs_11_.refs_9_), channel_id=1, source_target_pairs={{0,4},{2,6},{4,8},{6,10},{8,12},{10,14},{12,0},{14,2},{1,5},{3,7},... | collective-permute-start | bytes 393224 | tf_op jit(solution)/shard_map/ppermute | solution.py:280
  13.1 11.8 %collective-permute-start.4 = (bf16[4,2,48,256]{3,2,1,0:T(8,128)(2,1)S(1)}, bf16[4,2,48,256]{3,2,1,0:T(8,128)(2,1)S(1)}, u32[]{:S(2)}, u32[]{:S(2)}) collective-permute-start(bf16[4,2,48,256]{3,2,1,0:T(8,128)(2,1)S(1)} %pad_maximum_fusion.pa_ref.refs_7_.refs_5_), channel_id=1, source_target_pairs={{0,16},{16,0},{1,17},{17,1},{2,18},{18,2},{3,19},{19,3},{4,20},{20... | collective-permute-start | bytes 589832 | tf_op jit(solution)/shard_map/ppermute | solution.py:286
  14.7 11.7 %collective-permute-start.3 = (bf16[4,2,48,256]{3,2,1,0:T(8,128)(2,1)S(1)}, bf16[4,2,48,256]{3,2,1,0:T(8,128)(2,1)S(1)}, u32[]{:S(2)}, u32[]{:S(2)}) collective-permute-start(bf16[4,2,48,256]{3,2,1,0:T(8,128)(2,1)S(1)} %pad_maximum_fusion.pa_ref.refs_7_.refs_5_), channel_id=1, source_target_pairs={{0,2},{2,0},{4,6},{6,4},{8,10},{10,8},{12,14},{14,12},{1,3},{3,1},... | collective-permute-start | bytes 589832 | tf_op jit(solution)/shard_map/ppermute | solution.py:283
  16.9 19.7 %collective-permute-start.9 = (bf16[2,2,64,256]{3,2,1,0:T(8,128)(2,1)S(1)}, bf16[2,2,64,256]{3,2,1,0:T(8,128)(2,1)S(1)}, u32[]{:S(2)}, u32[]{:S(2)}) collective-permute-start(bf16[2,2,64,256]{3,2,1,0:T(8,128)(2,1)S(1)} %pad_maximum_fusion.1.refs_11_.refs_9_), channel_id=1, source_target_pairs={{0,2},{2,0},{4,6},{6,4},{8,10},{10,8},{12,14},{14,12},{1,3},{3,1},... | collective-permute-start | bytes 393224 | tf_op jit(solution)/shard_map/ppermute | solution.py:283
  22.8 13.8 %collective-permute-start.12 = (bf16[2,2,64,256]{3,2,1,0:T(8,128)(2,1)S(1)}, bf16[2,2,64,256]{3,2,1,0:T(8,128)(2,1)S(1)}, u32[]{:S(2)}, u32[]{:S(2)}) collective-permute-start(bf16[2,2,64,256]{3,2,1,0:T(8,128)(2,1)S(1)} %collective-permute-done.8.refs_14_.refs_12_), channel_id=1, source_target_pairs={{0,2},{2,0},{4,6},{6,4},{8,10},{10,8},{12,14},{14,12},{1,3},{3,1},... | collective-permute-start | bytes 393224 | tf_op jit(solution)/shard_map/ppermute | solution.py:283
  24.3 12.3 %collective-permute-start.11 = (bf16[2,2,64,256]{3,2,1,0:T(8,128)(2,1)S(1)}, bf16[2,2,64,256]{3,2,1,0:T(8,128)(2,1)S(1)}, u32[]{:S(2)}, u32[]{:S(2)}) collective-permute-start(bf16[2,2,64,256]{3,2,1,0:T(8,128)(2,1)S(1)} %collective-permute-done.7.refs_13_.refs_11_), channel_id=1, source_target_pairs={{0,2},{2,0},{4,6},{6,4},{8,10},{10,8},{12,14},{14,12},{1,3},{3,1},... | collective-permute-start | bytes 393224 | tf_op jit(solution)/shard_map/ppermute | solution.py:283
  24.9 11.8 %collective-permute-start.10 = (bf16[2,2,64,256]{3,2,1,0:T(8,128)(2,1)S(1)}, bf16[2,2,64,256]{3,2,1,0:T(8,128)(2,1)S(1)}, u32[]{:S(2)}, u32[]{:S(2)}) collective-permute-start(bf16[2,2,64,256]{3,2,1,0:T(8,128)(2,1)S(1)} %collective-permute-done.6.refs_12_.refs_10_), channel_id=1, source_target_pairs={{0,2},{2,0},{4,6},{6,4},{8,10},{10,8},{12,14},{14,12},{1,3},{3,1},... | collective-permute-start | bytes 393224 | tf_op jit(solution)/shard_map/ppermute | solution.py:283
  26.4 5.7 %collective-permute-start.5 = (bf16[4,2,48,256]{3,2,1,0:T(8,128)(2,1)S(1)}, bf16[4,2,48,256]{3,2,1,0:T(8,128)(2,1)S(1)}, u32[]{:S(2)}, u32[]{:S(2)}) collective-permute-start(bf16[4,2,48,256]{3,2,1,0:T(8,128)(2,1)S(1)} %collective-permute-done.3.pb_ref.refs_8_.refs_6_), channel_id=1, source_target_pairs={{0,16},{16,0},{1,17},{17,1},{2,18},{18,2},{3,19},{19,3},{4,20},{20... | collective-permute-start | bytes 589832 | tf_op jit(solution)/shard_map/ppermute | solution.py:286
  43.0 4.0 %copy-start.2 = (bf16[2,192,256]{2,1,0:T(8,128)(2,1)}, bf16[2,192,256]{2,1,0:T(8,128)(2,1)S(1)}, u32[]{:S(2)}) copy-start(bf16[2,192,256]{2,1,0:T(8,128)(2,1)S(1)} %get-tuple-element.43) | copy-start | bytes 589828
  43.0 4.0 %copy-start.4 = (bf16[2,192,256]{2,1,0:T(8,128)(2,1)}, bf16[2,192,256]{2,1,0:T(8,128)(2,1)S(1)}, u32[]{:S(2)}) copy-start(bf16[2,192,256]{2,1,0:T(8,128)(2,1)S(1)} %get-tuple-element.45) | copy-start | bytes 589828
  47.0 0.9 %copy-start = (bf16[2,2,64,256]{3,2,1,0:T(8,128)(2,1)}, bf16[2,2,64,256]{3,2,1,0:T(8,128)(2,1)S(1)}, u32[]{:S(2)}) copy-start(bf16[2,2,64,256]{3,2,1,0:T(8,128)(2,1)S(1)} %get-tuple-element.41) | copy-start | bytes 393220
  47.0 0.9 %copy-start.6 = (bf16[2,2,64,256]{3,2,1,0:T(8,128)(2,1)}, bf16[2,2,64,256]{3,2,1,0:T(8,128)(2,1)S(1)}, u32[]{:S(2)}) copy-start(bf16[2,2,64,256]{3,2,1,0:T(8,128)(2,1)S(1)} %get-tuple-element.42) | copy-start | bytes 393220
  47.0 0.9 %copy-start.8 = (bf16[2,2,64,256]{3,2,1,0:T(8,128)(2,1)}, bf16[2,2,64,256]{3,2,1,0:T(8,128)(2,1)S(1)}, u32[]{:S(2)}) copy-start(bf16[2,2,64,256]{3,2,1,0:T(8,128)(2,1)S(1)} %get-tuple-element.40) | copy-start | bytes 393220
  47.0 0.9 %copy-start.10 = (bf16[2,2,64,256]{3,2,1,0:T(8,128)(2,1)}, bf16[2,2,64,256]{3,2,1,0:T(8,128)(2,1)S(1)}, u32[]{:S(2)}) copy-start(bf16[2,2,64,256]{3,2,1,0:T(8,128)(2,1)S(1)} %get-tuple-element.38) | copy-start | bytes 393220
  47.0 9.8 %collective-permute-start.13 = (bf16[2,2,64,256]{3,2,1,0:T(8,128)(2,1)}, bf16[2,2,64,256]{3,2,1,0:T(8,128)(2,1)S(1)}, u32[]{:S(2)}, u32[]{:S(2)}) collective-permute-start(bf16[2,2,64,256]{3,2,1,0:T(8,128)(2,1)} %get-tuple-element.36), channel_id=1, source_target_pairs={{0,2},{2,0},{4,6},{6,4},{8,10},{10,8},{12,14},{14,12},{1,3},{3,1},... | collective-permute-start | bytes 393224 | tf_op jit(solution)/shard_map/ppermute | solution.py:283
  47.6 7.8 %copy-start.3 = (bf16[2,192,256]{2,1,0:T(8,128)(2,1)S(1)}, bf16[2,192,256]{2,1,0:T(8,128)(2,1)}, u32[]{:S(2)}) copy-start(bf16[2,192,256]{2,1,0:T(8,128)(2,1)} %copy-done.2) | copy-start | bytes 589828
  47.6 9.3 %copy-start.5 = (bf16[2,192,256]{2,1,0:T(8,128)(2,1)S(1)}, bf16[2,192,256]{2,1,0:T(8,128)(2,1)}, u32[]{:S(2)}) copy-start(bf16[2,192,256]{2,1,0:T(8,128)(2,1)} %copy-done.4) | copy-start | bytes 589828
  47.9 3.9 %copy-start.11 = (bf16[2,2,64,256]{3,2,1,0:T(8,128)(2,1)S(1)}, bf16[2,2,64,256]{3,2,1,0:T(8,128)(2,1)}, u32[]{:S(2)}) copy-start(bf16[2,2,64,256]{3,2,1,0:T(8,128)(2,1)} %copy-done.10) | copy-start | bytes 393220
  47.9 5.4 %copy-start.9 = (bf16[2,2,64,256]{3,2,1,0:T(8,128)(2,1)S(1)}, bf16[2,2,64,256]{3,2,1,0:T(8,128)(2,1)}, u32[]{:S(2)}) copy-start(bf16[2,2,64,256]{3,2,1,0:T(8,128)(2,1)} %copy-done.8) | copy-start | bytes 393220
  47.9 5.9 %copy-start.7 = (bf16[2,2,64,256]{3,2,1,0:T(8,128)(2,1)S(1)}, bf16[2,2,64,256]{3,2,1,0:T(8,128)(2,1)}, u32[]{:S(2)}) copy-start(bf16[2,2,64,256]{3,2,1,0:T(8,128)(2,1)} %copy-done.6) | copy-start | bytes 393220
  48.5 20.4 %copy-start.1 = (bf16[2,2,64,256]{3,2,1,0:T(8,128)(2,1)S(1)}, bf16[2,2,64,256]{3,2,1,0:T(8,128)(2,1)}, u32[]{:S(2)}) copy-start(bf16[2,2,64,256]{3,2,1,0:T(8,128)(2,1)} %copy-done) | copy-start | bytes 393220
  51.8 6.0 %collective-permute-start.15 = (bf16[2,2,64,256]{3,2,1,0:T(8,128)(2,1)S(1)}, bf16[2,2,64,256]{3,2,1,0:T(8,128)(2,1)S(1)}, u32[]{:S(2)}, u32[]{:S(2)}) collective-permute-start(bf16[2,2,64,256]{3,2,1,0:T(8,128)(2,1)S(1)} %copy-done.11), channel_id=1, source_target_pairs={{0,2},{2,0},{4,6},{6,4},{8,10},{10,8},{12,14},{14,12},{1,3},{3,1},... | collective-permute-start | bytes 393224 | tf_op jit(solution)/shard_map/ppermute | solution.py:283
  53.3 5.9 %collective-permute-start.17 = (bf16[2,2,64,256]{3,2,1,0:T(8,128)(2,1)S(1)}, bf16[2,2,64,256]{3,2,1,0:T(8,128)(2,1)S(1)}, u32[]{:S(2)}, u32[]{:S(2)}) collective-permute-start(bf16[2,2,64,256]{3,2,1,0:T(8,128)(2,1)S(1)} %copy-done.9), channel_id=1, source_target_pairs={{0,2},{2,0},{4,6},{6,4},{8,10},{10,8},{12,14},{14,12},{1,3},{3,1},... | collective-permute-start | bytes 393224 | tf_op jit(solution)/shard_map/ppermute | solution.py:283
  53.8 10.2 %collective-permute-start.19 = (bf16[2,2,64,256]{3,2,1,0:T(8,128)(2,1)S(1)}, bf16[2,2,64,256]{3,2,1,0:T(8,128)(2,1)S(1)}, u32[]{:S(2)}, u32[]{:S(2)}) collective-permute-start(bf16[2,2,64,256]{3,2,1,0:T(8,128)(2,1)S(1)} %copy-done.7), channel_id=1, source_target_pairs={{0,2},{2,0},{4,6},{6,4},{8,10},{10,8},{12,14},{14,12},{1,3},{3,1},... | collective-permute-start | bytes 393224 | tf_op jit(solution)/shard_map/ppermute | solution.py:283
  55.3 13.6 %collective-permute-start.20 = (bf16[2,192,256]{2,1,0:T(8,128)(2,1)S(1)}, bf16[2,192,256]{2,1,0:T(8,128)(2,1)S(1)}, u32[]{:S(2)}, u32[]{:S(2)}) collective-permute-start(bf16[2,192,256]{2,1,0:T(8,128)(2,1)S(1)} %copy-done.3), channel_id=1, source_target_pairs={{0,16},{16,0},{1,17},{17,1},{2,18},{18,2},{3,19},{19,3},{4,20},{20... | collective-permute-start | bytes 589832 | tf_op jit(solution)/shard_map/ppermute | solution.py:286
  56.8 6.3 %collective-permute-start.21 = (bf16[2,192,256]{2,1,0:T(8,128)(2,1)S(1)}, bf16[2,192,256]{2,1,0:T(8,128)(2,1)S(1)}, u32[]{:S(2)}, u32[]{:S(2)}) collective-permute-start(bf16[2,192,256]{2,1,0:T(8,128)(2,1)S(1)} %copy-done.5), channel_id=1, source_target_pairs={{0,16},{16,0},{1,17},{17,1},{2,18},{18,2},{3,19},{19,3},{4,20},{20... | collective-permute-start | bytes 589832 | tf_op jit(solution)/shard_map/ppermute | solution.py:286
  57.8 7.4 %collective-permute-start.14 = (bf16[2,2,64,256]{3,2,1,0:T(8,128)(2,1)S(1)}, bf16[2,2,64,256]{3,2,1,0:T(8,128)(2,1)S(1)}, u32[]{:S(2)}, u32[]{:S(2)}) collective-permute-start(bf16[2,2,64,256]{3,2,1,0:T(8,128)(2,1)S(1)} %add_convert_fusion.4), channel_id=1, source_target_pairs={{0,4},{2,6},{4,8},{6,10},{8,12},{10,14},{12,0},{14,2},{1,5},{3,7},... | collective-permute-start | bytes 393224 | tf_op jit(solution)/shard_map/ppermute | solution.py:280
  59.2 9.3 %collective-permute-start.16 = (bf16[2,2,64,256]{3,2,1,0:T(8,128)(2,1)S(1)}, bf16[2,2,64,256]{3,2,1,0:T(8,128)(2,1)S(1)}, u32[]{:S(2)}, u32[]{:S(2)}) collective-permute-start(bf16[2,2,64,256]{3,2,1,0:T(8,128)(2,1)S(1)} %add_convert_fusion.3), channel_id=1, source_target_pairs={{0,8},{2,10},{4,12},{6,14},{8,0},{10,2},{12,4},{14,6},{1,9},{3,11}... | collective-permute-start | bytes 393224 | tf_op jit(solution)/shard_map/ppermute | solution.py:280
  63.1 5.7 %collective-permute-start.18 = (bf16[2,2,64,256]{3,2,1,0:T(8,128)(2,1)S(1)}, bf16[2,2,64,256]{3,2,1,0:T(8,128)(2,1)S(1)}, u32[]{:S(2)}, u32[]{:S(2)}) collective-permute-start(bf16[2,2,64,256]{3,2,1,0:T(8,128)(2,1)S(1)} %add_convert_fusion.2), channel_id=1, source_target_pairs={{0,12},{2,14},{4,0},{6,2},{8,4},{10,6},{12,8},{14,10},{1,13},{3,15... | collective-permute-start | bytes 393224 | tf_op jit(solution)/shard_map/ppermute | solution.py:280
  64.1 5.7 %collective-permute-start.22 = (bf16[2,192,256]{2,1,0:T(8,128)(2,1)S(1)}, bf16[2,192,256]{2,1,0:T(8,128)(2,1)S(1)}, u32[]{:S(2)}, u32[]{:S(2)}) collective-permute-start(bf16[2,192,256]{2,1,0:T(8,128)(2,1)S(1)} %add_convert_fusion), channel_id=1, source_target_pairs={{0,2},{2,0},{4,6},{6,4},{8,10},{10,8},{12,14},{14,12},{1,3},{3,1},... | collective-permute-start | bytes 589832 | tf_op jit(solution)/shard_map/ppermute | solution.py:283
  69.9 4.7 %collective-permute-start.23 = (bf16[2,48,256]{2,1,0:T(8,128)(2,1)S(1)}, bf16[2,48,256]{2,1,0:T(8,128)(2,1)S(1)}, u32[]{:S(2)}, u32[]{:S(2)}) collective-permute-start(bf16[2,48,256]{2,1,0:T(8,128)(2,1)S(1)} %get-tuple-element.58), channel_id=1, source_target_pairs={{0,12},{2,14},{4,0},{6,2},{8,4},{10,6},{12,8},{14,10},{1,13},{3,15... | collective-permute-start | bytes 147464 | tf_op jit(solution)/shard_map/ppermute | solution.py:280
  72.6 5.9 %collective-permute-start.25 = (bf16[2,48,256]{2,1,0:T(8,128)(2,1)S(1)}, bf16[2,48,256]{2,1,0:T(8,128)(2,1)S(1)}, u32[]{:S(2)}, u32[]{:S(2)}) collective-permute-start(bf16[2,48,256]{2,1,0:T(8,128)(2,1)S(1)} %get-tuple-element.59), channel_id=1, source_target_pairs={{0,4},{2,6},{4,8},{6,10},{8,12},{10,14},{12,0},{14,2},{1,5},{3,7},... | collective-permute-start | bytes 147464 | tf_op jit(solution)/shard_map/ppermute | solution.py:280
  72.6 5.9 %collective-permute-start.24 = (bf16[2,48,256]{2,1,0:T(8,128)(2,1)S(1)}, bf16[2,48,256]{2,1,0:T(8,128)(2,1)S(1)}, u32[]{:S(2)}, u32[]{:S(2)}) collective-permute-start(bf16[2,48,256]{2,1,0:T(8,128)(2,1)S(1)} %get-tuple-element.60), channel_id=1, source_target_pairs={{0,8},{2,10},{4,12},{6,14},{8,0},{10,2},{12,4},{14,6},{1,9},{3,11}... | collective-permute-start | bytes 147464 | tf_op jit(solution)/shard_map/ppermute | solution.py:280
where the time goes:
time: 79.4 us; the launch traced here: 79.1 us
  starting transfers between devices  32.7 us (41%)
  waiting for transfers between devices  18.3 us (23%)
  Pallas kernels  14.8 us (19%)
  local copies, waits for them, and re-layouts  9.36 us (12%)
  other arithmetic  3.04 us (4%)
  between operations  0.97 us (1%)
    ppermute x12, starting transfers between devices, shift_z(): lax.ppermute(x, 'seq', [(i, (i + 2 * k) % size) for i in range(size)])  17.2 us
    ppermute x12, waiting for transfers between devices, shift_z(): lax.ppermute(x, 'seq', [(i, (i + 2 * k) % size) for i in range(size)])  13.4 us
    ppermute x10, starting transfers between devices, swap_y(): return lax.ppermute(x, 'seq', [(i, i ^ 1) for i in range(size)])  10.4 us
    pallas_call x1, Pallas kernels, on_device(): pl.pallas_call(lambda *refs: middle_body(pieces, *refs), grid=(kv,), in_s...  6.22 us
    ppermute x4, starting transfers between devices, swap_x(): return lax.ppermute(x, 'pair', [(0, 1), (1, 0)])  5.07 us
    pallas_call x1, Pallas kernels, on_device(): pl.pallas_call(prefix_forward_body, grid=(kv,), in_specs=[whole(prefix_bi...  4.55 us
    pallas_call x1, Pallas kernels, on_device(): pl.pallas_call(lambda *refs: answer_backward_body(pieces, *refs), grid=(k...  3.99 us
    unnamed x30, local copies, waits for them, and re-layouts  3.93 us
  transfers between devices with their start and end apart: 26, of which 10 were waited for; matrix products, arithmetic and copies ran while one was open for 14% of the time, Pallas kernels for 6%

commit v1 on v0

--- a/solution.py
+++ b/solution.py
@@ -4,6 +4,7 @@
 import jax.numpy as jnp
 from jax import lax
 from jax.experimental import pallas as pl
+from jax.experimental.layout import Layout, with_layout_constraint
 from jax.experimental.pallas import tpu as pltpu
 from jax.sharding import PartitionSpec as P
 
@@ -30,7 +31,7 @@
 
 
 def params(cells):
-    limit = 24 if cells <= 2**20 else 60
+    limit = 18 if cells <= 2**20 else 60
     return pltpu.CompilerParams(
         dimension_semantics=("arbitrary",), vmem_limit_bytes=limit * 1024 * 1024
     )
@@ -56,7 +57,8 @@
     for t, ref in enumerate(refs):
         for b in range(ref.shape[1]):
             k_s[b, t * rows : (t + 1) * rows, :] = ref[0, b]
-            v_s[b, t * rows : (t + 1) * rows, 0:HEAD_DIM] = ref[1, b]
+            if v_s is not None:
+                v_s[b, t * rows : (t + 1) * rows, 0:HEAD_DIM] = ref[1, b]
 
 
 def lanes(ref, here, update):
@@ -120,32 +122,26 @@
     bias_ref,
     q_ref,
     do_ref,
-    p_ref,
     ol_ref,
     m_ref,
     *rest,
 ):
-    prefix = rest[:4]
-    answer = rest[4 : 4 + pieces]
+    answer = rest[:pieces]
     (
         out_ref,
-        pb_ref,
-        dob_ref,
-        deltab_ref,
+        doa_ref,
+        deltaa_ref,
         ds_ref,
-        own_ref,
-        near_ref,
-        far_ref,
-        k_s,
-        v_s,
+        *grads,
         s_s,
         ka_s,
         va_s,
         olb_s,
         mb_s,
-        doa_s,
-        deltaa_s,
-    ) = rest[4 + pieces :]
+        p_s,
+        dob_s,
+        deltab_s,
+    ) = rest[pieces:]
     scale = HEAD_DIM ** (-0.5)
     batch = ka_s.shape[0]
     keys = ka_s.shape[1]
@@ -153,9 +149,9 @@
     total = q_ref.shape[1]
     per = total // batch
     groups = per // rows
+    piece_rows = answer[0].shape[-2]
     place_answer(answer, ka_s, va_s)
     va_s[:, :, HEAD_DIM:] = jnp.ones((batch, keys, HEAD_DIM), bf16)
-    place_prefix(prefix, k_s, v_s)
     for b in range(batch):
         for part in blocks(per, rows, keys):
             base = b * per + part.start
@@ -167,8 +163,8 @@
                 s_s[span, :] = s
                 mb_s[span, :] = row_top(s)
     for b in range(batch):
-        exponents(pb_ref, s_s, lambda here: mb_s[here, :], b * per, per)
-        olb_s[b * per : (b + 1) * per, :] = mm(pb_ref[0, b * per : (b + 1) * per, :], va_s[b])
+        exponents(p_s, s_s, lambda here: mb_s[here, :], b * per, per)
+        olb_s[b * per : (b + 1) * per, :] = mm(p_s[0, b * per : (b + 1) * per, :], va_s[b])
 
     for b in range(batch):
 
@@ -190,23 +186,46 @@
             douts = do_ref[0, here, :].astype(f32) * live
             da = (douts * ea).astype(bf16)
             db = (douts * eb).astype(bf16)
-            doa_s[here, :] = da
-            dob_ref[0, here, :] = db
-            deltaa_s[here, :] = jnp.broadcast_to(
+            doa_ref[0, here, :] = da
+            dob_s[here, :] = db
+            deltaa_ref[0, here, :] = jnp.broadcast_to(
                 jnp.sum(da.astype(f32) * attended, axis=1, keepdims=True), (rows, HEAD_DIM)
             )
-            deltab_ref[0, here, :] = jnp.broadcast_to(
+            deltab_s[here, :] = jnp.broadcast_to(
                 jnp.sum(db.astype(f32) * attended, axis=1, keepdims=True), (rows, HEAD_DIM)
             )
             return carry
 
         lax.fori_loop(0, groups, combine, 0, unroll=groups)
-    for span in blocks(total, per if per * k_s.shape[0] <= 2**19 else rows, k_s.shape[0]):
-        dp = mm_nt(doa_s[span, :], v_s[...])
-        score_grads(ds_ref.at[0, span], p_ref[0, span, :], dp, deltaa_s[span, :])
+    for b in range(batch):
+        for part in blocks(per, rows, keys):
+            span = slice(b * per + part.start, b * per + part.stop)
+            dp = mm_nt(dob_s[span, :], va_s[b, :, 0:HEAD_DIM])
+            score_grads(ds_ref.at[0, span], p_s[0, span, :], dp, deltab_s[span, :])
+    for b in range(batch):
+        span = slice(b * per, (b + 1) * per)
+        value_term = jnp.transpose(mm_tn(dob_s[span, :], p_s[0, span, :])).astype(bf16)
+        key_term = (jnp.transpose(mm_tn(q_ref[0, span, :], ds_ref[0, span, :])) * scale).astype(bf16)
+        for t in range(pieces):
+            part = slice(t * piece_rows, (t + 1) * piece_rows)
+            ref = grads[4 * t // pieces]
+            ref[t % (pieces // 4), 0, b] = key_term[part]
+            ref[t % (pieces // 4), 1, b] = value_term[part]
+
+
+def prefix_backward_body(q_ref, p_ref, doa_ref, deltaa_ref, *rest):
+    prefix = rest[:4]
+    ds_ref, own_ref, near_ref, far_ref, k_s, v_s = rest[4:]
+    scale = HEAD_DIM ** (-0.5)
+    total = q_ref.shape[1]
+    place_prefix(prefix, k_s, v_s)
+    size = total // 2 if total // 2 * k_s.shape[0] <= 2**19 else 64
+    for span in blocks(total, size, k_s.shape[0]):
+        dp = mm_nt(doa_ref[0, span, :], v_s[...])
+        score_grads(ds_ref.at[0, span], p_ref[0, span, :], dp, deltaa_ref[0, span, :])
     half = own_ref.shape[1]
     quarter = half // 2
-    value_term = jnp.transpose(mm_tn(doa_s[...], p_ref[0])).astype(bf16)
+    value_term = jnp.transpose(mm_tn(doa_ref[0], p_ref[0])).astype(bf16)
     key_term = (jnp.transpose(mm_tn(q_ref[0], ds_ref[0])) * scale).astype(bf16)
     for t, term in ((0, key_term), (1, value_term)):
         own_ref[t] = term[:half]
@@ -214,38 +233,18 @@
         far_ref[t] = term[half + quarter :]
 
 
-def answer_backward_body(
-    pieces, q_ref, ds_ref, pb_ref, dob_ref, deltab_ref, *rest
-):
+def query_backward_body(pieces, dsa_ref, dsb_ref, *rest):
     prefix = rest[:4]
-    rest = rest[4:]
-    answer = rest[:pieces]
-    dq_ref = rest[pieces]
-    grads = rest[pieces + 1 : 2 * pieces + 1]
-    k_s, ka_s, va_s, dsb_s = rest[2 * pieces + 1 :]
+    answer = rest[4 : 4 + pieces]
+    dq_ref, k_s, ka_s = rest[4 + pieces :]
     scale = HEAD_DIM ** (-0.5)
     batch = ka_s.shape[0]
-    total = q_ref.shape[1]
-    per = total // batch
-    piece_rows = answer[0].shape[-2]
-    place_answer(answer, ka_s, va_s)
+    per = dq_ref.shape[1] // batch
     place_prefix(prefix, k_s, None)
-    for b in range(batch):
-        for part in blocks(per, 64, ka_s.shape[1]):
-            rows = slice(b * per + part.start, b * per + part.stop)
-            dp = mm_nt(dob_ref[0, rows, :], va_s[b])
-            score_grads(dsb_s.at[rows], pb_ref[0, rows, :], dp, deltab_ref[0, rows, :])
+    place_answer(answer, ka_s, None)
     for b in range(batch):
         rows = slice(b * per, (b + 1) * per)
-        key_term = (jnp.transpose(mm_tn(q_ref[0, rows, :], dsb_s[rows, :])) * scale).astype(bf16)
-        value_term = jnp.transpose(mm_tn(dob_ref[0, rows, :], pb_ref[0, rows, :])).astype(bf16)
-        for t, ref in enumerate(grads):
-            span = slice(t * piece_rows, (t + 1) * piece_rows)
-            ref[0, b] = key_term[span]
-            ref[1, b] = value_term[span]
-    for b in range(batch):
-        rows = slice(b * per, (b + 1) * per)
-        dq = mm(ds_ref[0, rows, :], k_s[...]) + mm(dsb_s[rows, :], ka_s[b])
+        dq = mm(dsa_ref[0, rows, :], k_s[...]) + mm(dsb_ref[0, rows, :], ka_s[b])
         dq_ref[0, rows, :] = (dq * scale).astype(bf16)
 
 
@@ -261,7 +260,7 @@
 ):
     size = lax.axis_size("seq")
     sides = lax.axis_size("pair")
-    assert sides == 2 and size % 2 == 0
+    assert sides == 2 and size >= 4 and size & (size - 1) == 0
     outer = size // 2
     rows = queries.shape[1]
     batch = queries.shape[2]
@@ -276,8 +275,8 @@
     side = lax.axis_index("pair")
     z, y = place // 2, place % 2
 
-    def shift_z(x, k):
-        return lax.ppermute(x, "seq", [(i, (i + 2 * k) % size) for i in range(size)])
+    def swap_z(x, k):
+        return lax.ppermute(x, "seq", [(i, i ^ (2 * k)) for i in range(size)])
 
     def swap_y(x):
         return lax.ppermute(x, "seq", [(i, i ^ 1) for i in range(size)])
@@ -287,16 +286,16 @@
 
     prefix_own = jnp.stack([prefix_keys, prefix_values])
     answer_own = jnp.stack([a[0].transpose(1, 0, 2) for a in (answer_keys, answer_values)])
-    prefix_z = jnp.stack([prefix_own] + [shift_z(prefix_own, k) for k in range(1, outer)])
+    prefix_z = jnp.stack([prefix_own] + [swap_z(prefix_own, k) for k in range(1, outer)])
     prefix_y = swap_y(prefix_z)
     prefix = [prefix_z, prefix_y, swap_x(prefix_z), swap_x(prefix_y)]
-    near = [answer_own] + [shift_z(answer_own, k) for k in range(1, outer)]
+    near = [answer_own] + [swap_z(answer_own, k) for k in range(1, outer)]
     far = [swap_y(piece) for piece in near]
     answer = near + far
     pieces = len(answer)
 
     dz = jnp.arange(outer, dtype=jnp.int32)
-    z_from = (z - dz) % outer
+    z_from = z ^ dz
     pair_from = (side + jnp.arange(2, dtype=jnp.int32)) % 2
     y_from = (y + jnp.arange(2, dtype=jnp.int32)) % 2
     seq_from = z_from[None, :] * 2 + y_from[:, None]
@@ -320,7 +319,8 @@
 
     def row_major(x):
         x = x.reshape(kv, batch, group, rows, HEAD_DIM)
-        return x.transpose(3, 1, 0, 2, 4).reshape(queries.shape)
+        x = x.transpose(3, 1, 0, 2, 4).reshape(queries.shape)
+        return with_layout_constraint(x, Layout((0, 1, 2, 3)))
 
     query_view = head_major(queries)
     grad_view = head_major(grad_out)
@@ -345,6 +345,7 @@
     ol_shape = (kv, total, 2 * HEAD_DIM)
     own_shape = (2, prefix_total // 2, kv * HEAD_DIM)
     sent_shape = (2, prefix_total // 4, kv * HEAD_DIM)
+    stack_shape = (outer // 2,) + answer_own.shape
     unit_a = 2 * kv * total * prefix_total * HEAD_DIM
     unit_b = 2 * kv * total * answer_total * HEAD_DIM
 
@@ -368,87 +369,80 @@
         name="prefix_forward",
     )(prefix_bias, query_view, *prefix)
 
-    (out_view, probs_b, grad_b, delta_b, ds_a, prefix_own_sum, prefix_near, prefix_far) = (
-        pl.pallas_call(
-            lambda *refs: middle_body(pieces, *refs),
-            grid=(kv,),
-            in_specs=[
-                whole(live.shape),
-                whole(answer_bias.shape),
-                q_spec,
-                q_spec,
-                by_head(pa_shape),
-                by_head(ol_shape),
-                q_spec,
-            ]
-            + prefix_specs
-            + [answer_spec] * pieces,
-            out_specs=[
-                q_spec,
-                by_head(pb_shape),
-                q_spec,
-                q_spec,
-                by_head(pa_shape),
-                lane_block(own_shape),
-                lane_block(sent_shape),
-                lane_block(sent_shape),
-            ],
-            out_shape=[
-                jax.ShapeDtypeStruct(q_shape, bf16),
-                jax.ShapeDtypeStruct(pb_shape, bf16),
-                jax.ShapeDtypeStruct(q_shape, bf16),
-                jax.ShapeDtypeStruct(q_shape, f32),
-                jax.ShapeDtypeStruct(pa_shape, bf16),
-                jax.ShapeDtypeStruct(own_shape, bf16),
-                jax.ShapeDtypeStruct(sent_shape, bf16),
-                jax.ShapeDtypeStruct(sent_shape, bf16),
-            ],
-            scratch_shapes=[
-                pltpu.VMEM((prefix_total, HEAD_DIM), bf16),
-                pltpu.VMEM((prefix_total, HEAD_DIM), bf16),
-                pltpu.VMEM((total, answer_total), f32),
-                pltpu.VMEM((batch, answer_total, HEAD_DIM), bf16),
-                pltpu.VMEM((batch, answer_total, 2 * HEAD_DIM), bf16),
-                pltpu.VMEM((total, 2 * HEAD_DIM), f32),
-                pltpu.VMEM((total, HEAD_DIM), f32),
-                pltpu.VMEM((total, HEAD_DIM), bf16),
-                pltpu.VMEM((total, HEAD_DIM), f32),
-            ],
-            compiler_params=params(total * prefix_total),
-            cost_estimate=cost(2 * unit_b + 3 * unit_a, 12 << 20, kv * total * answer_total),
-            name="middle",
-        )(
-            live,
-            answer_bias,
-            query_view,
-            grad_view,
-            probs_a,
-            ol_a,
-            top_a,
-            *prefix,
-            *answer,
-        )
-    )
-
-    dq_view, *answer_grads = pl.pallas_call(
-        lambda *refs: answer_backward_body(pieces, *refs),
+    (out_view, grad_a, delta_a, ds_b, near_low, near_high, far_low, far_high) = pl.pallas_call(
+        lambda *refs: middle_body(pieces, *refs),
         grid=(kv,),
-        in_specs=[q_spec, by_head(pa_shape), by_head(pb_shape), q_spec, q_spec]
-        + prefix_specs
+        in_specs=[
+            whole(live.shape),
+            whole(answer_bias.shape),
+            q_spec,
+            q_spec,
+            by_head(ol_shape),
+            q_spec,
+        ]
         + [answer_spec] * pieces,
-        out_specs=[q_spec] + [answer_spec] * pieces,
-        out_shape=[jax.ShapeDtypeStruct(q_shape, bf16)]
-        + [jax.ShapeDtypeStruct(answer_own.shape, bf16)] * pieces,
+        out_specs=[q_spec, q_spec, q_spec, by_head(pb_shape)] + [lane_block(stack_shape)] * 4,
+        out_shape=[
+            jax.ShapeDtypeStruct(q_shape, bf16),
+            jax.ShapeDtypeStruct(q_shape, bf16),
+            jax.ShapeDtypeStruct(q_shape, f32),
+            jax.ShapeDtypeStruct(pb_shape, bf16),
+        ]
+        + [jax.ShapeDtypeStruct(stack_shape, bf16)] * 4,
+        scratch_shapes=[
+            pltpu.VMEM((total, answer_total), f32),
+            pltpu.VMEM((batch, answer_total, HEAD_DIM), bf16),
+            pltpu.VMEM((batch, answer_total, 2 * HEAD_DIM), bf16),
+            pltpu.VMEM((total, 2 * HEAD_DIM), f32),
+            pltpu.VMEM((total, HEAD_DIM), f32),
+            pltpu.VMEM((1, total, answer_total), bf16),
+            pltpu.VMEM((total, HEAD_DIM), bf16),
+            pltpu.VMEM((total, HEAD_DIM), f32),
+        ],
+        compiler_params=params(total * prefix_total),
+        cost_estimate=cost(5 * unit_b, 12 << 20, kv * total * answer_total),
+        name="middle",
+    )(live, answer_bias, query_view, grad_view, ol_a, top_a, *answer)
+
+    ds_a, prefix_own_sum, prefix_near, prefix_far = pl.pallas_call(
+        prefix_backward_body,
+        grid=(kv,),
+        in_specs=[q_spec, by_head(pa_shape), q_spec, q_spec] + prefix_specs,
+        out_specs=[
+            by_head(pa_shape),
+            lane_block(own_shape),
+            lane_block(sent_shape),
+            lane_block(sent_shape),
+        ],
+        out_shape=[
+            jax.ShapeDtypeStruct(pa_shape, bf16),
+            jax.ShapeDtypeStruct(own_shape, bf16),
+            jax.ShapeDtypeStruct(sent_shape, bf16),
+            jax.ShapeDtypeStruct(sent_shape, bf16),
+        ],
+        scratch_shapes=[
+            pltpu.VMEM((prefix_total, HEAD_DIM), bf16),
+            pltpu.VMEM((prefix_total, HEAD_DIM), bf16),
+        ],
+        compiler_params=params(total * prefix_total),
+        cost_estimate=cost(3 * unit_a, 12 << 20, 0),
+        name="prefix_backward",
+    )(query_view, probs_a, grad_a, delta_a, *prefix)
+
+    dq_view = pl.pallas_call(
+        lambda *refs: query_backward_body(pieces, *refs),
+        grid=(kv,),
+        in_specs=[by_head(pa_shape), by_head(pb_shape)] + prefix_specs + [answer_spec] * pieces,
+        out_specs=q_spec,
+        out_shape=jax.ShapeDtypeStruct(q_shape, bf16),
         scratch_shapes=[
             pltpu.VMEM((prefix_total, HEAD_DIM), bf16),
             pltpu.VMEM((batch, answer_total, HEAD_DIM), bf16),
-            pltpu.VMEM((batch, answer_total, HEAD_DIM), bf16),
-            pltpu.VMEM((total, answer_total), bf16),
         ],
         compiler_params=params(total * prefix_total),
-        cost_estimate=cost(4 * unit_b + unit_a, 8 << 20, 0),
-        name="answer_backward",
-    )(query_view, ds_a, probs_b, grad_b, delta_b, *prefix, *answer)
+        cost_estimate=cost(unit_a + unit_b, 8 << 20, 0),
+        name="query_backward",
+    )(ds_a, ds_b, *prefix, *answer)
 
     split = (2, outer, prefix_rows, kv * HEAD_DIM)
     half = prefix_total // 4
@@ -458,14 +452,16 @@
     z_sum = (near_got + y_got).reshape(split)
     prefix_sum = z_sum[:, 0]
     for k in range(1, outer):
-        prefix_sum = prefix_sum + shift_z(z_sum[:, k].astype(bf16), -k).astype(f32)
-    answer_sum = None
-    for k in reversed(range(outer)):
-        got = swap_y(answer_grads[outer + k]).astype(f32)
-        piece = answer_grads[k].astype(f32) + got
-        if k:
-            piece = shift_z(piece.astype(bf16), -k).astype(f32)
-        answer_sum = piece if answer_sum is None else answer_sum + piece
+        prefix_sum = prefix_sum + swap_z(z_sum[:, k].astype(bf16), k).astype(f32)
+    high_got = swap_y(far_high)
+    low_got = swap_y(far_low)
+    high = (near_high.astype(f32) + high_got.astype(f32)).astype(bf16)
+    low = near_low.astype(f32) + low_got.astype(f32)
+    answer_sum = low[0]
+    for k in range(1, outer):
+        at = k % (outer // 2)
+        piece = (high if k >= outer // 2 else low)[at]
+        answer_sum = answer_sum + swap_z(piece.astype(bf16), k).astype(f32)
     answer_sum = answer_sum.astype(bf16)
 
     def answer_out(x):

time: 79.4 us -> 92.8 us (1.17)
  local copies, waits for them, and re-layouts: 9.36 us -> 26 us
  waiting for transfers between devices: 18.3 us -> 12.3 us
  other arithmetic: 3.04 us -> 5.86 us
    unnamed x30 -> x74, local copies, waits for them, and re-layouts: 3.93 us -> 14.5 us
    reshape x2 -> x4, local copies, waits for them, and re-layouts: 1.01 us -> 6.31 us  [row_major(): x = x.transpose(3, 1, 0, 2, 4).reshape(queries.shape)]
    ppermute x12, waiting for transfers between devices: 13.4 us -> 10.9 us  [swap_z(): return lax.ppermute(x, 'seq', [(i, i ^ 2 * k) for i in range(size)])]
    ppermute x10 -> x8, waiting for transfers between devices: 2.4 us -> 0.02 us  [swap_y(): return lax.ppermute(x, 'seq', [(i, i ^ 1) for i in range(size)])]
    ppermute x10 -> x8, starting transfers between devices: 10.4 us -> 8.31 us  [swap_y(): return lax.ppermute(x, 'seq', [(i, i ^ 1) for i in range(size)])]
    ppermute x4, waiting for transfers between devices: 2.56 us -> 1.42 us  [swap_x(): return lax.ppermute(x, 'pair', [(0, 1), (1, 0)])]
    ppermute x12, starting transfers between devices: 17.2 us -> 18.4 us  [swap_z(): return lax.ppermute(x, 'seq', [(i, i ^ 2 * k) for i in range(size)])]
    pallas_call x1 -> x2, Pallas kernels: 3.99 us -> 5.07 us  [the longest x1 3.09 us: on_device(): pl.pallas_call(prefix_backward_body, grid=(kv,), in_specs=[q_spec, by_hea...]
  transfers between devices with their start and end apart: 26 -> 24, of which waited for: 10 -> 5; matrix products, arithmetic and copies ran while one was open for 14% -> 19% of each run, Pallas kernels for 6% -> 7%
where the time goes in v1:
time: 92.8 us; the launch traced here: 92.2 us
  starting transfers between devices  31.8 us (34%)
  local copies, waits for them, and re-layouts  26 us (28%)
  Pallas kernels  15.1 us (16%)
  waiting for transfers between devices  12.3 us (13%)
  other arithmetic  5.86 us (6%)
  between operations  1.06 us (1%)
    ppermute x12, starting transfers between devices, swap_z(): return lax.ppermute(x, 'seq', [(i, i ^ 2 * k) for i in range(size)])  18.4 us
    unnamed x74, local copies, waits for them, and re-layouts  14.5 us
    ppermute x12, waiting for transfers between devices, swap_z(): return lax.ppermute(x, 'seq', [(i, i ^ 2 * k) for i in range(size)])  10.9 us
    ppermute x8, starting transfers between devices, swap_y(): return lax.ppermute(x, 'seq', [(i, i ^ 1) for i in range(size)])  8.31 us
    reshape x4, local copies, waits for them, and re-layouts, row_major(): x = x.transpose(3, 1, 0, 2, 4).reshape(queries.shape)  6.31 us
    pallas_call x1, Pallas kernels, on_device(): pl.pallas_call(lambda *refs: middle_body(pieces, *refs), grid=(kv,), in_s...  5.44 us
    ppermute x4, starting transfers between devices, swap_x(): return lax.ppermute(x, 'pair', [(0, 1), (1, 0)])  5.14 us
    pallas_call x1, Pallas kernels, on_device(): pl.pallas_call(prefix_forward_body, grid=(kv,), in_specs=[whole(prefix_bi...  4.56 us
  transfers between devices with their start and end apart: 24, of which 5 were waited for; matrix products, arithmetic and copies ran while one was open for 19% of the time, Pallas kernels for 7%

profile of v1, /device:TPU:0, one launch (start us, length us, event | category | flops | bytes accessed | tf_op | source)
XLA Modules:
  0.0 92.2 jit_solution(2251580374797727025)
XLA Ops:
  0.6 0.8 fusion.11
  1.5 4.1 %collective-permute-start.1 = (bf16[2,48,256]{2,1,0:T(8,128)(2,1)S(1)}, bf16[2,48,256]{2,1,0:T(8,128)(2,1)S(1)}, u32[]{:S(2)}, u32[]{:S(2)}) collective-permute-start(bf16[2,48,256]{2,1,0:T(8,128)(2,1)S(1)} %get-tuple-element.58), channel_id=1, source_target_pairs={{0,8},{2,10},{4,12},{6,14},{8,0},{10,2},{12,4},{14,6},{1,9},{3,11}... | collective-permute-start | bytes 147464 | tf_op jit(solution)/shard_map/ppermute | solution.py:279
  5.6 1.6 %collective-permute-start = (bf16[2,48,256]{2,1,0:T(8,128)(2,1)S(1)}, bf16[2,48,256]{2,1,0:T(8,128)(2,1)S(1)}, u32[]{:S(2)}, u32[]{:S(2)}) collective-permute-start(bf16[2,48,256]{2,1,0:T(8,128)(2,1)S(1)} %get-tuple-element.58), channel_id=1, source_target_pairs={{0,4},{2,6},{4,0},{6,2},{8,12},{10,14},{12,8},{14,10},{1,5},{3,7},... | collective-permute-start | bytes 147464 | tf_op jit(solution)/shard_map/ppermute | solution.py:279
  7.2 0.9 copy_bitcast_fusion.2
  8.1 3.9 %collective-permute-start.8 = (bf16[2,2,64,256]{3,2,1,0:T(8,128)(2,1)S(1)}, bf16[2,2,64,256]{3,2,1,0:T(8,128)(2,1)S(1)}, u32[]{:S(2)}, u32[]{:S(2)}) collective-permute-start(bf16[2,2,64,256]{3,2,1,0:T(8,128)(2,1)S(1)} %pad_maximum_fusion.1.refs_6_), channel_id=1, source_target_pairs={{0,12},{2,14},{4,8},{6,10},{8,4},{10,6},{12,0},{14,2},{1,13},{3,15... | collective-permute-start | bytes 393224 | tf_op jit(solution)/shard_map/ppermute | solution.py:279
  13.6 1.6 %collective-permute-start.4 = (bf16[4,2,48,256]{3,2,1,0:T(8,128)(2,1)S(1)}, bf16[4,2,48,256]{3,2,1,0:T(8,128)(2,1)S(1)}, u32[]{:S(2)}, u32[]{:S(2)}) collective-permute-start(bf16[4,2,48,256]{3,2,1,0:T(8,128)(2,1)S(1)} %pad_maximum_fusion.pa_ref.rest_0_.refs_2_), channel_id=1, source_target_pairs={{0,16},{16,0},{1,17},{17,1},{2,18},{18,2},{3,19},{19,3},{4,20},{20... | collective-permute-start | bytes 589832 | tf_op jit(solution)/shard_map/ppermute | solution.py:285
  15.2 1.5 %collective-permute-start.3 = (bf16[4,2,48,256]{3,2,1,0:T(8,128)(2,1)S(1)}, bf16[4,2,48,256]{3,2,1,0:T(8,128)(2,1)S(1)}, u32[]{:S(2)}, u32[]{:S(2)}) collective-permute-start(bf16[4,2,48,256]{3,2,1,0:T(8,128)(2,1)S(1)} %pad_maximum_fusion.pa_ref.rest_0_.refs_2_), channel_id=1, source_target_pairs={{0,2},{2,0},{4,6},{6,4},{8,10},{10,8},{12,14},{14,12},{1,3},{3,1},... | collective-permute-start | bytes 589832 | tf_op jit(solution)/shard_map/ppermute | solution.py:282
  16.7 0.7 compare_select_fusion.1
  18.1 4.8 %collective-permute-done.7.refs_8_ = bf16[2,2,64,256]{3,2,1,0:T(8,128)(2,1)S(1)} collective-permute-done((bf16[2,2,64,256]{3,2,1,0:T(8,128)(2,1)S(1)}, bf16[2,2,64,256]{3,2,1,0:T(8,128)(2,1)S(1)}, u32[]{:S(2)}, u32[]{:S(2)}) %collective-permute-start.7) | collective-permute-done | bytes 131104 | tf_op jit(solution)/shard_map/ppermute | solution.py:279
  22.9 1.5 %collective-permute-start.12 = (bf16[2,2,64,256]{3,2,1,0:T(8,128)(2,1)S(1)}, bf16[2,2,64,256]{3,2,1,0:T(8,128)(2,1)S(1)}, u32[]{:S(2)}, u32[]{:S(2)}) collective-permute-start(bf16[2,2,64,256]{3,2,1,0:T(8,128)(2,1)S(1)} %collective-permute-done.8.refs_9_), channel_id=1, source_target_pairs={{0,2},{2,0},{4,6},{6,4},{8,10},{10,8},{12,14},{14,12},{1,3},{3,1},... | collective-permute-start | bytes 393224 | tf_op jit(solution)/shard_map/ppermute | solution.py:282
  24.9 1.5 %collective-permute-start.10 = (bf16[2,2,64,256]{3,2,1,0:T(8,128)(2,1)S(1)}, bf16[2,2,64,256]{3,2,1,0:T(8,128)(2,1)S(1)}, u32[]{:S(2)}, u32[]{:S(2)}) collective-permute-start(bf16[2,2,64,256]{3,2,1,0:T(8,128)(2,1)S(1)} %collective-permute-done.6.refs_7_), channel_id=1, source_target_pairs={{0,2},{2,0},{4,6},{6,4},{8,10},{10,8},{12,14},{14,12},{1,3},{3,1},... | collective-permute-start | bytes 393224 | tf_op jit(solution)/shard_map/ppermute | solution.py:282
  26.5 1.5 %collective-permute-start.5 = (bf16[4,2,48,256]{3,2,1,0:T(8,128)(2,1)S(1)}, bf16[4,2,48,256]{3,2,1,0:T(8,128)(2,1)S(1)}, u32[]{:S(2)}, u32[]{:S(2)}) collective-permute-start(bf16[4,2,48,256]{3,2,1,0:T(8,128)(2,1)S(1)} %collective-permute-done.3.pb_ref.rest_1_.refs_3_), channel_id=1, source_target_pairs={{0,16},{16,0},{1,17},{17,1},{2,18},{18,2},{3,19},{19,3},{4,20},{20... | collective-permute-start | bytes 589832 | tf_op jit(solution)/shard_map/ppermute | solution.py:285
  28.0 0.7 compare_select_fusion.6
  28.7 1.3 %reshape.251 = bf16[64,2,2,7,128]{4,3,2,1,0:T(8,128)(2,1)S(1)} reshape(bf16[1,64,2,1792]{3,2,1,0:T(2,128)(2,1)} %param.8) | data formatting | bytes 917504 | tf_op jit(solution)/shard_map/reshape;squeeze | solution.py:317
  30.7 1.4 %collective-permute-done.5.pd_ref.rest_3_.refs_5_ = bf16[4,2,48,256]{3,2,1,0:T(8,128)(2,1)S(1)} collective-permute-done((bf16[4,2,48,256]{3,2,1,0:T(8,128)(2,1)S(1)}, bf16[4,2,48,256]{3,2,1,0:T(8,128)(2,1)S(1)}, u32[]{:S(2)}, u32[]{:S(2)}) %collective-permute-start.5) | collective-permute-done | bytes 196640 | tf_op jit(solution)/shard_map/ppermute | solution.py:285
  32.1 4.6 %prefix_forward.1 = (bf16[2,896,768]{2,1,0:T(8,128)(2,1)S(1)}, f32[2,896,256]{2,1,0:T(8,128)S(1)}, f32[2,896,128]{2,1,0:T(8,128)S(1)}) custom-call(f32[2,8,768]{2,1,0:T(8,128)S(1)} %broadcast_in_dim.52.bias_ref, bf16[2,896,128]{2,1,0:T(8,128)(2,1)S(1)} %bitcast.86, bf16[4,2,48,256]{3,2,1,0:T(8,128)(2,1)S(1)} %pad_maximum_fusion.pa_ref.rest_0_.refs_2_, ...), custom_call_target="tpu_custom_call" | custom-call | flops 704643072 | bytes 8388608 | tf_op jit(solution)/shard_map/prefix_forward/pallas_call | solution.py:352
  36.9 5.4 %middle.1 = (bf16[2,896,128]{2,1,0:T(8,128)(2,1)S(1)}, bf16[2,896,128]{2,1,0:T(8,128)(2,1)S(1)}, f32[2,896,128]{2,1,0:T(8,128)S(1)}, bf16[2,896,512]{2,1,0:T(8,1...) custom-call(f32[2,64,128]{2,1,0:T(8,128)S(1)} %broadcast_in_dim.47.r, ...), custom_call_target="tpu_custom_call" | custom-call | flops 1174405120 | bytes 12582912 | tf_op jit(solution)/shard_map/middle/pallas_call | solution.py:372
  42.4 1.2 %copy-done = bf16[2,896,512]{2,1,0:T(8,128)(2,1)} copy-done((bf16[2,896,512]{2,1,0:T(8,128)(2,1)}, bf16[2,896,512]{2,1,0:T(8,128)(2,1)S(1)}, u32[]{:S(2)}) %copy-start) | copy-done | bytes 1835032
  43.7 0.7 copy-done.27
  45.8 0.9 %copy-done.9 = bf16[4,2,48,256]{3,2,1,0:T(8,128)(2,1)S(1)} copy-done((bf16[4,2,48,256]{3,2,1,0:T(8,128)(2,1)S(1)}, bf16[4,2,48,256]{3,2,1,0:T(8,128)(2,1)}, u32[]{:S(2)}) %copy-start.9) | copy-done | bytes 196632
  46.7 3.1 %prefix_backward.1 = (bf16[2,896,768]{2,1,0:T(8,128)(2,1)S(1)}, bf16[2,384,256]{2,1,0:T(8,128)(2,1)S(1)}, bf16[2,192,256]{2,1,0:T(8,128)(2,1)S(1)}, bf16[2,192,256]{2,1,0:T(8,128)(2,1)}) custom-call(bf16[2,896,128]{2,1,0:T(8,128)(2,1)S(1)} %bitcast.88, bf16[2,896,768]{2,1,0:T(8,128)(2,1)S(1)} %get-tuple-element.24.p_ref, ...), custom_call_target="tpu_custom_call" | custom-call | flops 1056964608 | bytes 12582912 | tf_op jit(solution)/shard_map/prefix_backward/pallas_call | solution.py:407
  49.8 1.6 %collective-permute-start.19 = (bf16[2,192,256]{2,1,0:T(8,128)(2,1)}, bf16[2,192,256]{2,1,0:T(8,128)(2,1)}, u32[]{:S(2)}, u32[]{:S(2)}) collective-permute-start(bf16[2,192,256]{2,1,0:T(8,128)(2,1)} %get-tuple-element.35), channel_id=1, source_target_pairs={{0,16},{16,0},{1,17},{17,1},{2,18},{18,2},{3,19},{19,3},{4,20},{20... | collective-permute-start | bytes 589832 | tf_op jit(solution)/shard_map/ppermute | solution.py:285
  51.3 1.1 %copy.53 = bf16[2,2,7,64,128]{4,2,0,3,1:T(8,128)(2,1)} copy(bf16[2,2,7,64,128]{4,3,2,1,0:T(8,128)(2,1)S(1)} %bitcast.91) | data formatting | bytes 917504 | tf_op jit(solution)/shard_map/reshape | solution.py:321
  52.5 2.3 %reshape.245 = bf16[1,64,2,1792]{3,1,2,0:T(8,128)(2,1)} reshape(bf16[64,2,2,7,128]{4,3,2,0,1:T(8,128)(2,1)} %bitcast.92) | data formatting | bytes 917504 | tf_op jit(solution)/shard_map/reshape | solution.py:322
  54.8 2.3 %copy.31 = bf16[1,64,2,1792]{3,2,1,0:T(2,128)(2,1)} copy(bf16[1,64,2,1792]{3,1,2,0:T(8,128)(2,1)} %reshape.245) | data formatting | bytes 917504 | tf_op jit(solution)/shard_map/reshape | solution.py:322
  57.5 1.5 %collective-permute-start.15 = (bf16[2,2,2,64,256]{4,3,2,1,0:T(8,128)(2,1)}, bf16[2,2,2,64,256]{4,3,2,1,0:T(8,128)(2,1)}, u32[]{:S(2)}, u32[]{:S(2)}) collective-permute-start(bf16[2,2,2,64,256]{4,3,2,1,0:T(8,128)(2,1)} %copy-done.31), channel_id=1, source_target_pairs={{0,2},{2,0},{4,6},{6,4},{8,10},{10,8},{12,14},{14,12},{1,3},{3,1},... | collective-permute-start | bytes 786440 | tf_op jit(solution)/shard_map/ppermute | solution.py:282
  59.1 1.5 %copy-done.1 = bf16[2,896,512]{2,1,0:T(8,128)(2,1)S(1)} copy-done((bf16[2,896,512]{2,1,0:T(8,128)(2,1)S(1)}, bf16[2,896,512]{2,1,0:T(8,128)(2,1)}, u32[]{:S(2)}) %copy-start.1) | copy-done | bytes 1835032
  60.6 0.9 %copy-done.10 = bf16[4,2,48,256]{3,2,1,0:T(8,128)(2,1)S(1)} copy-done((bf16[4,2,48,256]{3,2,1,0:T(8,128)(2,1)S(1)}, bf16[4,2,48,256]{3,2,1,0:T(8,128)(2,1)}, u32[]{:S(2)}) %copy-start.10) | copy-done | bytes 196632
  61.5 0.9 copy-done.12
  62.4 0.9 copy-done.14
  63.3 0.9 copy-done.16
  64.2 0.9 copy-done.18
  65.1 0.9 copy-done.20
  66.0 0.9 copy-done.22
  66.9 0.9 copy-done.24
  67.8 2.0 %query_backward.1 = bf16[2,896,128]{2,1,0:T(8,128)(2,1)S(1)} custom-call(bf16[2,896,768]{2,1,0:T(8,128)(2,1)S(1)} %get-tuple-element.27.refs_0_, bf16[2,896,512]{2,1,0:T(8,128)(2,1)S(1)} %copy-done.1, bf16[4,2,48,256]{3,2,1,0:T(8,128)(2,1)S(1)} %pad_maximum_fusion.pa_ref.rest_0_.refs_2_, bf16[4,2,48,256]{3,2,1,0:T(8,128)(2,1)S(1)} %copy-done.7, ...), custom_call_target="tpu_custom_call" | custom-call | flops 587202560 | bytes 8388608 | tf_op jit(solution)/shard_map/query_backward/pallas_call | solution.py:432
  70.7 1.2 %copy.33 = bf16[1,64,2,1792]{3,2,1,0:T(2,128)(2,1)} copy(bf16[1,64,2,1792]{3,1,2,0:T(8,128)(2,1)S(1)} %reshape.247) | data formatting | bytes 917504 | tf_op jit(solution)/shard_map/reshape | solution.py:322
  72.5 1.0 %add_convert_fusion.1 = bf16[2,192,256]{2,1,0:T(8,128)(2,1)S(1)} fusion(bf16[2,192,256]{2,1,0:T(8,128)(2,1)} %collective-permute-done.19, bf16[2,384,256]{2,1,0:T(8,128)(2,1)S(1)} %copy-done.26), kind=kLoop, calls=%fused_computation.5 | loop fusion | flops 393216 | bytes 589824 | tf_op jit(solution)/shard_map/convert_element_type | solution.py:450
  74.0 1.0 %convert_add_fusion = f32[2,2,2,64,256]{4,3,2,1,0:T(8,128)S(1)} fusion(bf16[2,2,2,64,256]{4,3,2,1,0:T(8,128)(2,1)} %collective-permute-done.13, bf16[2,2,2,64,256]{4,3,2,1,0:T(8,128)(2,1)S(1)} %copy-done.30), kind=kLoop, calls=%fused_computation.3 | loop fusion | flops 393216 | bytes 1048576 | tf_op jit(solution)/shard_map/add | solution.py:459
  75.0 1.2 %collective-permute-start.14 = (bf16[2,2,64,256]{3,2,1,0:T(8,128)(2,1)S(1)}, bf16[2,2,64,256]{3,2,1,0:T(8,128)(2,1)S(1)}, u32[]{:S(2)}, u32[]{:S(2)}) collective-permute-start(bf16[2,2,64,256]{3,2,1,0:T(8,128)(2,1)S(1)} %fusion.4), channel_id=1, source_target_pairs={{0,4},{2,6},{4,0},{6,2},{8,12},{10,14},{12,8},{14,10},{1,5},{3,7},... | collective-permute-start | bytes 393224 | tf_op jit(solution)/shard_map/ppermute | solution.py:279
  76.2 1.0 %add_convert_fusion = bf16[2,2,2,64,256]{4,3,2,1,0:T(8,128)(2,1)S(1)} fusion(bf16[2,2,2,64,256]{4,3,2,1,0:T(8,128)(2,1)} %collective-permute-done.15, bf16[2,2,2,64,256]{4,3,2,1,0:T(8,128)(2,1)S(1)} %copy-done.28), kind=kLoop, calls=%fused_computation.2 | loop fusion | flops 524288 | bytes 786432 | tf_op jit(solution)/shard_map/convert_element_type | solution.py:458
  77.3 1.8 %collective-permute-start.16 = (bf16[2,2,64,256]{3,2,1,0:T(8,128)(2,1)S(1)}, bf16[2,2,64,256]{3,2,1,0:T(8,128)(2,1)S(1)}, u32[]{:S(2)}, u32[]{:S(2)}) collective-permute-start(bf16[2,2,64,256]{3,2,1,0:T(8,128)(2,1)S(1)} %get-tuple-element.48), channel_id=1, source_target_pairs={{0,8},{2,10},{4,12},{6,14},{8,0},{10,2},{12,4},{14,6},{1,9},{3,11}... | collective-permute-start | bytes 393224 | tf_op jit(solution)/shard_map/ppermute | solution.py:279
  79.1 1.5 %collective-permute-start.17 = (bf16[2,2,64,256]{3,2,1,0:T(8,128)(2,1)S(1)}, bf16[2,2,64,256]{3,2,1,0:T(8,128)(2,1)S(1)}, u32[]{:S(2)}, u32[]{:S(2)}) collective-permute-start(bf16[2,2,64,256]{3,2,1,0:T(8,128)(2,1)S(1)} %get-tuple-element.49), channel_id=1, source_target_pairs={{0,12},{2,14},{4,8},{6,10},{8,4},{10,6},{12,0},{14,2},{1,13},{3,15... | collective-permute-start | bytes 393224 | tf_op jit(solution)/shard_map/ppermute | solution.py:279
  81.0 2.2 %collective-permute-start.23 = (bf16[2,48,256]{2,1,0:T(8,128)(2,1)S(1)}, bf16[2,48,256]{2,1,0:T(8,128)(2,1)S(1)}, u32[]{:S(2)}, u32[]{:S(2)}) collective-permute-start(bf16[2,48,256]{2,1,0:T(8,128)(2,1)S(1)} %get-tuple-element.51), channel_id=1, source_target_pairs={{0,12},{2,14},{4,8},{6,10},{8,4},{10,6},{12,0},{14,2},{1,13},{3,15... | collective-permute-start | bytes 147464 | tf_op jit(solution)/shard_map/ppermute | solution.py:279
  83.2 1.1 %collective-permute-start.22 = (bf16[2,48,256]{2,1,0:T(8,128)(2,1)S(1)}, bf16[2,48,256]{2,1,0:T(8,128)(2,1)S(1)}, u32[]{:S(2)}, u32[]{:S(2)}) collective-permute-start(bf16[2,48,256]{2,1,0:T(8,128)(2,1)S(1)} %get-tuple-element.52), channel_id=1, source_target_pairs={{0,8},{2,10},{4,12},{6,14},{8,0},{10,2},{12,4},{14,6},{1,9},{3,11}... | collective-permute-start | bytes 147464 | tf_op jit(solution)/shard_map/ppermute | solution.py:279
  84.3 4.8 %collective-permute-done.16 = bf16[2,2,64,256]{3,2,1,0:T(8,128)(2,1)S(1)} collective-permute-done((bf16[2,2,64,256]{3,2,1,0:T(8,128)(2,1)S(1)}, bf16[2,2,64,256]{3,2,1,0:T(8,128)(2,1)S(1)}, u32[]{:S(2)}, u32[]{:S(2)}) %collective-permute-start.16) | collective-permute-done | bytes 131104 | tf_op jit(solution)/shard_map/ppermute | solution.py:279
  89.1 0.7 copy.37
  90.5 1.0 %collective-permute-done.22 = bf16[2,48,256]{2,1,0:T(8,128)(2,1)S(1)} collective-permute-done((bf16[2,48,256]{2,1,0:T(8,128)(2,1)S(1)}, bf16[2,48,256]{2,1,0:T(8,128)(2,1)S(1)}, u32[]{:S(2)}, u32[]{:S(2)}) %collective-permute-start.22) | collective-permute-done | bytes 49184 | tf_op jit(solution)/shard_map/ppermute | solution.py:279
  (118 shorter events, 9.3 us)
Async XLA Ops:
  0.6 29.6 %copy-start.35 = (bf16[1,64,2,1792]{3,2,1,0:T(2,128)(2,1)S(1)}, bf16[1,64,2,1792]{3,2,1,0:T(2,128)(2,1)}, u32[]{:S(2)}) copy-start(bf16[1,64,2,1792]{3,2,1,0:T(2,128)(2,1)} %param.13) | copy-start | bytes 1376260
  1.5 11.1 %collective-permute-start.1 = (bf16[2,48,256]{2,1,0:T(8,128)(2,1)S(1)}, bf16[2,48,256]{2,1,0:T(8,128)(2,1)S(1)}, u32[]{:S(2)}, u32[]{:S(2)}) collective-permute-start(bf16[2,48,256]{2,1,0:T(8,128)(2,1)S(1)} %get-tuple-element.58), channel_id=1, source_target_pairs={{0,8},{2,10},{4,12},{6,14},{8,0},{10,2},{12,4},{14,6},{1,9},{3,11}... | collective-permute-start | bytes 147464 | tf_op jit(solution)/shard_map/ppermute | solution.py:279
  5.6 7.7 %collective-permute-start = (bf16[2,48,256]{2,1,0:T(8,128)(2,1)S(1)}, bf16[2,48,256]{2,1,0:T(8,128)(2,1)S(1)}, u32[]{:S(2)}, u32[]{:S(2)}) collective-permute-start(bf16[2,48,256]{2,1,0:T(8,128)(2,1)S(1)} %get-tuple-element.58), channel_id=1, source_target_pairs={{0,4},{2,6},{4,0},{6,2},{8,12},{10,14},{12,8},{14,10},{1,5},{3,7},... | collective-permute-start | bytes 147464 | tf_op jit(solution)/shard_map/ppermute | solution.py:279
  7.2 6.4 %collective-permute-start.2 = (bf16[2,48,256]{2,1,0:T(8,128)(2,1)S(1)}, bf16[2,48,256]{2,1,0:T(8,128)(2,1)S(1)}, u32[]{:S(2)}, u32[]{:S(2)}) collective-permute-start(bf16[2,48,256]{2,1,0:T(8,128)(2,1)S(1)} %get-tuple-element.58), channel_id=1, source_target_pairs={{0,12},{2,14},{4,8},{6,10},{8,4},{10,6},{12,0},{14,2},{1,13},{3,15... | collective-permute-start | bytes 147464 | tf_op jit(solution)/shard_map/ppermute | solution.py:279
  8.1 9.3 %collective-permute-start.8 = (bf16[2,2,64,256]{3,2,1,0:T(8,128)(2,1)S(1)}, bf16[2,2,64,256]{3,2,1,0:T(8,128)(2,1)S(1)}, u32[]{:S(2)}, u32[]{:S(2)}) collective-permute-start(bf16[2,2,64,256]{3,2,1,0:T(8,128)(2,1)S(1)} %pad_maximum_fusion.1.refs_6_), channel_id=1, source_target_pairs={{0,12},{2,14},{4,8},{6,10},{8,4},{10,6},{12,0},{14,2},{1,13},{3,15... | collective-permute-start | bytes 393224 | tf_op jit(solution)/shard_map/ppermute | solution.py:279
  12.0 10.9 %collective-permute-start.7 = (bf16[2,2,64,256]{3,2,1,0:T(8,128)(2,1)S(1)}, bf16[2,2,64,256]{3,2,1,0:T(8,128)(2,1)S(1)}, u32[]{:S(2)}, u32[]{:S(2)}) collective-permute-start(bf16[2,2,64,256]{3,2,1,0:T(8,128)(2,1)S(1)} %pad_maximum_fusion.1.refs_6_), channel_id=1, source_target_pairs={{0,8},{2,10},{4,12},{6,14},{8,0},{10,2},{12,4},{14,6},{1,9},{3,11}... | collective-permute-start | bytes 393224 | tf_op jit(solution)/shard_map/ppermute | solution.py:279
  12.6 11.9 %collective-permute-start.6 = (bf16[2,2,64,256]{3,2,1,0:T(8,128)(2,1)S(1)}, bf16[2,2,64,256]{3,2,1,0:T(8,128)(2,1)S(1)}, u32[]{:S(2)}, u32[]{:S(2)}) collective-permute-start(bf16[2,2,64,256]{3,2,1,0:T(8,128)(2,1)S(1)} %pad_maximum_fusion.1.refs_6_), channel_id=1, source_target_pairs={{0,4},{2,6},{4,0},{6,2},{8,12},{10,14},{12,8},{14,10},{1,5},{3,7},... | collective-permute-start | bytes 393224 | tf_op jit(solution)/shard_map/ppermute | solution.py:279
  13.6 11.3 %collective-permute-start.4 = (bf16[4,2,48,256]{3,2,1,0:T(8,128)(2,1)S(1)}, bf16[4,2,48,256]{3,2,1,0:T(8,128)(2,1)S(1)}, u32[]{:S(2)}, u32[]{:S(2)}) collective-permute-start(bf16[4,2,48,256]{3,2,1,0:T(8,128)(2,1)S(1)} %pad_maximum_fusion.pa_ref.rest_0_.refs_2_), channel_id=1, source_target_pairs={{0,16},{16,0},{1,17},{17,1},{2,18},{18,2},{3,19},{19,3},{4,20},{20... | collective-permute-start | bytes 589832 | tf_op jit(solution)/shard_map/ppermute | solution.py:285
  15.2 11.3 %collective-permute-start.3 = (bf16[4,2,48,256]{3,2,1,0:T(8,128)(2,1)S(1)}, bf16[4,2,48,256]{3,2,1,0:T(8,128)(2,1)S(1)}, u32[]{:S(2)}, u32[]{:S(2)}) collective-permute-start(bf16[4,2,48,256]{3,2,1,0:T(8,128)(2,1)S(1)} %pad_maximum_fusion.pa_ref.rest_0_.refs_2_), channel_id=1, source_target_pairs={{0,2},{2,0},{4,6},{6,4},{8,10},{10,8},{12,14},{14,12},{1,3},{3,1},... | collective-permute-start | bytes 589832 | tf_op jit(solution)/shard_map/ppermute | solution.py:282
  17.4 19.5 %copy-start.11 = (bf16[2,2,64,256]{3,2,1,0:T(8,128)(2,1)}, bf16[2,2,64,256]{3,2,1,0:T(8,128)(2,1)S(1)}, u32[]{:S(2)}) copy-start(bf16[2,2,64,256]{3,2,1,0:T(8,128)(2,1)S(1)} %collective-permute-done.8.refs_9_) | copy-start | bytes 393220
  17.4 19.3 %collective-permute-start.9 = (bf16[2,2,64,256]{3,2,1,0:T(8,128)(2,1)S(1)}, bf16[2,2,64,256]{3,2,1,0:T(8,128)(2,1)S(1)}, u32[]{:S(2)}, u32[]{:S(2)}) collective-permute-start(bf16[2,2,64,256]{3,2,1,0:T(8,128)(2,1)S(1)} %pad_maximum_fusion.1.refs_6_), channel_id=1, source_target_pairs={{0,2},{2,0},{4,6},{6,4},{8,10},{10,8},{12,14},{14,12},{1,3},{3,1},... | collective-permute-start | bytes 393224 | tf_op jit(solution)/shard_map/ppermute | solution.py:282
  22.9 14.0 %copy-start.13 = (bf16[2,2,64,256]{3,2,1,0:T(8,128)(2,1)}, bf16[2,2,64,256]{3,2,1,0:T(8,128)(2,1)S(1)}, u32[]{:S(2)}) copy-start(bf16[2,2,64,256]{3,2,1,0:T(8,128)(2,1)S(1)} %collective-permute-done.7.refs_8_) | copy-start | bytes 393220
  22.9 13.9 %collective-permute-start.12 = (bf16[2,2,64,256]{3,2,1,0:T(8,128)(2,1)S(1)}, bf16[2,2,64,256]{3,2,1,0:T(8,128)(2,1)S(1)}, u32[]{:S(2)}, u32[]{:S(2)}) collective-permute-start(bf16[2,2,64,256]{3,2,1,0:T(8,128)(2,1)S(1)} %collective-permute-done.8.refs_9_), channel_id=1, source_target_pairs={{0,2},{2,0},{4,6},{6,4},{8,10},{10,8},{12,14},{14,12},{1,3},{3,1},... | collective-permute-start | bytes 393224 | tf_op jit(solution)/shard_map/ppermute | solution.py:282
  24.4 12.5 %copy-start.15 = (bf16[2,2,64,256]{3,2,1,0:T(8,128)(2,1)}, bf16[2,2,64,256]{3,2,1,0:T(8,128)(2,1)S(1)}, u32[]{:S(2)}) copy-start(bf16[2,2,64,256]{3,2,1,0:T(8,128)(2,1)S(1)} %collective-permute-done.6.refs_7_) | copy-start | bytes 393220
  24.4 12.4 %collective-permute-start.11 = (bf16[2,2,64,256]{3,2,1,0:T(8,128)(2,1)S(1)}, bf16[2,2,64,256]{3,2,1,0:T(8,128)(2,1)S(1)}, u32[]{:S(2)}, u32[]{:S(2)}) collective-permute-start(bf16[2,2,64,256]{3,2,1,0:T(8,128)(2,1)S(1)} %collective-permute-done.7.refs_8_), channel_id=1, source_target_pairs={{0,2},{2,0},{4,6},{6,4},{8,10},{10,8},{12,14},{14,12},{1,3},{3,1},... | collective-permute-start | bytes 393224 | tf_op jit(solution)/shard_map/ppermute | solution.py:282
  24.9 11.8 %copy-start.2 = (bf16[4,2,48,256]{3,2,1,0:T(8,128)(2,1)}, bf16[4,2,48,256]{3,2,1,0:T(8,128)(2,1)S(1)}, u32[]{:S(2)}) copy-start(bf16[4,2,48,256]{3,2,1,0:T(8,128)(2,1)S(1)} %collective-permute-done.4.pc_ref.rest_2_.refs_4_) | copy-start | bytes 589828
  24.9 11.9 %collective-permute-start.10 = (bf16[2,2,64,256]{3,2,1,0:T(8,128)(2,1)S(1)}, bf16[2,2,64,256]{3,2,1,0:T(8,128)(2,1)S(1)}, u32[]{:S(2)}, u32[]{:S(2)}) collective-permute-start(bf16[2,2,64,256]{3,2,1,0:T(8,128)(2,1)S(1)} %collective-permute-done.6.refs_7_), channel_id=1, source_target_pairs={{0,2},{2,0},{4,6},{6,4},{8,10},{10,8},{12,14},{14,12},{1,3},{3,1},... | collective-permute-start | bytes 393224 | tf_op jit(solution)/shard_map/ppermute | solution.py:282
  26.5 10.3 %copy-start.5 = (bf16[4,2,48,256]{3,2,1,0:T(8,128)(2,1)}, bf16[4,2,48,256]{3,2,1,0:T(8,128)(2,1)S(1)}, u32[]{:S(2)}) copy-start(bf16[4,2,48,256]{3,2,1,0:T(8,128)(2,1)S(1)} %collective-permute-done.3.pb_ref.rest_1_.refs_3_) | copy-start | bytes 589828
  26.5 5.7 %collective-permute-start.5 = (bf16[4,2,48,256]{3,2,1,0:T(8,128)(2,1)S(1)}, bf16[4,2,48,256]{3,2,1,0:T(8,128)(2,1)S(1)}, u32[]{:S(2)}, u32[]{:S(2)}) collective-permute-start(bf16[4,2,48,256]{3,2,1,0:T(8,128)(2,1)S(1)} %collective-permute-done.3.pb_ref.rest_1_.refs_3_), channel_id=1, source_target_pairs={{0,16},{16,0},{1,17},{17,1},{2,18},{18,2},{3,19},{19,3},{4,20},{20... | collective-permute-start | bytes 589832 | tf_op jit(solution)/shard_map/ppermute | solution.py:285
  32.1 10.3 %copy-start.8 = (bf16[4,2,48,256]{3,2,1,0:T(8,128)(2,1)}, bf16[4,2,48,256]{3,2,1,0:T(8,128)(2,1)S(1)}, u32[]{:S(2)}) copy-start(bf16[4,2,48,256]{3,2,1,0:T(8,128)(2,1)S(1)} %collective-permute-done.5.pd_ref.rest_3_.refs_5_) | copy-start | bytes 589828
  36.7 8.3 %copy-start.17 = (bf16[2,2,64,256]{3,2,1,0:T(8,128)(2,1)}, bf16[2,2,64,256]{3,2,1,0:T(8,128)(2,1)S(1)}, u32[]{:S(2)}) copy-start(bf16[2,2,64,256]{3,2,1,0:T(8,128)(2,1)S(1)} %collective-permute-done.9.refs_10_) | copy-start | bytes 393220
  36.8 9.0 %copy-start.3 = (bf16[4,2,48,256]{3,2,1,0:T(8,128)(2,1)S(1)}, bf16[4,2,48,256]{3,2,1,0:T(8,128)(2,1)}, u32[]{:S(2)}) copy-start(bf16[4,2,48,256]{3,2,1,0:T(8,128)(2,1)} %copy-done.2) | copy-start | bytes 589828
  36.8 9.0 %copy-start.6 = (bf16[4,2,48,256]{3,2,1,0:T(8,128)(2,1)S(1)}, bf16[4,2,48,256]{3,2,1,0:T(8,128)(2,1)}, u32[]{:S(2)}) copy-start(bf16[4,2,48,256]{3,2,1,0:T(8,128)(2,1)} %copy-done.5) | copy-start | bytes 589828
  36.8 8.3 %copy-start.19 = (bf16[2,2,64,256]{3,2,1,0:T(8,128)(2,1)}, bf16[2,2,64,256]{3,2,1,0:T(8,128)(2,1)S(1)}, u32[]{:S(2)}) copy-start(bf16[2,2,64,256]{3,2,1,0:T(8,128)(2,1)S(1)} %collective-permute-done.12.refs_13_) | copy-start | bytes 393220
  36.8 8.3 %copy-start.21 = (bf16[2,2,64,256]{3,2,1,0:T(8,128)(2,1)}, bf16[2,2,64,256]{3,2,1,0:T(8,128)(2,1)S(1)}, u32[]{:S(2)}) copy-start(bf16[2,2,64,256]{3,2,1,0:T(8,128)(2,1)S(1)} %collective-permute-done.11.refs_12_) | copy-start | bytes 393220
  36.8 8.2 %copy-start.23 = (bf16[2,2,64,256]{3,2,1,0:T(8,128)(2,1)}, bf16[2,2,64,256]{3,2,1,0:T(8,128)(2,1)S(1)}, u32[]{:S(2)}) copy-start(bf16[2,2,64,256]{3,2,1,0:T(8,128)(2,1)S(1)} %collective-permute-done.10.refs_11_) | copy-start | bytes 393220
  42.4 1.3 %copy-start = (bf16[2,896,512]{2,1,0:T(8,128)(2,1)}, bf16[2,896,512]{2,1,0:T(8,128)(2,1)S(1)}, u32[]{:S(2)}) copy-start(bf16[2,896,512]{2,1,0:T(8,128)(2,1)S(1)} %get-tuple-element.28.refs_1_) | copy-start | bytes 5505028
  45.1 7.4 %copy-start.31 = (bf16[2,2,2,64,256]{4,3,2,1,0:T(8,128)(2,1)}, bf16[2,2,2,64,256]{4,3,2,1,0:T(8,128)(2,1)S(1)}, u32[]{:S(2)}) copy-start(bf16[2,2,2,64,256]{4,3,2,1,0:T(8,128)(2,1)S(1)} %get-tuple-element.32) | copy-start | bytes 786436
  49.8 2.7 %copy-start.25 = (bf16[2,384,256]{2,1,0:T(8,128)(2,1)}, bf16[2,384,256]{2,1,0:T(8,128)(2,1)S(1)}, u32[]{:S(2)}) copy-start(bf16[2,384,256]{2,1,0:T(8,128)(2,1)S(1)} %get-tuple-element.34) | copy-start | bytes 1179652
  49.8 2.7 %copy-start.33 = (bf16[2,192,256]{2,1,0:T(8,128)(2,1)}, bf16[2,192,256]{2,1,0:T(8,128)(2,1)S(1)}, u32[]{:S(2)}) copy-start(bf16[2,192,256]{2,1,0:T(8,128)(2,1)S(1)} %get-tuple-element.33) | copy-start | bytes 589828
  49.8 9.3 %copy-start.4 = (bf16[4,2,48,256]{3,2,1,0:T(8,128)(2,1)S(1)}, bf16[4,2,48,256]{3,2,1,0:T(8,128)(2,1)}, u32[]{:S(2)}) copy-start(bf16[4,2,48,256]{3,2,1,0:T(8,128)(2,1)} %copy-done.2) | copy-start | bytes 589828
  49.8 9.3 %copy-start.7 = (bf16[4,2,48,256]{3,2,1,0:T(8,128)(2,1)S(1)}, bf16[4,2,48,256]{3,2,1,0:T(8,128)(2,1)}, u32[]{:S(2)}) copy-start(bf16[4,2,48,256]{3,2,1,0:T(8,128)(2,1)} %copy-done.5) | copy-start | bytes 589828
  49.8 22.7 %collective-permute-start.19 = (bf16[2,192,256]{2,1,0:T(8,128)(2,1)}, bf16[2,192,256]{2,1,0:T(8,128)(2,1)}, u32[]{:S(2)}, u32[]{:S(2)}) collective-permute-start(bf16[2,192,256]{2,1,0:T(8,128)(2,1)} %get-tuple-element.35), channel_id=1, source_target_pairs={{0,16},{16,0},{1,17},{17,1},{2,18},{18,2},{3,19},{19,3},{4,20},{20... | collective-permute-start | bytes 589832 | tf_op jit(solution)/shard_map/ppermute | solution.py:285
  57.0 17.0 %collective-permute-start.13 = (bf16[2,2,2,64,256]{4,3,2,1,0:T(8,128)(2,1)}, bf16[2,2,2,64,256]{4,3,2,1,0:T(8,128)(2,1)}, u32[]{:S(2)}, u32[]{:S(2)}) collective-permute-start(bf16[2,2,2,64,256]{4,3,2,1,0:T(8,128)(2,1)} %copy-done.32), channel_id=1, source_target_pairs={{0,2},{2,0},{4,6},{6,4},{8,10},{10,8},{12,14},{14,12},{1,3},{3,1},... | collective-permute-start | bytes 786440 | tf_op jit(solution)/shard_map/ppermute | solution.py:282
  57.5 18.7 %collective-permute-start.15 = (bf16[2,2,2,64,256]{4,3,2,1,0:T(8,128)(2,1)}, bf16[2,2,2,64,256]{4,3,2,1,0:T(8,128)(2,1)}, u32[]{:S(2)}, u32[]{:S(2)}) collective-permute-start(bf16[2,2,2,64,256]{4,3,2,1,0:T(8,128)(2,1)} %copy-done.31), channel_id=1, source_target_pairs={{0,2},{2,0},{4,6},{6,4},{8,10},{10,8},{12,14},{14,12},{1,3},{3,1},... | collective-permute-start | bytes 786440 | tf_op jit(solution)/shard_map/ppermute | solution.py:282
  59.1 1.5 %copy-start.1 = (bf16[2,896,512]{2,1,0:T(8,128)(2,1)S(1)}, bf16[2,896,512]{2,1,0:T(8,128)(2,1)}, u32[]{:S(2)}) copy-start(bf16[2,896,512]{2,1,0:T(8,128)(2,1)} %copy-done) | copy-start | bytes 5505028
  69.8 2.1 %copy-start.34 = (bf16[2,192,256]{2,1,0:T(8,128)(2,1)S(1)}, bf16[2,192,256]{2,1,0:T(8,128)(2,1)}, u32[]{:S(2)}) copy-start(bf16[2,192,256]{2,1,0:T(8,128)(2,1)} %copy-done.33) | copy-start | bytes 589828
  69.8 2.6 %copy-start.26 = (bf16[2,384,256]{2,1,0:T(8,128)(2,1)S(1)}, bf16[2,384,256]{2,1,0:T(8,128)(2,1)}, u32[]{:S(2)}) copy-start(bf16[2,384,256]{2,1,0:T(8,128)(2,1)} %copy-done.25) | copy-start | bytes 1179652
  69.8 4.2 %copy-start.30 = (bf16[2,2,2,64,256]{4,3,2,1,0:T(8,128)(2,1)S(1)}, bf16[2,2,2,64,256]{4,3,2,1,0:T(8,128)(2,1)}, u32[]{:S(2)}) copy-start(bf16[2,2,2,64,256]{4,3,2,1,0:T(8,128)(2,1)} %copy-done.29) | copy-start | bytes 786436
  69.8 6.4 %copy-start.28 = (bf16[2,2,2,64,256]{4,3,2,1,0:T(8,128)(2,1)S(1)}, bf16[2,2,2,64,256]{4,3,2,1,0:T(8,128)(2,1)}, u32[]{:S(2)}) copy-start(bf16[2,2,2,64,256]{4,3,2,1,0:T(8,128)(2,1)} %copy-done.27) | copy-start | bytes 786436
  71.9 8.7 %collective-permute-start.18 = (bf16[2,192,256]{2,1,0:T(8,128)(2,1)S(1)}, bf16[2,192,256]{2,1,0:T(8,128)(2,1)S(1)}, u32[]{:S(2)}, u32[]{:S(2)}) collective-permute-start(bf16[2,192,256]{2,1,0:T(8,128)(2,1)S(1)} %copy-done.34), channel_id=1, source_target_pairs={{0,16},{16,0},{1,17},{17,1},{2,18},{18,2},{3,19},{19,3},{4,20},{20... | collective-permute-start | bytes 589832 | tf_op jit(solution)/shard_map/ppermute | solution.py:285
  73.4 7.2 %collective-permute-start.20 = (bf16[2,192,256]{2,1,0:T(8,128)(2,1)S(1)}, bf16[2,192,256]{2,1,0:T(8,128)(2,1)S(1)}, u32[]{:S(2)}, u32[]{:S(2)}) collective-permute-start(bf16[2,192,256]{2,1,0:T(8,128)(2,1)S(1)} %add_convert_fusion.1), channel_id=1, source_target_pairs={{0,2},{2,0},{4,6},{6,4},{8,10},{10,8},{12,14},{14,12},{1,3},{3,1},... | collective-permute-start | bytes 589832 | tf_op jit(solution)/shard_map/ppermute | solution.py:282
  75.0 8.2 %collective-permute-start.14 = (bf16[2,2,64,256]{3,2,1,0:T(8,128)(2,1)S(1)}, bf16[2,2,64,256]{3,2,1,0:T(8,128)(2,1)S(1)}, u32[]{:S(2)}, u32[]{:S(2)}) collective-permute-start(bf16[2,2,64,256]{3,2,1,0:T(8,128)(2,1)S(1)} %fusion.4), channel_id=1, source_target_pairs={{0,4},{2,6},{4,0},{6,2},{8,12},{10,14},{12,8},{14,10},{1,5},{3,7},... | collective-permute-start | bytes 393224 | tf_op jit(solution)/shard_map/ppermute | solution.py:279
  77.3 11.7 %collective-permute-start.16 = (bf16[2,2,64,256]{3,2,1,0:T(8,128)(2,1)S(1)}, bf16[2,2,64,256]{3,2,1,0:T(8,128)(2,1)S(1)}, u32[]{:S(2)}, u32[]{:S(2)}) collective-permute-start(bf16[2,2,64,256]{3,2,1,0:T(8,128)(2,1)S(1)} %get-tuple-element.48), channel_id=1, source_target_pairs={{0,8},{2,10},{4,12},{6,14},{8,0},{10,2},{12,4},{14,6},{1,9},{3,11}... | collective-permute-start | bytes 393224 | tf_op jit(solution)/shard_map/ppermute | solution.py:279
  79.1 9.9 %collective-permute-start.17 = (bf16[2,2,64,256]{3,2,1,0:T(8,128)(2,1)S(1)}, bf16[2,2,64,256]{3,2,1,0:T(8,128)(2,1)S(1)}, u32[]{:S(2)}, u32[]{:S(2)}) collective-permute-start(bf16[2,2,64,256]{3,2,1,0:T(8,128)(2,1)S(1)} %get-tuple-element.49), channel_id=1, source_target_pairs={{0,12},{2,14},{4,8},{6,10},{8,4},{10,6},{12,0},{14,2},{1,13},{3,15... | collective-permute-start | bytes 393224 | tf_op jit(solution)/shard_map/ppermute | solution.py:279
  80.7 9.8 %collective-permute-start.21 = (bf16[2,48,256]{2,1,0:T(8,128)(2,1)S(1)}, bf16[2,48,256]{2,1,0:T(8,128)(2,1)S(1)}, u32[]{:S(2)}, u32[]{:S(2)}) collective-permute-start(bf16[2,48,256]{2,1,0:T(8,128)(2,1)S(1)} %get-tuple-element.50), channel_id=1, source_target_pairs={{0,4},{2,6},{4,0},{6,2},{8,12},{10,14},{12,8},{14,10},{1,5},{3,7},... | collective-permute-start | bytes 147464 | tf_op jit(solution)/shard_map/ppermute | solution.py:279
  81.0 9.5 %collective-permute-start.23 = (bf16[2,48,256]{2,1,0:T(8,128)(2,1)S(1)}, bf16[2,48,256]{2,1,0:T(8,128)(2,1)S(1)}, u32[]{:S(2)}, u32[]{:S(2)}) collective-permute-start(bf16[2,48,256]{2,1,0:T(8,128)(2,1)S(1)} %get-tuple-element.51), channel_id=1, source_target_pairs={{0,12},{2,14},{4,8},{6,10},{8,4},{10,6},{12,0},{14,2},{1,13},{3,15... | collective-permute-start | bytes 147464 | tf_op jit(solution)/shard_map/ppermute | solution.py:279
  83.2 8.3 %collective-permute-start.22 = (bf16[2,48,256]{2,1,0:T(8,128)(2,1)S(1)}, bf16[2,48,256]{2,1,0:T(8,128)(2,1)S(1)}, u32[]{:S(2)}, u32[]{:S(2)}) collective-permute-start(bf16[2,48,256]{2,1,0:T(8,128)(2,1)S(1)} %get-tuple-element.52), channel_id=1, source_target_pairs={{0,8},{2,10},{4,12},{6,14},{8,0},{10,2},{12,4},{14,6},{1,9},{3,11}... | collective-permute-start | bytes 147464 | tf_op jit(solution)/shard_map/ppermute | solution.py:279
  (12 other events, 10.3 us)

commit v2 on v1

--- a/solution.py
+++ b/solution.py
@@ -4,7 +4,6 @@
 import jax.numpy as jnp
 from jax import lax
 from jax.experimental import pallas as pl
-from jax.experimental.layout import Layout, with_layout_constraint
 from jax.experimental.pallas import tpu as pltpu
 from jax.sharding import PartitionSpec as P
 
@@ -76,7 +75,8 @@
         lanes(p_ref, here, lambda c: jnp.exp2(s_s[here, c] * factor - top).astype(bf16))
         return carry
 
-    lax.fori_loop(0, rows // CHUNK, step, 0, unroll=7)
+    small = rows * s_s.shape[1] <= 2**19
+    lax.fori_loop(0, rows // CHUNK, step, 0, unroll=rows // CHUNK if small else 7)
 
 
 def blocks(total, rows, columns):
@@ -94,6 +94,41 @@
     for j in range(ds_s.shape[-1] // HEAD_DIM):
         columns = slice(j * HEAD_DIM, (j + 1) * HEAD_DIM)
         ds_s[:, columns] = (p[:, columns].astype(f32) * (dp[:, columns] - delta)).astype(bf16)
+
+
+def interleave(rows, batch):
+    size = rows * batch
+    at = lax.broadcasted_iota(jnp.int32, (size, size), 0)
+    source = lax.broadcasted_iota(jnp.int32, (size, size), 1)
+    return jnp.where(source == (at % rows) * batch + at // rows, 1.0, 0.0).astype(bf16)
+
+
+def gather_rows(raw_ref, out):
+    _, rows, batch, width = raw_ref.shape
+    select = interleave(rows, batch)
+    group = width // HEAD_DIM
+    for g in range(group):
+        x = raw_ref[0, :, :, g * HEAD_DIM : (g + 1) * HEAD_DIM].reshape(rows * batch, HEAD_DIM)
+        x = mm(select, x).astype(bf16)
+        for b in range(batch):
+            at = (b * group + g) * rows
+            out[at : at + rows, :] = x[b * rows : (b + 1) * rows]
+
+
+def scatter_rows(view, raw_ref):
+    _, rows, batch, width = raw_ref.shape
+    select = interleave(rows, batch)
+    group = width // HEAD_DIM
+    for g in range(group):
+        spans = [(b * group + g) * rows for b in range(batch)]
+        x = jnp.concatenate([view[at : at + rows, :] for at in spans], axis=0)
+        x = mm_tn(select, x).astype(bf16)
+        raw_ref[0, :, :, g * HEAD_DIM : (g + 1) * HEAD_DIM] = x.reshape(rows, batch, HEAD_DIM)
+
+
+def arrange_body(raw_q_ref, raw_do_ref, q_ref, do_ref):
+    gather_rows(raw_q_ref, q_ref.at[0])
+    gather_rows(raw_do_ref, do_ref.at[0])
 
 
 def prefix_forward_body(
@@ -233,19 +268,21 @@
         far_ref[t] = term[half + quarter :]
 
 
-def query_backward_body(pieces, dsa_ref, dsb_ref, *rest):
+def query_backward_body(pieces, out_ref, dsa_ref, dsb_ref, *rest):
     prefix = rest[:4]
     answer = rest[4 : 4 + pieces]
-    dq_ref, k_s, ka_s = rest[4 + pieces :]
+    raw_out_ref, raw_dq_ref, k_s, ka_s, dq_s = rest[4 + pieces :]
     scale = HEAD_DIM ** (-0.5)
     batch = ka_s.shape[0]
-    per = dq_ref.shape[1] // batch
+    per = dq_s.shape[0] // batch
     place_prefix(prefix, k_s, None)
     place_answer(answer, ka_s, None)
     for b in range(batch):
         rows = slice(b * per, (b + 1) * per)
         dq = mm(dsa_ref[0, rows, :], k_s[...]) + mm(dsb_ref[0, rows, :], ka_s[b])
-        dq_ref[0, rows, :] = (dq * scale).astype(bf16)
+        dq_s[rows, :] = (dq * scale).astype(bf16)
+    scatter_rows(out_ref.at[0], raw_out_ref)
+    scatter_rows(dq_s, raw_dq_ref)
 
 
 def on_device(
@@ -313,18 +350,6 @@
     live = jnp.where(row_places[None, :] < answer_length[0][:, None], 1.0, 0.0).astype(f32)
     live = jnp.broadcast_to(live[:, :, None], (batch, rows, HEAD_DIM))
 
-    def head_major(x):
-        x = x[0].reshape(rows, batch, kv, group, HEAD_DIM)
-        return x.transpose(2, 1, 3, 0, 4).reshape(kv, total, HEAD_DIM)
-
-    def row_major(x):
-        x = x.reshape(kv, batch, group, rows, HEAD_DIM)
-        x = x.transpose(3, 1, 0, 2, 4).reshape(queries.shape)
-        return with_layout_constraint(x, Layout((0, 1, 2, 3)))
-
-    query_view = head_major(queries)
-    grad_view = head_major(grad_out)
-
     def whole(shape):
         return pl.BlockSpec(shape, lambda c: (0,) * len(shape))
 
@@ -336,6 +361,7 @@
         last = len(shape) - 1
         return pl.BlockSpec(shape[:-1] + (HEAD_DIM,), lambda c: (0,) * last + (c,))
 
+    raw_spec = pl.BlockSpec((1, rows, batch, group * HEAD_DIM), lambda c: (0, 0, 0, c))
     q_shape = (kv, total, HEAD_DIM)
     q_spec = by_head(q_shape)
     prefix_specs = [lane_block(prefix_z.shape)] * 4
@@ -348,6 +374,17 @@
     stack_shape = (outer // 2,) + answer_own.shape
     unit_a = 2 * kv * total * prefix_total * HEAD_DIM
     unit_b = 2 * kv * total * answer_total * HEAD_DIM
+
+    query_view, grad_view = pl.pallas_call(
+        arrange_body,
+        grid=(kv,),
+        in_specs=[raw_spec, raw_spec],
+        out_specs=[q_spec, q_spec],
+        out_shape=[jax.ShapeDtypeStruct(q_shape, bf16)] * 2,
+        compiler_params=params(total * prefix_total),
+        cost_estimate=cost(4 * kv * total * HEAD_DIM * HEAD_DIM, 4 << 20, 0),
+        name="arrange",
+    )(queries, grad_out)
 
     probs_a, ol_a, top_a = pl.pallas_call(
         prefix_forward_body,
@@ -429,27 +466,30 @@
         name="prefix_backward",
     )(query_view, probs_a, grad_a, delta_a, *prefix)
 
-    dq_view = pl.pallas_call(
+    attention_out, grad_queries = pl.pallas_call(
         lambda *refs: query_backward_body(pieces, *refs),
         grid=(kv,),
-        in_specs=[by_head(pa_shape), by_head(pb_shape)] + prefix_specs + [answer_spec] * pieces,
-        out_specs=q_spec,
-        out_shape=jax.ShapeDtypeStruct(q_shape, bf16),
+        in_specs=[q_spec, by_head(pa_shape), by_head(pb_shape)]
+        + prefix_specs
+        + [answer_spec] * pieces,
+        out_specs=[raw_spec, raw_spec],
+        out_shape=[jax.ShapeDtypeStruct(queries.shape, bf16)] * 2,
         scratch_shapes=[
             pltpu.VMEM((prefix_total, HEAD_DIM), bf16),
             pltpu.VMEM((batch, answer_total, HEAD_DIM), bf16),
+            pltpu.VMEM((total, HEAD_DIM), bf16),
         ],
         compiler_params=params(total * prefix_total),
         cost_estimate=cost(unit_a + unit_b, 8 << 20, 0),
         name="query_backward",
-    )(ds_a, ds_b, *prefix, *answer)
+    )(out_view, ds_a, ds_b, *prefix, *answer)
 
     split = (2, outer, prefix_rows, kv * HEAD_DIM)
     half = prefix_total // 4
     far_got = swap_x(prefix_far).astype(f32) + prefix_own_sum[:, half:].astype(f32)
     y_got = swap_y(far_got.astype(bf16)).astype(f32)
-    near_got = swap_x(prefix_near).astype(f32) + prefix_own_sum[:, :half].astype(f32)
-    z_sum = (near_got + y_got).reshape(split)
+    near_got = swap_x(prefix_near).astype(f32)
+    z_sum = (near_got + prefix_own_sum[:, :half].astype(f32) + y_got).reshape(split)
     prefix_sum = z_sum[:, 0]
     for k in range(1, outer):
         prefix_sum = prefix_sum + swap_z(z_sum[:, k].astype(bf16), k).astype(f32)
@@ -467,8 +507,6 @@
     def answer_out(x):
         return x.transpose(1, 0, 2).reshape(answer_keys.shape)
 
-    attention_out = row_major(out_view)
-    grad_queries = row_major(dq_view)
     return (
         attention_out,
         grad_queries,

time: 92.8 us -> 71 us (0.77)
  local copies, waits for them, and re-layouts: 26 us -> 5.26 us
  waiting for transfers between devices: 12.3 us -> 16.5 us
  other arithmetic: 5.86 us -> 2.98 us
  Pallas kernels: 15.1 us -> 13.9 us
    unnamed x74 -> x6, local copies, waits for them, and re-layouts: 14.5 us -> 3.43 us
    reshape x6 -> x0, local copies, waits for them, and re-layouts: 7.73 us -> none  [the longest x4 6.31 us: row_major(): x = x.transpose(3, 1, 0, 2, 4).reshape(queries.shape)]
    ppermute x8, waiting for transfers between devices: 0.02 us -> 5.92 us  [swap_y(): return lax.ppermute(x, 'seq', [(i, i ^ 1) for i in range(size)])]
    pallas_call x1, Pallas kernels: 4.56 us -> 2.68 us  [on_device(): pl.pallas_call(prefix_forward_body, grid=(kv,), in_specs=[whole(prefix_bi...]
    another operation x2 -> x0, local copies, waits for them, and re-layouts: 1.61 us -> none  [head_major(): x = x[0].reshape(rows, batch, kv, group, HEAD_DIM)]
    pallas_call x1, Pallas kernels: 1.97 us -> 3.29 us  [on_device(): pl.pallas_call(lambda *refs: query_backward_body(pieces, *refs), grid=(kv...]
    convert_element_type x1, other arithmetic: 1.01 us -> 0.06 us  [on_device(): high = (near_high.astype(f32) + high_got.astype(f32)).astype(bf16)]
    add x1, other arithmetic: 1 us -> 0.06 us  [on_device(): low = near_low.astype(f32) + low_got.astype(f32)]
  transfers between devices with their start and end apart: 24 -> 24, of which waited for: 5 -> 7; matrix products, arithmetic and copies ran while one was open for 19% -> 7% of each run, Pallas kernels for 7% -> 10%
where the time goes in v2:
time: 71 us; the launch traced here: 70.6 us
  starting transfers between devices  31.1 us (44%)
  waiting for transfers between devices  16.5 us (23%)
  Pallas kernels  13.9 us (20%)
  local copies, waits for them, and re-layouts  5.26 us (7%)
  other arithmetic  2.98 us (4%)
  between operations  0.84 us (1%)
    ppermute x12, starting transfers between devices, swap_z(): return lax.ppermute(x, 'seq', [(i, i ^ 2 * k) for i in range(size)])  17.7 us
    ppermute x12, waiting for transfers between devices, swap_z(): return lax.ppermute(x, 'seq', [(i, i ^ 2 * k) for i in range(size)])  10 us
    ppermute x8, starting transfers between devices, swap_y(): return lax.ppermute(x, 'seq', [(i, i ^ 1) for i in range(size)])  8.3 us
    ppermute x8, waiting for transfers between devices, swap_y(): return lax.ppermute(x, 'seq', [(i, i ^ 1) for i in range(size)])  5.92 us
    ppermute x4, starting transfers between devices, swap_x(): return lax.ppermute(x, 'pair', [(0, 1), (1, 0)])  5.14 us
    pallas_call x1, Pallas kernels, on_device(): pl.pallas_call(lambda *refs: middle_body(pieces, *refs), grid=(kv,), in_s...  4.56 us
    unnamed x6, local copies, waits for them, and re-layouts  3.43 us
    pallas_call x1, Pallas kernels, on_device(): pl.pallas_call(lambda *refs: query_backward_body(pieces, *refs), grid=(kv...  3.29 us
  transfers between devices with their start and end apart: 24, of which 7 were waited for; matrix products, arithmetic and copies ran while one was open for 7% of the time, Pallas kernels for 10%

profile of v2, /device:TPU:0, one launch (start us, length us, event | category | flops | bytes accessed | tf_op | source)
XLA Modules:
  0.0 70.6 jit_solution(9857258110224808208)
XLA Ops:
  0.6 0.8 %fusion.11 = (bf16[1,2,48,256]{3,2,1,0:T(8,128)(2,1)S(1)}, bf16[2,48,256]{2,1,0:T(8,128)(2,1)S(1)}) fusion(bf16[1,48,256]{2,1,0:T(8,128)(2,1)} %bitcast.73, bf16[1,48,256]{2,1,0:T(8,128)(2,1)} %bitcast.74), kind=kLoop, calls=%fused_computation.48 | loop fusion | flops 24576 | bytes 147456 | tf_op jit(solution)/shard_map/stack | solution.py:326
  1.4 4.1 %collective-permute-start.1 = (bf16[2,48,256]{2,1,0:T(8,128)(2,1)S(1)}, bf16[2,48,256]{2,1,0:T(8,128)(2,1)S(1)}, u32[]{:S(2)}, u32[]{:S(2)}) collective-permute-start(bf16[2,48,256]{2,1,0:T(8,128)(2,1)S(1)} %get-tuple-element.60), channel_id=1, source_target_pairs={{0,8},{2,10},{4,12},{6,14},{8,0},{10,2},{12,4},{14,6},{1,9},{3,11}... | collective-permute-start | bytes 147464 | tf_op jit(solution)/shard_map/ppermute | solution.py:316
  5.5 1.6 %collective-permute-start = (bf16[2,48,256]{2,1,0:T(8,128)(2,1)S(1)}, bf16[2,48,256]{2,1,0:T(8,128)(2,1)S(1)}, u32[]{:S(2)}, u32[]{:S(2)}) collective-permute-start(bf16[2,48,256]{2,1,0:T(8,128)(2,1)S(1)} %get-tuple-element.60), channel_id=1, source_target_pairs={{0,4},{2,6},{4,0},{6,2},{8,12},{10,14},{12,8},{14,10},{1,5},{3,7},... | collective-permute-start | bytes 147464 | tf_op jit(solution)/shard_map/ppermute | solution.py:316
  7.1 0.9 %copy_bitcast_fusion = (bf16[1,2,64,256]{3,2,1,0:T(8,128)(2,1)S(1)}, bf16[1,2,64,256]{3,2,1,0:T(8,128)(2,1)S(1)}) fusion(bf16[1,64,2,256]{3,2,1,0:T(2,128)(2,1)} %param.10, bf16[1,64,2,256]{3,2,1,0:T(2,128)(2,1)} %param.9), kind=kLoop, calls=%fused_computation.22 | loop fusion | bytes 262144 | tf_op jit(solution)/shard_map/stack | solution.py:325
  8.0 3.9 %collective-permute-start.8 = (bf16[2,2,64,256]{3,2,1,0:T(8,128)(2,1)S(1)}, bf16[2,2,64,256]{3,2,1,0:T(8,128)(2,1)S(1)}, u32[]{:S(2)}, u32[]{:S(2)}) collective-permute-start(bf16[2,2,64,256]{3,2,1,0:T(8,128)(2,1)S(1)} %pad_maximum_fusion.1.refs_6_.refs_7_), channel_id=1, source_target_pairs={{0,12},{2,14},{4,8},{6,10},{8,4},{10,6},{12,0},{14,2},{1,13},{3,15... | collective-permute-start | bytes 393224 | tf_op jit(solution)/shard_map/ppermute | solution.py:316
  12.0 0.1 broadcast_add_fusion
  12.0 0.1 iota_add_fusion.1
  12.1 0.1 add.180
  12.3 0.1 compare_select_fusion.refs_1_
  12.4 0.1 add.190
  12.5 0.7 collective-permute-start.6
  13.2 0.3 collective-permute-done.2
  13.5 1.6 %collective-permute-start.4 = (bf16[4,2,48,256]{3,2,1,0:T(8,128)(2,1)S(1)}, bf16[4,2,48,256]{3,2,1,0:T(8,128)(2,1)S(1)}, u32[]{:S(2)}, u32[]{:S(2)}) collective-permute-start(bf16[4,2,48,256]{3,2,1,0:T(8,128)(2,1)S(1)} %pad_maximum_fusion.pa_ref.rest_0_.refs_3_), channel_id=1, source_target_pairs={{0,16},{16,0},{1,17},{17,1},{2,18},{18,2},{3,19},{19,3},{4,20},{20... | collective-permute-start | bytes 589832 | tf_op jit(solution)/shard_map/ppermute | solution.py:322
  15.1 1.5 %collective-permute-start.3 = (bf16[4,2,48,256]{3,2,1,0:T(8,128)(2,1)S(1)}, bf16[4,2,48,256]{3,2,1,0:T(8,128)(2,1)S(1)}, u32[]{:S(2)}, u32[]{:S(2)}) collective-permute-start(bf16[4,2,48,256]{3,2,1,0:T(8,128)(2,1)S(1)} %pad_maximum_fusion.pa_ref.rest_0_.refs_3_), channel_id=1, source_target_pairs={{0,2},{2,0},{4,6},{6,4},{8,10},{10,8},{12,14},{14,12},{1,3},{3,1},... | collective-permute-start | bytes 589832 | tf_op jit(solution)/shard_map/ppermute | solution.py:319
  16.6 0.7 %compare_select_fusion.1 = f32[2,768]{1,0:T(2,128)S(1)} fusion(s32[768]{0:T(1024)S(1)} %add.190, s32[2]{0:T(128)} %bitcast.76), kind=kLoop, calls=%fused_computation.30 | loop fusion | flops 3072 | bytes 9224 | tf_op jit(solution)/shard_map/jit(_where)/select_n | solution.py:343
  17.4 0.6 collective-permute-start.9
  18.0 4.8 %collective-permute-done.7.refs_8_.refs_9_ = bf16[2,2,64,256]{3,2,1,0:T(8,128)(2,1)S(1)} collective-permute-done((bf16[2,2,64,256]{3,2,1,0:T(8,128)(2,1)S(1)}, bf16[2,2,64,256]{3,2,1,0:T(8,128)(2,1)S(1)}, u32[]{:S(2)}, u32[]{:S(2)}) %collective-permute-start.7) | collective-permute-done | bytes 131104 | tf_op jit(solution)/shard_map/ppermute | solution.py:316
  22.8 1.5 %collective-permute-start.12 = (bf16[2,2,64,256]{3,2,1,0:T(8,128)(2,1)S(1)}, bf16[2,2,64,256]{3,2,1,0:T(8,128)(2,1)S(1)}, u32[]{:S(2)}, u32[]{:S(2)}) collective-permute-start(bf16[2,2,64,256]{3,2,1,0:T(8,128)(2,1)S(1)} %collective-permute-done.8.refs_9_.refs_10_), channel_id=1, source_target_pairs={{0,2},{2,0},{4,6},{6,4},{8,10},{10,8},{12,14},{14,12},{1,3},{3,1},... | collective-permute-start | bytes 393224 | tf_op jit(solution)/shard_map/ppermute | solution.py:319
  24.4 0.5 collective-permute-start.11
  24.9 1.5 %collective-permute-start.10 = (bf16[2,2,64,256]{3,2,1,0:T(8,128)(2,1)S(1)}, bf16[2,2,64,256]{3,2,1,0:T(8,128)(2,1)S(1)}, u32[]{:S(2)}, u32[]{:S(2)}) collective-permute-start(bf16[2,2,64,256]{3,2,1,0:T(8,128)(2,1)S(1)} %collective-permute-done.6.refs_7_.refs_8_), channel_id=1, source_target_pairs={{0,2},{2,0},{4,6},{6,4},{8,10},{10,8},{12,14},{14,12},{1,3},{3,1},... | collective-permute-start | bytes 393224 | tf_op jit(solution)/shard_map/ppermute | solution.py:319
  26.4 1.5 %collective-permute-start.5 = (bf16[4,2,48,256]{3,2,1,0:T(8,128)(2,1)S(1)}, bf16[4,2,48,256]{3,2,1,0:T(8,128)(2,1)S(1)}, u32[]{:S(2)}, u32[]{:S(2)}) collective-permute-start(bf16[4,2,48,256]{3,2,1,0:T(8,128)(2,1)S(1)} %collective-permute-done.3.pb_ref.rest_1_.refs_4_), channel_id=1, source_target_pairs={{0,16},{16,0},{1,17},{17,1},{2,18},{18,2},{3,19},{19,3},{4,20},{20... | collective-permute-start | bytes 589832 | tf_op jit(solution)/shard_map/ppermute | solution.py:322
  27.9 0.7 %compare_select_fusion.6 = f32[2,64]{1,0:T(2,128)S(1)} fusion(s32[64]{0:T(128)S(1)} %iota_add_fusion.2, s32[2]{0:T(128)} %bitcast.75), kind=kLoop, calls=%fused_computation.40 | loop fusion | flops 256 | bytes 776 | tf_op jit(solution)/shard_map/jit(_where)/select_n | solution.py:350
  28.6 1.0 %copy-done = bf16[1,64,2,1792]{3,2,1,0:T(2,128)(2,1)S(1)} copy-done((bf16[1,64,2,1792]{3,2,1,0:T(2,128)(2,1)S(1)}, bf16[1,64,2,1792]{3,2,1,0:T(2,128)(2,1)}, u32[]{:S(2)}) %copy-start) | copy-done | bytes 458776
  29.6 1.0 %copy-done.1 = bf16[1,64,2,1792]{3,2,1,0:T(2,128)(2,1)S(1)} copy-done((bf16[1,64,2,1792]{3,2,1,0:T(2,128)(2,1)S(1)}, bf16[1,64,2,1792]{3,2,1,0:T(2,128)(2,1)}, u32[]{:S(2)}) %copy-start.1) | copy-done | bytes 458776
  30.7 0.9 %arrange.1 = (bf16[2,896,128]{2,1,0:T(8,128)(2,1)S(1)}, bf16[2,896,128]{2,1,0:T(8,128)(2,1)S(1)}) custom-call(bf16[1,64,2,1792]{3,2,1,0:T(2,128)(2,1)S(1)} %copy-done, bf16[1,64,2,1792]{3,2,1,0:T(2,128)(2,1)S(1)} %copy-done.1), custom_call_target="tpu_custom_call" | custom-call | flops 117440512 | bytes 4194304 | tf_op jit(solution)/shard_map/arrange/pallas_call | solution.py:378
  31.5 0.6 collective-permute-done.5.pd_ref.rest_3_.refs_6_
  32.1 2.7 %prefix_forward.1 = (bf16[2,896,768]{2,1,0:T(8,128)(2,1)S(1)}, f32[2,896,256]{2,1,0:T(8,128)S(1)}, f32[2,896,128]{2,1,0:T(8,128)S(1)}) custom-call(f32[2,8,768]{2,1,0:T(8,128)S(1)} %broadcast_in_dim.52.bias_ref, bf16[2,896,128]{2,1,0:T(8,128)(2,1)S(1)} %get-tuple-element.25.q_ref.refs_2_, bf16[4,2,48,256]{3,2,1,0:T(8,128)(2,1)S(1)} %pad_maximum_fusion.pa_ref.rest_0_.refs_3_, ...), custom_call_target="tpu_custom_call" | custom-call | flops 704643072 | bytes 8388608 | tf_op jit(solution)/shard_map/prefix_forward/pallas_call | solution.py:389
  34.8 0.1 broadcast_in_dim.47.refs_0_
  34.9 4.6 %middle.1 = (bf16[2,896,128]{2,1,0:T(8,128)(2,1)S(1)}, bf16[2,896,128]{2,1,0:T(8,128)(2,1)S(1)}, f32[2,896,128]{2,1,0:T(8,128)S(1)}, bf16[2,896,512]{2,1,0:T(8,1...) custom-call(f32[2,64,128]{2,1,0:T(8,128)S(1)} %broadcast_in_dim.47.r, ...), custom_call_target="tpu_custom_call" | custom-call | flops 1174405120 | bytes 12582912 | tf_op jit(solution)/shard_map/middle/pallas_call | solution.py:409
  39.4 2.5 %prefix_backward.1 = (bf16[2,896,768]{2,1,0:T(8,128)(2,1)S(1)}, bf16[2,384,256]{2,1,0:T(8,128)(2,1)S(1)}, bf16[2,192,256]{2,1,0:T(8,128)(2,1)S(1)}, bf16[2,192,256]{2,1,0:T(8,128)(2,1)S(1)}) custom-call(bf16[2,896,128]{2,1,0:T(8,128)(2,1)S(1)} %get-tuple-element.25.q_ref.refs_2_, bf16[2,896,768]{2,1,0:T(8,128)(2,1)S(1)} %get-tuple-element.30.p_ref, ...), custom_call_target="tpu_custom_call" | custom-call | flops 1056964608 | bytes 12582912 | tf_op jit(solution)/shard_map/prefix_backward/pallas_call | solution.py:444
  41.9 1.6 %collective-permute-start.19 = (bf16[2,192,256]{2,1,0:T(8,128)(2,1)S(1)}, bf16[2,192,256]{2,1,0:T(8,128)(2,1)S(1)}, u32[]{:S(2)}, u32[]{:S(2)}) collective-permute-start(bf16[2,192,256]{2,1,0:T(8,128)(2,1)S(1)} %get-tuple-element.43), channel_id=1, source_target_pairs={{0,16},{16,0},{1,17},{17,1},{2,18},{18,2},{3,19},{19,3},{4,20},{20... | collective-permute-start | bytes 589832 | tf_op jit(solution)/shard_map/ppermute | solution.py:322
  43.5 0.5 collective-permute-start.13
  44.0 1.5 %collective-permute-start.15 = (bf16[2,2,2,64,256]{4,3,2,1,0:T(8,128)(2,1)S(1)}, bf16[2,2,2,64,256]{4,3,2,1,0:T(8,128)(2,1)S(1)}, u32[]{:S(2)}, u32[]{:S(2)}) collective-permute-start(bf16[2,2,2,64,256]{4,3,2,1,0:T(8,128)(2,1)S(1)} %get-tuple-element.40), channel_id=1, source_target_pairs={{0,2},{2,0},{4,6},{6,4},{8,10},{10,8},{12,14},{14,12},{1,3},{3,1},... | collective-permute-start | bytes 786440 | tf_op jit(solution)/shard_map/ppermute | solution.py:319
  45.5 0.5 collective-permute-start.18
  46.1 3.3 %query_backward.1 = (bf16[1,64,2,1792]{3,2,1,0:T(2,128)(2,1)}, bf16[1,64,2,1792]{3,2,1,0:T(2,128)(2,1)}) custom-call(bf16[2,896,128]{2,1,0:T(8,128)(2,1)S(1)} %get-tuple-element.29.refs_0_, bf16[2,896,768]{2,1,0:T(8,128)(2,1)S(1)} %get-tuple-element.33.refs_1_, bf16[2,896,512]{2,1,0:T(8,128)(2,1)S(1)} %get-tuple-element.34.refs_2_, ...), custom_call_target="tpu_custom_call" | custom-call | flops 587202560 | bytes 8388608 | tf_op jit(solution)/shard_map/query_backward/pallas_call | solution.py:469
  49.4 0.6 collective-permute-start.20
  50.0 2.7 %collective-permute-done.13 = bf16[2,2,2,64,256]{4,3,2,1,0:T(8,128)(2,1)S(1)} collective-permute-done((bf16[2,2,2,64,256]{4,3,2,1,0:T(8,128)(2,1)S(1)}, bf16[2,2,2,64,256]{4,3,2,1,0:T(8,128)(2,1)S(1)}, u32[]{:S(2)}, u32[]{:S(2)}) %collective-permute-start.13) | collective-permute-done | bytes 262176 | tf_op jit(solution)/shard_map/ppermute | solution.py:319
  52.8 0.5 collective-permute-start.14
  53.3 3.2 %collective-permute-done.15 = bf16[2,2,2,64,256]{4,3,2,1,0:T(8,128)(2,1)S(1)} collective-permute-done((bf16[2,2,2,64,256]{4,3,2,1,0:T(8,128)(2,1)S(1)}, bf16[2,2,2,64,256]{4,3,2,1,0:T(8,128)(2,1)S(1)}, u32[]{:S(2)}, u32[]{:S(2)}) %collective-permute-start.15) | collective-permute-done | bytes 262176 | tf_op jit(solution)/shard_map/ppermute | solution.py:319
  56.7 3.3 %collective-permute-start.17 = (bf16[2,2,64,256]{3,2,1,0:T(8,128)(2,1)S(1)}, bf16[2,2,64,256]{3,2,1,0:T(8,128)(2,1)S(1)}, u32[]{:S(2)}, u32[]{:S(2)}) collective-permute-start(bf16[2,2,64,256]{3,2,1,0:T(8,128)(2,1)S(1)} %get-tuple-element.51), channel_id=1, source_target_pairs={{0,12},{2,14},{4,8},{6,10},{8,4},{10,6},{12,0},{14,2},{1,13},{3,15... | collective-permute-start | bytes 393224 | tf_op jit(solution)/shard_map/ppermute | solution.py:316
  60.0 0.3 collective-permute-start.21
  60.3 2.7 %collective-permute-start.23 = (bf16[2,48,256]{2,1,0:T(8,128)(2,1)S(1)}, bf16[2,48,256]{2,1,0:T(8,128)(2,1)S(1)}, u32[]{:S(2)}, u32[]{:S(2)}) collective-permute-start(bf16[2,48,256]{2,1,0:T(8,128)(2,1)S(1)} %get-tuple-element.53), channel_id=1, source_target_pairs={{0,12},{2,14},{4,8},{6,10},{8,4},{10,6},{12,0},{14,2},{1,13},{3,15... | collective-permute-start | bytes 147464 | tf_op jit(solution)/shard_map/ppermute | solution.py:316
  63.0 0.6 collective-permute-start.22
  63.6 3.9 %collective-permute-done.16 = bf16[2,2,64,256]{3,2,1,0:T(8,128)(2,1)S(1)} collective-permute-done((bf16[2,2,64,256]{3,2,1,0:T(8,128)(2,1)S(1)}, bf16[2,2,64,256]{3,2,1,0:T(8,128)(2,1)S(1)}, u32[]{:S(2)}, u32[]{:S(2)}) %collective-permute-start.16) | collective-permute-done | bytes 131104 | tf_op jit(solution)/shard_map/ppermute | solution.py:316
  67.6 0.7 copy.19
  68.3 0.7 copy.18
  69.0 1.0 %collective-permute-done.22 = bf16[2,48,256]{2,1,0:T(8,128)(2,1)S(1)} collective-permute-done((bf16[2,48,256]{2,1,0:T(8,128)(2,1)S(1)}, bf16[2,48,256]{2,1,0:T(8,128)(2,1)S(1)}, u32[]{:S(2)}, u32[]{:S(2)}) %collective-permute-start.22) | collective-permute-done | bytes 49184 | tf_op jit(solution)/shard_map/ppermute | solution.py:316
  70.0 0.6 slice_bitcast_fusion.6
  (41 shorter events, 0.7 us)
Async XLA Ops:
  1.4 11.1 %collective-permute-start.1 = (bf16[2,48,256]{2,1,0:T(8,128)(2,1)S(1)}, bf16[2,48,256]{2,1,0:T(8,128)(2,1)S(1)}, u32[]{:S(2)}, u32[]{:S(2)}) collective-permute-start(bf16[2,48,256]{2,1,0:T(8,128)(2,1)S(1)} %get-tuple-element.60), channel_id=1, source_target_pairs={{0,8},{2,10},{4,12},{6,14},{8,0},{10,2},{12,4},{14,6},{1,9},{3,11}... | collective-permute-start | bytes 147464 | tf_op jit(solution)/shard_map/ppermute | solution.py:316
  5.5 7.7 %collective-permute-start = (bf16[2,48,256]{2,1,0:T(8,128)(2,1)S(1)}, bf16[2,48,256]{2,1,0:T(8,128)(2,1)S(1)}, u32[]{:S(2)}, u32[]{:S(2)}) collective-permute-start(bf16[2,48,256]{2,1,0:T(8,128)(2,1)S(1)} %get-tuple-element.60), channel_id=1, source_target_pairs={{0,4},{2,6},{4,0},{6,2},{8,12},{10,14},{12,8},{14,10},{1,5},{3,7},... | collective-permute-start | bytes 147464 | tf_op jit(solution)/shard_map/ppermute | solution.py:316
  7.1 6.4 %collective-permute-start.2 = (bf16[2,48,256]{2,1,0:T(8,128)(2,1)S(1)}, bf16[2,48,256]{2,1,0:T(8,128)(2,1)S(1)}, u32[]{:S(2)}, u32[]{:S(2)}) collective-permute-start(bf16[2,48,256]{2,1,0:T(8,128)(2,1)S(1)} %get-tuple-element.60), channel_id=1, source_target_pairs={{0,12},{2,14},{4,8},{6,10},{8,4},{10,6},{12,0},{14,2},{1,13},{3,15... | collective-permute-start | bytes 147464 | tf_op jit(solution)/shard_map/ppermute | solution.py:316
  8.0 9.3 %collective-permute-start.8 = (bf16[2,2,64,256]{3,2,1,0:T(8,128)(2,1)S(1)}, bf16[2,2,64,256]{3,2,1,0:T(8,128)(2,1)S(1)}, u32[]{:S(2)}, u32[]{:S(2)}) collective-permute-start(bf16[2,2,64,256]{3,2,1,0:T(8,128)(2,1)S(1)} %pad_maximum_fusion.1.refs_6_.refs_7_), channel_id=1, source_target_pairs={{0,12},{2,14},{4,8},{6,10},{8,4},{10,6},{12,0},{14,2},{1,13},{3,15... | collective-permute-start | bytes 393224 | tf_op jit(solution)/shard_map/ppermute | solution.py:316
  11.9 10.9 %collective-permute-start.7 = (bf16[2,2,64,256]{3,2,1,0:T(8,128)(2,1)S(1)}, bf16[2,2,64,256]{3,2,1,0:T(8,128)(2,1)S(1)}, u32[]{:S(2)}, u32[]{:S(2)}) collective-permute-start(bf16[2,2,64,256]{3,2,1,0:T(8,128)(2,1)S(1)} %pad_maximum_fusion.1.refs_6_.refs_7_), channel_id=1, source_target_pairs={{0,8},{2,10},{4,12},{6,14},{8,0},{10,2},{12,4},{14,6},{1,9},{3,11}... | collective-permute-start | bytes 393224 | tf_op jit(solution)/shard_map/ppermute | solution.py:316
  12.5 11.9 %collective-permute-start.6 = (bf16[2,2,64,256]{3,2,1,0:T(8,128)(2,1)S(1)}, bf16[2,2,64,256]{3,2,1,0:T(8,128)(2,1)S(1)}, u32[]{:S(2)}, u32[]{:S(2)}) collective-permute-start(bf16[2,2,64,256]{3,2,1,0:T(8,128)(2,1)S(1)} %pad_maximum_fusion.1.refs_6_.refs_7_), channel_id=1, source_target_pairs={{0,4},{2,6},{4,0},{6,2},{8,12},{10,14},{12,8},{14,10},{1,5},{3,7},... | collective-permute-start | bytes 393224 | tf_op jit(solution)/shard_map/ppermute | solution.py:316
  13.5 11.3 %collective-permute-start.4 = (bf16[4,2,48,256]{3,2,1,0:T(8,128)(2,1)S(1)}, bf16[4,2,48,256]{3,2,1,0:T(8,128)(2,1)S(1)}, u32[]{:S(2)}, u32[]{:S(2)}) collective-permute-start(bf16[4,2,48,256]{3,2,1,0:T(8,128)(2,1)S(1)} %pad_maximum_fusion.pa_ref.rest_0_.refs_3_), channel_id=1, source_target_pairs={{0,16},{16,0},{1,17},{17,1},{2,18},{18,2},{3,19},{19,3},{4,20},{20... | collective-permute-start | bytes 589832 | tf_op jit(solution)/shard_map/ppermute | solution.py:322
  15.1 11.3 %collective-permute-start.3 = (bf16[4,2,48,256]{3,2,1,0:T(8,128)(2,1)S(1)}, bf16[4,2,48,256]{3,2,1,0:T(8,128)(2,1)S(1)}, u32[]{:S(2)}, u32[]{:S(2)}) collective-permute-start(bf16[4,2,48,256]{3,2,1,0:T(8,128)(2,1)S(1)} %pad_maximum_fusion.pa_ref.rest_0_.refs_3_), channel_id=1, source_target_pairs={{0,2},{2,0},{4,6},{6,4},{8,10},{10,8},{12,14},{14,12},{1,3},{3,1},... | collective-permute-start | bytes 589832 | tf_op jit(solution)/shard_map/ppermute | solution.py:319
  17.4 17.4 %collective-permute-start.9 = (bf16[2,2,64,256]{3,2,1,0:T(8,128)(2,1)S(1)}, bf16[2,2,64,256]{3,2,1,0:T(8,128)(2,1)S(1)}, u32[]{:S(2)}, u32[]{:S(2)}) collective-permute-start(bf16[2,2,64,256]{3,2,1,0:T(8,128)(2,1)S(1)} %pad_maximum_fusion.1.refs_6_.refs_7_), channel_id=1, source_target_pairs={{0,2},{2,0},{4,6},{6,4},{8,10},{10,8},{12,14},{14,12},{1,3},{3,1},... | collective-permute-start | bytes 393224 | tf_op jit(solution)/shard_map/ppermute | solution.py:319
  22.8 11.9 %collective-permute-start.12 = (bf16[2,2,64,256]{3,2,1,0:T(8,128)(2,1)S(1)}, bf16[2,2,64,256]{3,2,1,0:T(8,128)(2,1)S(1)}, u32[]{:S(2)}, u32[]{:S(2)}) collective-permute-start(bf16[2,2,64,256]{3,2,1,0:T(8,128)(2,1)S(1)} %collective-permute-done.8.refs_9_.refs_10_), channel_id=1, source_target_pairs={{0,2},{2,0},{4,6},{6,4},{8,10},{10,8},{12,14},{14,12},{1,3},{3,1},... | collective-permute-start | bytes 393224 | tf_op jit(solution)/shard_map/ppermute | solution.py:319
  24.4 10.4 %collective-permute-start.11 = (bf16[2,2,64,256]{3,2,1,0:T(8,128)(2,1)S(1)}, bf16[2,2,64,256]{3,2,1,0:T(8,128)(2,1)S(1)}, u32[]{:S(2)}, u32[]{:S(2)}) collective-permute-start(bf16[2,2,64,256]{3,2,1,0:T(8,128)(2,1)S(1)} %collective-permute-done.7.refs_8_.refs_9_), channel_id=1, source_target_pairs={{0,2},{2,0},{4,6},{6,4},{8,10},{10,8},{12,14},{14,12},{1,3},{3,1},... | collective-permute-start | bytes 393224 | tf_op jit(solution)/shard_map/ppermute | solution.py:319
  24.9 9.9 %collective-permute-start.10 = (bf16[2,2,64,256]{3,2,1,0:T(8,128)(2,1)S(1)}, bf16[2,2,64,256]{3,2,1,0:T(8,128)(2,1)S(1)}, u32[]{:S(2)}, u32[]{:S(2)}) collective-permute-start(bf16[2,2,64,256]{3,2,1,0:T(8,128)(2,1)S(1)} %collective-permute-done.6.refs_7_.refs_8_), channel_id=1, source_target_pairs={{0,2},{2,0},{4,6},{6,4},{8,10},{10,8},{12,14},{14,12},{1,3},{3,1},... | collective-permute-start | bytes 393224 | tf_op jit(solution)/shard_map/ppermute | solution.py:319
  26.4 5.7 %collective-permute-start.5 = (bf16[4,2,48,256]{3,2,1,0:T(8,128)(2,1)S(1)}, bf16[4,2,48,256]{3,2,1,0:T(8,128)(2,1)S(1)}, u32[]{:S(2)}, u32[]{:S(2)}) collective-permute-start(bf16[4,2,48,256]{3,2,1,0:T(8,128)(2,1)S(1)} %collective-permute-done.3.pb_ref.rest_1_.refs_4_), channel_id=1, source_target_pairs={{0,16},{16,0},{1,17},{17,1},{2,18},{18,2},{3,19},{19,3},{4,20},{20... | collective-permute-start | bytes 589832 | tf_op jit(solution)/shard_map/ppermute | solution.py:322
  28.6 1.0 %copy-start = (bf16[1,64,2,1792]{3,2,1,0:T(2,128)(2,1)S(1)}, bf16[1,64,2,1792]{3,2,1,0:T(2,128)(2,1)}, u32[]{:S(2)}) copy-start(bf16[1,64,2,1792]{3,2,1,0:T(2,128)(2,1)} %raw_q_ref.1) | copy-start | bytes 1376260
  29.6 1.0 %copy-start.1 = (bf16[1,64,2,1792]{3,2,1,0:T(2,128)(2,1)S(1)}, bf16[1,64,2,1792]{3,2,1,0:T(2,128)(2,1)}, u32[]{:S(2)}) copy-start(bf16[1,64,2,1792]{3,2,1,0:T(2,128)(2,1)} %raw_do_ref.1) | copy-start | bytes 1376260
  41.9 7.4 %collective-permute-start.19 = (bf16[2,192,256]{2,1,0:T(8,128)(2,1)S(1)}, bf16[2,192,256]{2,1,0:T(8,128)(2,1)S(1)}, u32[]{:S(2)}, u32[]{:S(2)}) collective-permute-start(bf16[2,192,256]{2,1,0:T(8,128)(2,1)S(1)} %get-tuple-element.43), channel_id=1, source_target_pairs={{0,16},{16,0},{1,17},{17,1},{2,18},{18,2},{3,19},{19,3},{4,20},{20... | collective-permute-start | bytes 589832 | tf_op jit(solution)/shard_map/ppermute | solution.py:322
  43.5 9.2 %collective-permute-start.13 = (bf16[2,2,2,64,256]{4,3,2,1,0:T(8,128)(2,1)S(1)}, bf16[2,2,2,64,256]{4,3,2,1,0:T(8,128)(2,1)S(1)}, u32[]{:S(2)}, u32[]{:S(2)}) collective-permute-start(bf16[2,2,2,64,256]{4,3,2,1,0:T(8,128)(2,1)S(1)} %get-tuple-element.38), channel_id=1, source_target_pairs={{0,2},{2,0},{4,6},{6,4},{8,10},{10,8},{12,14},{14,12},{1,3},{3,1},... | collective-permute-start | bytes 786440 | tf_op jit(solution)/shard_map/ppermute | solution.py:319
  44.0 12.5 %collective-permute-start.15 = (bf16[2,2,2,64,256]{4,3,2,1,0:T(8,128)(2,1)S(1)}, bf16[2,2,2,64,256]{4,3,2,1,0:T(8,128)(2,1)S(1)}, u32[]{:S(2)}, u32[]{:S(2)}) collective-permute-start(bf16[2,2,2,64,256]{4,3,2,1,0:T(8,128)(2,1)S(1)} %get-tuple-element.40), channel_id=1, source_target_pairs={{0,2},{2,0},{4,6},{6,4},{8,10},{10,8},{12,14},{14,12},{1,3},{3,1},... | collective-permute-start | bytes 786440 | tf_op jit(solution)/shard_map/ppermute | solution.py:319
  45.5 14.4 %collective-permute-start.18 = (bf16[2,192,256]{2,1,0:T(8,128)(2,1)S(1)}, bf16[2,192,256]{2,1,0:T(8,128)(2,1)S(1)}, u32[]{:S(2)}, u32[]{:S(2)}) collective-permute-start(bf16[2,192,256]{2,1,0:T(8,128)(2,1)S(1)} %get-tuple-element.41), channel_id=1, source_target_pairs={{0,16},{16,0},{1,17},{17,1},{2,18},{18,2},{3,19},{19,3},{4,20},{20... | collective-permute-start | bytes 589832 | tf_op jit(solution)/shard_map/ppermute | solution.py:322
  49.4 10.5 %collective-permute-start.20 = (bf16[2,192,256]{2,1,0:T(8,128)(2,1)S(1)}, bf16[2,192,256]{2,1,0:T(8,128)(2,1)S(1)}, u32[]{:S(2)}, u32[]{:S(2)}) collective-permute-start(bf16[2,192,256]{2,1,0:T(8,128)(2,1)S(1)} %add_convert_fusion.1), channel_id=1, source_target_pairs={{0,2},{2,0},{4,6},{6,4},{8,10},{10,8},{12,14},{14,12},{1,3},{3,1},... | collective-permute-start | bytes 589832 | tf_op jit(solution)/shard_map/ppermute | solution.py:319
  52.8 10.3 %collective-permute-start.14 = (bf16[2,2,64,256]{3,2,1,0:T(8,128)(2,1)S(1)}, bf16[2,2,64,256]{3,2,1,0:T(8,128)(2,1)S(1)}, u32[]{:S(2)}, u32[]{:S(2)}) collective-permute-start(bf16[2,2,64,256]{3,2,1,0:T(8,128)(2,1)S(1)} %fusion.4), channel_id=1, source_target_pairs={{0,4},{2,6},{4,0},{6,2},{8,12},{10,14},{12,8},{14,10},{1,5},{3,7},... | collective-permute-start | bytes 393224 | tf_op jit(solution)/shard_map/ppermute | solution.py:316
  56.6 10.9 %collective-permute-start.16 = (bf16[2,2,64,256]{3,2,1,0:T(8,128)(2,1)S(1)}, bf16[2,2,64,256]{3,2,1,0:T(8,128)(2,1)S(1)}, u32[]{:S(2)}, u32[]{:S(2)}) collective-permute-start(bf16[2,2,64,256]{3,2,1,0:T(8,128)(2,1)S(1)} %get-tuple-element.50), channel_id=1, source_target_pairs={{0,8},{2,10},{4,12},{6,14},{8,0},{10,2},{12,4},{14,6},{1,9},{3,11}... | collective-permute-start | bytes 393224 | tf_op jit(solution)/shard_map/ppermute | solution.py:316
  56.7 10.8 %collective-permute-start.17 = (bf16[2,2,64,256]{3,2,1,0:T(8,128)(2,1)S(1)}, bf16[2,2,64,256]{3,2,1,0:T(8,128)(2,1)S(1)}, u32[]{:S(2)}, u32[]{:S(2)}) collective-permute-start(bf16[2,2,64,256]{3,2,1,0:T(8,128)(2,1)S(1)} %get-tuple-element.51), channel_id=1, source_target_pairs={{0,12},{2,14},{4,8},{6,10},{8,4},{10,6},{12,0},{14,2},{1,13},{3,15... | collective-permute-start | bytes 393224 | tf_op jit(solution)/shard_map/ppermute | solution.py:316
  60.0 8.9 %collective-permute-start.21 = (bf16[2,48,256]{2,1,0:T(8,128)(2,1)S(1)}, bf16[2,48,256]{2,1,0:T(8,128)(2,1)S(1)}, u32[]{:S(2)}, u32[]{:S(2)}) collective-permute-start(bf16[2,48,256]{2,1,0:T(8,128)(2,1)S(1)} %get-tuple-element.52), channel_id=1, source_target_pairs={{0,4},{2,6},{4,0},{6,2},{8,12},{10,14},{12,8},{14,10},{1,5},{3,7},... | collective-permute-start | bytes 147464 | tf_op jit(solution)/shard_map/ppermute | solution.py:316
  60.3 8.7 %collective-permute-start.23 = (bf16[2,48,256]{2,1,0:T(8,128)(2,1)S(1)}, bf16[2,48,256]{2,1,0:T(8,128)(2,1)S(1)}, u32[]{:S(2)}, u32[]{:S(2)}) collective-permute-start(bf16[2,48,256]{2,1,0:T(8,128)(2,1)S(1)} %get-tuple-element.53), channel_id=1, source_target_pairs={{0,12},{2,14},{4,8},{6,10},{8,4},{10,6},{12,0},{14,2},{1,13},{3,15... | collective-permute-start | bytes 147464 | tf_op jit(solution)/shard_map/ppermute | solution.py:316
  63.0 6.9 %collective-permute-start.22 = (bf16[2,48,256]{2,1,0:T(8,128)(2,1)S(1)}, bf16[2,48,256]{2,1,0:T(8,128)(2,1)S(1)}, u32[]{:S(2)}, u32[]{:S(2)}) collective-permute-start(bf16[2,48,256]{2,1,0:T(8,128)(2,1)S(1)} %get-tuple-element.54), channel_id=1, source_target_pairs={{0,8},{2,10},{4,12},{6,14},{8,0},{10,2},{12,4},{14,6},{1,9},{3,11}... | collective-permute-start | bytes 147464 | tf_op jit(solution)/shard_map/ppermute | solution.py:316

commit v3 on v2

--- a/solution.py
+++ b/solution.py
@@ -40,24 +40,30 @@
     return pl.CostEstimate(flops=flops, bytes_accessed=moved, transcendentals=exps)
 
 
+def head_columns():
+    return pl.ds(pl.multiple_of(pl.program_id(0) * HEAD_DIM, HEAD_DIM), HEAD_DIM)
+
+
 def place_prefix(refs, k_s, v_s):
+    columns = head_columns()
     rows = refs[0].shape[-2]
     at = 0
     for ref in refs:
         for dz in range(ref.shape[0]):
-            k_s[at : at + rows, :] = ref[dz, 0]
+            k_s[at : at + rows, :] = ref[dz, 0, :, columns]
             if v_s is not None:
-                v_s[at : at + rows, 0:HEAD_DIM] = ref[dz, 1]
+                v_s[at : at + rows, 0:HEAD_DIM] = ref[dz, 1, :, columns]
             at += rows
 
 
 def place_answer(refs, k_s, v_s):
+    columns = head_columns()
     rows = refs[0].shape[-2]
     for t, ref in enumerate(refs):
         for b in range(ref.shape[1]):
-            k_s[b, t * rows : (t + 1) * rows, :] = ref[0, b]
+            k_s[b, t * rows : (t + 1) * rows, :] = ref[0, b, :, columns]
             if v_s is not None:
-                v_s[b, t * rows : (t + 1) * rows, 0:HEAD_DIM] = ref[1, b]
+                v_s[b, t * rows : (t + 1) * rows, 0:HEAD_DIM] = ref[1, b, :, columns]
 
 
 def lanes(ref, here, update):
@@ -184,6 +190,7 @@
     total = q_ref.shape[1]
     per = total // batch
     groups = per // rows
+    columns = head_columns()
     piece_rows = answer[0].shape[-2]
     place_answer(answer, ka_s, va_s)
     va_s[:, :, HEAD_DIM:] = jnp.ones((batch, keys, HEAD_DIM), bf16)
@@ -244,8 +251,8 @@
         for t in range(pieces):
             part = slice(t * piece_rows, (t + 1) * piece_rows)
             ref = grads[4 * t // pieces]
-            ref[t % (pieces // 4), 0, b] = key_term[part]
-            ref[t % (pieces // 4), 1, b] = value_term[part]
+            ref[t % (pieces // 4), 0, b, :, columns] = key_term[part]
+            ref[t % (pieces // 4), 1, b, :, columns] = value_term[part]
 
 
 def prefix_backward_body(q_ref, p_ref, doa_ref, deltaa_ref, *rest):
@@ -258,14 +265,15 @@
     for span in blocks(total, size, k_s.shape[0]):
         dp = mm_nt(doa_ref[0, span, :], v_s[...])
         score_grads(ds_ref.at[0, span], p_ref[0, span, :], dp, deltaa_ref[0, span, :])
+    columns = head_columns()
     half = own_ref.shape[1]
     quarter = half // 2
     value_term = jnp.transpose(mm_tn(doa_ref[0], p_ref[0])).astype(bf16)
     key_term = (jnp.transpose(mm_tn(q_ref[0], ds_ref[0])) * scale).astype(bf16)
     for t, term in ((0, key_term), (1, value_term)):
-        own_ref[t] = term[:half]
-        near_ref[t] = term[half : half + quarter]
-        far_ref[t] = term[half + quarter :]
+        own_ref[t, :, columns] = term[:half]
+        near_ref[t, :, columns] = term[half : half + quarter]
+        far_ref[t, :, columns] = term[half + quarter :]
 
 
 def query_backward_body(pieces, out_ref, dsa_ref, dsb_ref, *rest):
@@ -357,15 +365,11 @@
         block = tuple(1 if a == axis else n for a, n in enumerate(shape))
         return pl.BlockSpec(block, lambda c: tuple(c if a == axis else 0 for a in range(len(shape))))
 
-    def lane_block(shape):
-        last = len(shape) - 1
-        return pl.BlockSpec(shape[:-1] + (HEAD_DIM,), lambda c: (0,) * last + (c,))
-
     raw_spec = pl.BlockSpec((1, rows, batch, group * HEAD_DIM), lambda c: (0, 0, 0, c))
     q_shape = (kv, total, HEAD_DIM)
     q_spec = by_head(q_shape)
-    prefix_specs = [lane_block(prefix_z.shape)] * 4
-    answer_spec = lane_block(answer_own.shape)
+    prefix_specs = [whole(prefix_z.shape)] * 4
+    answer_spec = whole(answer_own.shape)
     pa_shape = (kv, total, prefix_total)
     pb_shape = (kv, total, answer_total)
     ol_shape = (kv, total, 2 * HEAD_DIM)
@@ -418,7 +422,7 @@
             q_spec,
         ]
         + [answer_spec] * pieces,
-        out_specs=[q_spec, q_spec, q_spec, by_head(pb_shape)] + [lane_block(stack_shape)] * 4,
+        out_specs=[q_spec, q_spec, q_spec, by_head(pb_shape)] + [whole(stack_shape)] * 4,
         out_shape=[
             jax.ShapeDtypeStruct(q_shape, bf16),
             jax.ShapeDtypeStruct(q_shape, bf16),
@@ -447,9 +451,9 @@
         in_specs=[q_spec, by_head(pa_shape), q_spec, q_spec] + prefix_specs,
         out_specs=[
             by_head(pa_shape),
-            lane_block(own_shape),
-            lane_block(sent_shape),
-            lane_block(sent_shape),
+            whole(own_shape),
+            whole(sent_shape),
+            whole(sent_shape),
         ],
         out_shape=[
             jax.ShapeDtypeStruct(pa_shape, bf16),

time: 71 us -> 70.2 us (0.989)
  Pallas kernels: 13.9 us -> 12.6 us
  transfers between devices with their start and end apart: 24 -> 24, of which waited for: 7 -> 7; matrix products, arithmetic and copies ran while one was open for 7% -> 7% of each run, Pallas kernels for 10% -> 9%
where the time goes in v3:
time: 70.2 us; the launch traced here: 69.8 us
  starting transfers between devices  31.6 us (45%)
  waiting for transfers between devices  16.5 us (24%)
  Pallas kernels  12.6 us (18%)
  local copies, waits for them, and re-layouts  5.26 us (7%)
  other arithmetic  2.98 us (4%)
  between operations  0.84 us (1%)
    ppermute x12, starting transfers between devices, swap_z(): return lax.ppermute(x, 'seq', [(i, i ^ 2 * k) for i in range(size)])  18.1 us
    ppermute x12, waiting for transfers between devices, swap_z(): return lax.ppermute(x, 'seq', [(i, i ^ 2 * k) for i in range(size)])  9.89 us
    ppermute x8, starting transfers between devices, swap_y(): return lax.ppermute(x, 'seq', [(i, i ^ 1) for i in range(size)])  8.36 us
    ppermute x8, waiting for transfers between devices, swap_y(): return lax.ppermute(x, 'seq', [(i, i ^ 1) for i in range(size)])  6.07 us
    ppermute x4, starting transfers between devices, swap_x(): return lax.ppermute(x, 'pair', [(0, 1), (1, 0)])  5.14 us
    pallas_call x1, Pallas kernels, on_device(): pl.pallas_call(lambda *refs: middle_body(pieces, *refs), grid=(kv,), in_s...  4.16 us
    unnamed x6, local copies, waits for them, and re-layouts  3.43 us
    pallas_call x1, Pallas kernels, on_device(): pl.pallas_call(lambda *refs: query_backward_body(pieces, *refs), grid=(kv...  2.91 us
  transfers between devices with their start and end apart: 24, of which 7 were waited for; matrix products, arithmetic and copies ran while one was open for 7% of the time, Pallas kernels for 9%

profile of v3, /device:TPU:0, one launch (start us, length us, event | category | flops | bytes accessed | tf_op | source)
XLA Modules:
  0.0 69.8 jit_solution(837730865831001924)
XLA Ops:
  0.6 0.8 %fusion.11 = (bf16[1,2,48,256]{3,2,1,0:T(8,128)(2,1)S(1)}, bf16[2,48,256]{2,1,0:T(8,128)(2,1)S(1)}) fusion(bf16[1,48,256]{2,1,0:T(8,128)(2,1)} %bitcast.73, bf16[1,48,256]{2,1,0:T(8,128)(2,1)} %bitcast.74), kind=kLoop, calls=%fused_computation.48 | loop fusion | flops 24576 | bytes 147456 | tf_op jit(solution)/shard_map/stack | solution.py:334
  1.4 4.1 %collective-permute-start.1 = (bf16[2,48,256]{2,1,0:T(8,128)(2,1)S(1)}, bf16[2,48,256]{2,1,0:T(8,128)(2,1)S(1)}, u32[]{:S(2)}, u32[]{:S(2)}) collective-permute-start(bf16[2,48,256]{2,1,0:T(8,128)(2,1)S(1)} %get-tuple-element.60), channel_id=1, source_target_pairs={{0,8},{2,10},{4,12},{6,14},{8,0},{10,2},{12,4},{14,6},{1,9},{3,11}... | collective-permute-start | bytes 147464 | tf_op jit(solution)/shard_map/ppermute | solution.py:324
  5.5 1.6 %collective-permute-start = (bf16[2,48,256]{2,1,0:T(8,128)(2,1)S(1)}, bf16[2,48,256]{2,1,0:T(8,128)(2,1)S(1)}, u32[]{:S(2)}, u32[]{:S(2)}) collective-permute-start(bf16[2,48,256]{2,1,0:T(8,128)(2,1)S(1)} %get-tuple-element.60), channel_id=1, source_target_pairs={{0,4},{2,6},{4,0},{6,2},{8,12},{10,14},{12,8},{14,10},{1,5},{3,7},... | collective-permute-start | bytes 147464 | tf_op jit(solution)/shard_map/ppermute | solution.py:324
  7.1 0.9 %copy_bitcast_fusion = (bf16[1,2,64,256]{3,2,1,0:T(8,128)(2,1)S(1)}, bf16[1,2,64,256]{3,2,1,0:T(8,128)(2,1)S(1)}) fusion(bf16[1,64,2,256]{3,2,1,0:T(2,128)(2,1)} %param.10, bf16[1,64,2,256]{3,2,1,0:T(2,128)(2,1)} %param.9), kind=kLoop, calls=%fused_computation.22 | loop fusion | bytes 262144 | tf_op jit(solution)/shard_map/stack | solution.py:333
  8.0 3.9 %collective-permute-start.8 = (bf16[2,2,64,256]{3,2,1,0:T(8,128)(2,1)S(1)}, bf16[2,2,64,256]{3,2,1,0:T(8,128)(2,1)S(1)}, u32[]{:S(2)}, u32[]{:S(2)}) collective-permute-start(bf16[2,2,64,256]{3,2,1,0:T(8,128)(2,1)S(1)} %pad_maximum_fusion.1.refs_6_.refs_7_), channel_id=1, source_target_pairs={{0,12},{2,14},{4,8},{6,10},{8,4},{10,6},{12,0},{14,2},{1,13},{3,15... | collective-permute-start | bytes 393224 | tf_op jit(solution)/shard_map/ppermute | solution.py:324
  12.0 0.1 broadcast_add_fusion
  12.0 0.1 iota_add_fusion.1
  12.1 0.1 add.180
  12.3 0.1 compare_select_fusion.refs_1_
  12.4 0.1 add.190
  12.5 0.7 collective-permute-start.6
  13.2 0.3 collective-permute-done.2
  13.5 1.6 %collective-permute-start.4 = (bf16[4,2,48,256]{3,2,1,0:T(8,128)(2,1)S(1)}, bf16[4,2,48,256]{3,2,1,0:T(8,128)(2,1)S(1)}, u32[]{:S(2)}, u32[]{:S(2)}) collective-permute-start(bf16[4,2,48,256]{3,2,1,0:T(8,128)(2,1)S(1)} %pad_maximum_fusion.pa_ref.rest_0_.refs_3_), channel_id=1, source_target_pairs={{0,16},{16,0},{1,17},{17,1},{2,18},{18,2},{3,19},{19,3},{4,20},{20... | collective-permute-start | bytes 589832 | tf_op jit(solution)/shard_map/ppermute | solution.py:330
  15.1 1.5 %collective-permute-start.3 = (bf16[4,2,48,256]{3,2,1,0:T(8,128)(2,1)S(1)}, bf16[4,2,48,256]{3,2,1,0:T(8,128)(2,1)S(1)}, u32[]{:S(2)}, u32[]{:S(2)}) collective-permute-start(bf16[4,2,48,256]{3,2,1,0:T(8,128)(2,1)S(1)} %pad_maximum_fusion.pa_ref.rest_0_.refs_3_), channel_id=1, source_target_pairs={{0,2},{2,0},{4,6},{6,4},{8,10},{10,8},{12,14},{14,12},{1,3},{3,1},... | collective-permute-start | bytes 589832 | tf_op jit(solution)/shard_map/ppermute | solution.py:327
  16.6 0.7 %compare_select_fusion.1 = f32[2,768]{1,0:T(2,128)S(1)} fusion(s32[768]{0:T(1024)S(1)} %add.190, s32[2]{0:T(128)} %bitcast.76), kind=kLoop, calls=%fused_computation.30 | loop fusion | flops 3072 | bytes 9224 | tf_op jit(solution)/shard_map/jit(_where)/select_n | solution.py:351
  17.4 0.6 collective-permute-start.9
  18.0 4.8 %collective-permute-done.7.refs_8_.refs_9_ = bf16[2,2,64,256]{3,2,1,0:T(8,128)(2,1)S(1)} collective-permute-done((bf16[2,2,64,256]{3,2,1,0:T(8,128)(2,1)S(1)}, bf16[2,2,64,256]{3,2,1,0:T(8,128)(2,1)S(1)}, u32[]{:S(2)}, u32[]{:S(2)}) %collective-permute-start.7) | collective-permute-done | bytes 131104 | tf_op jit(solution)/shard_map/ppermute | solution.py:324
  22.8 1.5 %collective-permute-start.12 = (bf16[2,2,64,256]{3,2,1,0:T(8,128)(2,1)S(1)}, bf16[2,2,64,256]{3,2,1,0:T(8,128)(2,1)S(1)}, u32[]{:S(2)}, u32[]{:S(2)}) collective-permute-start(bf16[2,2,64,256]{3,2,1,0:T(8,128)(2,1)S(1)} %collective-permute-done.8.refs_9_.refs_10_), channel_id=1, source_target_pairs={{0,2},{2,0},{4,6},{6,4},{8,10},{10,8},{12,14},{14,12},{1,3},{3,1},... | collective-permute-start | bytes 393224 | tf_op jit(solution)/shard_map/ppermute | solution.py:327
  24.4 0.5 collective-permute-start.11
  24.9 1.5 %collective-permute-start.10 = (bf16[2,2,64,256]{3,2,1,0:T(8,128)(2,1)S(1)}, bf16[2,2,64,256]{3,2,1,0:T(8,128)(2,1)S(1)}, u32[]{:S(2)}, u32[]{:S(2)}) collective-permute-start(bf16[2,2,64,256]{3,2,1,0:T(8,128)(2,1)S(1)} %collective-permute-done.6.refs_7_.refs_8_), channel_id=1, source_target_pairs={{0,2},{2,0},{4,6},{6,4},{8,10},{10,8},{12,14},{14,12},{1,3},{3,1},... | collective-permute-start | bytes 393224 | tf_op jit(solution)/shard_map/ppermute | solution.py:327
  26.4 1.5 %collective-permute-start.5 = (bf16[4,2,48,256]{3,2,1,0:T(8,128)(2,1)S(1)}, bf16[4,2,48,256]{3,2,1,0:T(8,128)(2,1)S(1)}, u32[]{:S(2)}, u32[]{:S(2)}) collective-permute-start(bf16[4,2,48,256]{3,2,1,0:T(8,128)(2,1)S(1)} %collective-permute-done.3.pb_ref.rest_1_.refs_4_), channel_id=1, source_target_pairs={{0,16},{16,0},{1,17},{17,1},{2,18},{18,2},{3,19},{19,3},{4,20},{20... | collective-permute-start | bytes 589832 | tf_op jit(solution)/shard_map/ppermute | solution.py:330
  27.9 0.7 %compare_select_fusion.6 = f32[2,64]{1,0:T(2,128)S(1)} fusion(s32[64]{0:T(128)S(1)} %iota_add_fusion.2, s32[2]{0:T(128)} %bitcast.75), kind=kLoop, calls=%fused_computation.40 | loop fusion | flops 256 | bytes 776 | tf_op jit(solution)/shard_map/jit(_where)/select_n | solution.py:358
  28.6 1.0 %copy-done = bf16[1,64,2,1792]{3,2,1,0:T(2,128)(2,1)S(1)} copy-done((bf16[1,64,2,1792]{3,2,1,0:T(2,128)(2,1)S(1)}, bf16[1,64,2,1792]{3,2,1,0:T(2,128)(2,1)}, u32[]{:S(2)}) %copy-start) | copy-done | bytes 458776
  29.6 1.0 %copy-done.1 = bf16[1,64,2,1792]{3,2,1,0:T(2,128)(2,1)S(1)} copy-done((bf16[1,64,2,1792]{3,2,1,0:T(2,128)(2,1)S(1)}, bf16[1,64,2,1792]{3,2,1,0:T(2,128)(2,1)}, u32[]{:S(2)}) %copy-start.1) | copy-done | bytes 458776
  30.7 0.9 %arrange.1 = (bf16[2,896,128]{2,1,0:T(8,128)(2,1)S(1)}, bf16[2,896,128]{2,1,0:T(8,128)(2,1)S(1)}) custom-call(bf16[1,64,2,1792]{3,2,1,0:T(2,128)(2,1)S(1)} %copy-done, bf16[1,64,2,1792]{3,2,1,0:T(2,128)(2,1)S(1)} %copy-done.1), custom_call_target="tpu_custom_call" | custom-call | flops 117440512 | bytes 4194304 | tf_op jit(solution)/shard_map/arrange/pallas_call | solution.py:382
  31.5 0.6 collective-permute-done.5.pd_ref.rest_3_.refs_6_
  32.1 2.5 %prefix_forward.1 = (bf16[2,896,768]{2,1,0:T(8,128)(2,1)S(1)}, f32[2,896,256]{2,1,0:T(8,128)S(1)}, f32[2,896,128]{2,1,0:T(8,128)S(1)}) custom-call(f32[2,8,768]{2,1,0:T(8,128)S(1)} %broadcast_in_dim.52.bias_ref, bf16[2,896,128]{2,1,0:T(8,128)(2,1)S(1)} %get-tuple-element.25.q_ref.refs_2_, bf16[4,2,48,256]{3,2,1,0:T(8,128)(2,1)S(1)} %pad_maximum_fusion.pa_ref.rest_0_.refs_3_, ...), custom_call_target="tpu_custom_call" | custom-call | flops 704643072 | bytes 8388608 | tf_op jit(solution)/shard_map/prefix_forward/pallas_call | solution.py:393
  34.6 0.1 broadcast_in_dim.47.refs_0_
  34.7 4.2 %middle.1 = (bf16[2,896,128]{2,1,0:T(8,128)(2,1)S(1)}, bf16[2,896,128]{2,1,0:T(8,128)(2,1)S(1)}, f32[2,896,128]{2,1,0:T(8,128)S(1)}, bf16[2,896,512]{2,1,0:T(8,1...) custom-call(f32[2,64,128]{2,1,0:T(8,128)S(1)} %broadcast_in_dim.47.r, ...), custom_call_target="tpu_custom_call" | custom-call | flops 1174405120 | bytes 12582912 | tf_op jit(solution)/shard_map/middle/pallas_call | solution.py:413
  38.8 2.2 %prefix_backward.1 = (bf16[2,896,768]{2,1,0:T(8,128)(2,1)S(1)}, bf16[2,384,256]{2,1,0:T(8,128)(2,1)S(1)}, bf16[2,192,256]{2,1,0:T(8,128)(2,1)S(1)}, bf16[2,192,256]{2,1,0:T(8,128)(2,1)S(1)}) custom-call(bf16[2,896,128]{2,1,0:T(8,128)(2,1)S(1)} %get-tuple-element.25.q_ref.refs_2_, bf16[2,896,768]{2,1,0:T(8,128)(2,1)S(1)} %get-tuple-element.30.p_ref, ...), custom_call_target="tpu_custom_call" | custom-call | flops 1056964608 | bytes 12582912 | tf_op jit(solution)/shard_map/prefix_backward/pallas_call | solution.py:448
  41.1 1.6 %collective-permute-start.19 = (bf16[2,192,256]{2,1,0:T(8,128)(2,1)S(1)}, bf16[2,192,256]{2,1,0:T(8,128)(2,1)S(1)}, u32[]{:S(2)}, u32[]{:S(2)}) collective-permute-start(bf16[2,192,256]{2,1,0:T(8,128)(2,1)S(1)} %get-tuple-element.43), channel_id=1, source_target_pairs={{0,16},{16,0},{1,17},{17,1},{2,18},{18,2},{3,19},{19,3},{4,20},{20... | collective-permute-start | bytes 589832 | tf_op jit(solution)/shard_map/ppermute | solution.py:330
  42.7 0.5 collective-permute-start.13
  43.1 1.5 %collective-permute-start.15 = (bf16[2,2,2,64,256]{4,3,2,1,0:T(8,128)(2,1)S(1)}, bf16[2,2,2,64,256]{4,3,2,1,0:T(8,128)(2,1)S(1)}, u32[]{:S(2)}, u32[]{:S(2)}) collective-permute-start(bf16[2,2,2,64,256]{4,3,2,1,0:T(8,128)(2,1)S(1)} %get-tuple-element.40), channel_id=1, source_target_pairs={{0,2},{2,0},{4,6},{6,4},{8,10},{10,8},{12,14},{14,12},{1,3},{3,1},... | collective-permute-start | bytes 786440 | tf_op jit(solution)/shard_map/ppermute | solution.py:327
  44.7 0.5 collective-permute-start.18
  45.2 2.9 %query_backward.1 = (bf16[1,64,2,1792]{3,2,1,0:T(2,128)(2,1)}, bf16[1,64,2,1792]{3,2,1,0:T(2,128)(2,1)}) custom-call(bf16[2,896,128]{2,1,0:T(8,128)(2,1)S(1)} %get-tuple-element.29.refs_0_, bf16[2,896,768]{2,1,0:T(8,128)(2,1)S(1)} %get-tuple-element.33.refs_1_, bf16[2,896,512]{2,1,0:T(8,128)(2,1)S(1)} %get-tuple-element.34.refs_2_, ...), custom_call_target="tpu_custom_call" | custom-call | flops 587202560 | bytes 8388608 | tf_op jit(solution)/shard_map/query_backward/pallas_call | solution.py:473
  48.2 0.6 collective-permute-start.20
  48.8 3.0 %collective-permute-done.13 = bf16[2,2,2,64,256]{4,3,2,1,0:T(8,128)(2,1)S(1)} collective-permute-done((bf16[2,2,2,64,256]{4,3,2,1,0:T(8,128)(2,1)S(1)}, bf16[2,2,2,64,256]{4,3,2,1,0:T(8,128)(2,1)S(1)}, u32[]{:S(2)}, u32[]{:S(2)}) %collective-permute-start.13) | collective-permute-done | bytes 262176 | tf_op jit(solution)/shard_map/ppermute | solution.py:327
  51.9 0.7 %collective-permute-start.14 = (bf16[2,2,64,256]{3,2,1,0:T(8,128)(2,1)S(1)}, bf16[2,2,64,256]{3,2,1,0:T(8,128)(2,1)S(1)}, u32[]{:S(2)}, u32[]{:S(2)}) collective-permute-start(bf16[2,2,64,256]{3,2,1,0:T(8,128)(2,1)S(1)} %fusion.4), channel_id=1, source_target_pairs={{0,4},{2,6},{4,0},{6,2},{8,12},{10,14},{12,8},{14,10},{1,5},{3,7},... | collective-permute-start | bytes 393224 | tf_op jit(solution)/shard_map/ppermute | solution.py:324
  52.6 3.0 %collective-permute-done.15 = bf16[2,2,2,64,256]{4,3,2,1,0:T(8,128)(2,1)S(1)} collective-permute-done((bf16[2,2,2,64,256]{4,3,2,1,0:T(8,128)(2,1)S(1)}, bf16[2,2,2,64,256]{4,3,2,1,0:T(8,128)(2,1)S(1)}, u32[]{:S(2)}, u32[]{:S(2)}) %collective-permute-start.15) | collective-permute-done | bytes 262176 | tf_op jit(solution)/shard_map/ppermute | solution.py:327
  55.8 3.4 %collective-permute-start.17 = (bf16[2,2,64,256]{3,2,1,0:T(8,128)(2,1)S(1)}, bf16[2,2,64,256]{3,2,1,0:T(8,128)(2,1)S(1)}, u32[]{:S(2)}, u32[]{:S(2)}) collective-permute-start(bf16[2,2,64,256]{3,2,1,0:T(8,128)(2,1)S(1)} %get-tuple-element.51), channel_id=1, source_target_pairs={{0,12},{2,14},{4,8},{6,10},{8,4},{10,6},{12,0},{14,2},{1,13},{3,15... | collective-permute-start | bytes 393224 | tf_op jit(solution)/shard_map/ppermute | solution.py:324
  59.4 0.1 collective-permute-start.21
  59.5 2.7 %collective-permute-start.23 = (bf16[2,48,256]{2,1,0:T(8,128)(2,1)S(1)}, bf16[2,48,256]{2,1,0:T(8,128)(2,1)S(1)}, u32[]{:S(2)}, u32[]{:S(2)}) collective-permute-start(bf16[2,48,256]{2,1,0:T(8,128)(2,1)S(1)} %get-tuple-element.53), channel_id=1, source_target_pairs={{0,12},{2,14},{4,8},{6,10},{8,4},{10,6},{12,0},{14,2},{1,13},{3,15... | collective-permute-start | bytes 147464 | tf_op jit(solution)/shard_map/ppermute | solution.py:324
  62.2 0.8 %collective-permute-start.22 = (bf16[2,48,256]{2,1,0:T(8,128)(2,1)S(1)}, bf16[2,48,256]{2,1,0:T(8,128)(2,1)S(1)}, u32[]{:S(2)}, u32[]{:S(2)}) collective-permute-start(bf16[2,48,256]{2,1,0:T(8,128)(2,1)S(1)} %get-tuple-element.54), channel_id=1, source_target_pairs={{0,8},{2,10},{4,12},{6,14},{8,0},{10,2},{12,4},{14,6},{1,9},{3,11}... | collective-permute-start | bytes 147464 | tf_op jit(solution)/shard_map/ppermute | solution.py:324
  62.9 3.7 %collective-permute-done.16 = bf16[2,2,64,256]{3,2,1,0:T(8,128)(2,1)S(1)} collective-permute-done((bf16[2,2,64,256]{3,2,1,0:T(8,128)(2,1)S(1)}, bf16[2,2,64,256]{3,2,1,0:T(8,128)(2,1)S(1)}, u32[]{:S(2)}, u32[]{:S(2)}) %collective-permute-start.16) | collective-permute-done | bytes 131104 | tf_op jit(solution)/shard_map/ppermute | solution.py:324
  66.8 0.7 copy.19
  67.5 0.7 copy.18
  68.2 1.0 %collective-permute-done.22 = bf16[2,48,256]{2,1,0:T(8,128)(2,1)S(1)} collective-permute-done((bf16[2,48,256]{2,1,0:T(8,128)(2,1)S(1)}, bf16[2,48,256]{2,1,0:T(8,128)(2,1)S(1)}, u32[]{:S(2)}, u32[]{:S(2)}) %collective-permute-start.22) | collective-permute-done | bytes 49184 | tf_op jit(solution)/shard_map/ppermute | solution.py:324
  69.2 0.6 slice_bitcast_fusion.6
  (41 shorter events, 0.7 us)
Async XLA Ops:
  1.4 11.1 %collective-permute-start.1 = (bf16[2,48,256]{2,1,0:T(8,128)(2,1)S(1)}, bf16[2,48,256]{2,1,0:T(8,128)(2,1)S(1)}, u32[]{:S(2)}, u32[]{:S(2)}) collective-permute-start(bf16[2,48,256]{2,1,0:T(8,128)(2,1)S(1)} %get-tuple-element.60), channel_id=1, source_target_pairs={{0,8},{2,10},{4,12},{6,14},{8,0},{10,2},{12,4},{14,6},{1,9},{3,11}... | collective-permute-start | bytes 147464 | tf_op jit(solution)/shard_map/ppermute | solution.py:324
  5.5 7.7 %collective-permute-start = (bf16[2,48,256]{2,1,0:T(8,128)(2,1)S(1)}, bf16[2,48,256]{2,1,0:T(8,128)(2,1)S(1)}, u32[]{:S(2)}, u32[]{:S(2)}) collective-permute-start(bf16[2,48,256]{2,1,0:T(8,128)(2,1)S(1)} %get-tuple-element.60), channel_id=1, source_target_pairs={{0,4},{2,6},{4,0},{6,2},{8,12},{10,14},{12,8},{14,10},{1,5},{3,7},... | collective-permute-start | bytes 147464 | tf_op jit(solution)/shard_map/ppermute | solution.py:324
  7.1 6.4 %collective-permute-start.2 = (bf16[2,48,256]{2,1,0:T(8,128)(2,1)S(1)}, bf16[2,48,256]{2,1,0:T(8,128)(2,1)S(1)}, u32[]{:S(2)}, u32[]{:S(2)}) collective-permute-start(bf16[2,48,256]{2,1,0:T(8,128)(2,1)S(1)} %get-tuple-element.60), channel_id=1, source_target_pairs={{0,12},{2,14},{4,8},{6,10},{8,4},{10,6},{12,0},{14,2},{1,13},{3,15... | collective-permute-start | bytes 147464 | tf_op jit(solution)/shard_map/ppermute | solution.py:324
  8.0 9.3 %collective-permute-start.8 = (bf16[2,2,64,256]{3,2,1,0:T(8,128)(2,1)S(1)}, bf16[2,2,64,256]{3,2,1,0:T(8,128)(2,1)S(1)}, u32[]{:S(2)}, u32[]{:S(2)}) collective-permute-start(bf16[2,2,64,256]{3,2,1,0:T(8,128)(2,1)S(1)} %pad_maximum_fusion.1.refs_6_.refs_7_), channel_id=1, source_target_pairs={{0,12},{2,14},{4,8},{6,10},{8,4},{10,6},{12,0},{14,2},{1,13},{3,15... | collective-permute-start | bytes 393224 | tf_op jit(solution)/shard_map/ppermute | solution.py:324
  11.9 10.9 %collective-permute-start.7 = (bf16[2,2,64,256]{3,2,1,0:T(8,128)(2,1)S(1)}, bf16[2,2,64,256]{3,2,1,0:T(8,128)(2,1)S(1)}, u32[]{:S(2)}, u32[]{:S(2)}) collective-permute-start(bf16[2,2,64,256]{3,2,1,0:T(8,128)(2,1)S(1)} %pad_maximum_fusion.1.refs_6_.refs_7_), channel_id=1, source_target_pairs={{0,8},{2,10},{4,12},{6,14},{8,0},{10,2},{12,4},{14,6},{1,9},{3,11}... | collective-permute-start | bytes 393224 | tf_op jit(solution)/shard_map/ppermute | solution.py:324
  12.5 11.9 %collective-permute-start.6 = (bf16[2,2,64,256]{3,2,1,0:T(8,128)(2,1)S(1)}, bf16[2,2,64,256]{3,2,1,0:T(8,128)(2,1)S(1)}, u32[]{:S(2)}, u32[]{:S(2)}) collective-permute-start(bf16[2,2,64,256]{3,2,1,0:T(8,128)(2,1)S(1)} %pad_maximum_fusion.1.refs_6_.refs_7_), channel_id=1, source_target_pairs={{0,4},{2,6},{4,0},{6,2},{8,12},{10,14},{12,8},{14,10},{1,5},{3,7},... | collective-permute-start | bytes 393224 | tf_op jit(solution)/shard_map/ppermute | solution.py:324
  13.5 11.3 %collective-permute-start.4 = (bf16[4,2,48,256]{3,2,1,0:T(8,128)(2,1)S(1)}, bf16[4,2,48,256]{3,2,1,0:T(8,128)(2,1)S(1)}, u32[]{:S(2)}, u32[]{:S(2)}) collective-permute-start(bf16[4,2,48,256]{3,2,1,0:T(8,128)(2,1)S(1)} %pad_maximum_fusion.pa_ref.rest_0_.refs_3_), channel_id=1, source_target_pairs={{0,16},{16,0},{1,17},{17,1},{2,18},{18,2},{3,19},{19,3},{4,20},{20... | collective-permute-start | bytes 589832 | tf_op jit(solution)/shard_map/ppermute | solution.py:330
  15.1 11.3 %collective-permute-start.3 = (bf16[4,2,48,256]{3,2,1,0:T(8,128)(2,1)S(1)}, bf16[4,2,48,256]{3,2,1,0:T(8,128)(2,1)S(1)}, u32[]{:S(2)}, u32[]{:S(2)}) collective-permute-start(bf16[4,2,48,256]{3,2,1,0:T(8,128)(2,1)S(1)} %pad_maximum_fusion.pa_ref.rest_0_.refs_3_), channel_id=1, source_target_pairs={{0,2},{2,0},{4,6},{6,4},{8,10},{10,8},{12,14},{14,12},{1,3},{3,1},... | collective-permute-start | bytes 589832 | tf_op jit(solution)/shard_map/ppermute | solution.py:327
  17.4 17.2 %collective-permute-start.9 = (bf16[2,2,64,256]{3,2,1,0:T(8,128)(2,1)S(1)}, bf16[2,2,64,256]{3,2,1,0:T(8,128)(2,1)S(1)}, u32[]{:S(2)}, u32[]{:S(2)}) collective-permute-start(bf16[2,2,64,256]{3,2,1,0:T(8,128)(2,1)S(1)} %pad_maximum_fusion.1.refs_6_.refs_7_), channel_id=1, source_target_pairs={{0,2},{2,0},{4,6},{6,4},{8,10},{10,8},{12,14},{14,12},{1,3},{3,1},... | collective-permute-start | bytes 393224 | tf_op jit(solution)/shard_map/ppermute | solution.py:327
  22.8 11.7 %collective-permute-start.12 = (bf16[2,2,64,256]{3,2,1,0:T(8,128)(2,1)S(1)}, bf16[2,2,64,256]{3,2,1,0:T(8,128)(2,1)S(1)}, u32[]{:S(2)}, u32[]{:S(2)}) collective-permute-start(bf16[2,2,64,256]{3,2,1,0:T(8,128)(2,1)S(1)} %collective-permute-done.8.refs_9_.refs_10_), channel_id=1, source_target_pairs={{0,2},{2,0},{4,6},{6,4},{8,10},{10,8},{12,14},{14,12},{1,3},{3,1},... | collective-permute-start | bytes 393224 | tf_op jit(solution)/shard_map/ppermute | solution.py:327
  24.4 10.2 %collective-permute-start.11 = (bf16[2,2,64,256]{3,2,1,0:T(8,128)(2,1)S(1)}, bf16[2,2,64,256]{3,2,1,0:T(8,128)(2,1)S(1)}, u32[]{:S(2)}, u32[]{:S(2)}) collective-permute-start(bf16[2,2,64,256]{3,2,1,0:T(8,128)(2,1)S(1)} %collective-permute-done.7.refs_8_.refs_9_), channel_id=1, source_target_pairs={{0,2},{2,0},{4,6},{6,4},{8,10},{10,8},{12,14},{14,12},{1,3},{3,1},... | collective-permute-start | bytes 393224 | tf_op jit(solution)/shard_map/ppermute | solution.py:327
  24.9 9.7 %collective-permute-start.10 = (bf16[2,2,64,256]{3,2,1,0:T(8,128)(2,1)S(1)}, bf16[2,2,64,256]{3,2,1,0:T(8,128)(2,1)S(1)}, u32[]{:S(2)}, u32[]{:S(2)}) collective-permute-start(bf16[2,2,64,256]{3,2,1,0:T(8,128)(2,1)S(1)} %collective-permute-done.6.refs_7_.refs_8_), channel_id=1, source_target_pairs={{0,2},{2,0},{4,6},{6,4},{8,10},{10,8},{12,14},{14,12},{1,3},{3,1},... | collective-permute-start | bytes 393224 | tf_op jit(solution)/shard_map/ppermute | solution.py:327
  26.4 5.7 %collective-permute-start.5 = (bf16[4,2,48,256]{3,2,1,0:T(8,128)(2,1)S(1)}, bf16[4,2,48,256]{3,2,1,0:T(8,128)(2,1)S(1)}, u32[]{:S(2)}, u32[]{:S(2)}) collective-permute-start(bf16[4,2,48,256]{3,2,1,0:T(8,128)(2,1)S(1)} %collective-permute-done.3.pb_ref.rest_1_.refs_4_), channel_id=1, source_target_pairs={{0,16},{16,0},{1,17},{17,1},{2,18},{18,2},{3,19},{19,3},{4,20},{20... | collective-permute-start | bytes 589832 | tf_op jit(solution)/shard_map/ppermute | solution.py:330
  28.6 1.0 %copy-start = (bf16[1,64,2,1792]{3,2,1,0:T(2,128)(2,1)S(1)}, bf16[1,64,2,1792]{3,2,1,0:T(2,128)(2,1)}, u32[]{:S(2)}) copy-start(bf16[1,64,2,1792]{3,2,1,0:T(2,128)(2,1)} %raw_q_ref.1) | copy-start | bytes 1376260
  29.6 1.0 %copy-start.1 = (bf16[1,64,2,1792]{3,2,1,0:T(2,128)(2,1)S(1)}, bf16[1,64,2,1792]{3,2,1,0:T(2,128)(2,1)}, u32[]{:S(2)}) copy-start(bf16[1,64,2,1792]{3,2,1,0:T(2,128)(2,1)} %raw_do_ref.1) | copy-start | bytes 1376260
  41.1 7.0 %collective-permute-start.19 = (bf16[2,192,256]{2,1,0:T(8,128)(2,1)S(1)}, bf16[2,192,256]{2,1,0:T(8,128)(2,1)S(1)}, u32[]{:S(2)}, u32[]{:S(2)}) collective-permute-start(bf16[2,192,256]{2,1,0:T(8,128)(2,1)S(1)} %get-tuple-element.43), channel_id=1, source_target_pairs={{0,16},{16,0},{1,17},{17,1},{2,18},{18,2},{3,19},{19,3},{4,20},{20... | collective-permute-start | bytes 589832 | tf_op jit(solution)/shard_map/ppermute | solution.py:330
  42.7 9.2 %collective-permute-start.13 = (bf16[2,2,2,64,256]{4,3,2,1,0:T(8,128)(2,1)S(1)}, bf16[2,2,2,64,256]{4,3,2,1,0:T(8,128)(2,1)S(1)}, u32[]{:S(2)}, u32[]{:S(2)}) collective-permute-start(bf16[2,2,2,64,256]{4,3,2,1,0:T(8,128)(2,1)S(1)} %get-tuple-element.38), channel_id=1, source_target_pairs={{0,2},{2,0},{4,6},{6,4},{8,10},{10,8},{12,14},{14,12},{1,3},{3,1},... | collective-permute-start | bytes 786440 | tf_op jit(solution)/shard_map/ppermute | solution.py:327
  43.1 12.5 %collective-permute-start.15 = (bf16[2,2,2,64,256]{4,3,2,1,0:T(8,128)(2,1)S(1)}, bf16[2,2,2,64,256]{4,3,2,1,0:T(8,128)(2,1)S(1)}, u32[]{:S(2)}, u32[]{:S(2)}) collective-permute-start(bf16[2,2,2,64,256]{4,3,2,1,0:T(8,128)(2,1)S(1)} %get-tuple-element.40), channel_id=1, source_target_pairs={{0,2},{2,0},{4,6},{6,4},{8,10},{10,8},{12,14},{14,12},{1,3},{3,1},... | collective-permute-start | bytes 786440 | tf_op jit(solution)/shard_map/ppermute | solution.py:327
  44.7 14.6 %collective-permute-start.18 = (bf16[2,192,256]{2,1,0:T(8,128)(2,1)S(1)}, bf16[2,192,256]{2,1,0:T(8,128)(2,1)S(1)}, u32[]{:S(2)}, u32[]{:S(2)}) collective-permute-start(bf16[2,192,256]{2,1,0:T(8,128)(2,1)S(1)} %get-tuple-element.41), channel_id=1, source_target_pairs={{0,16},{16,0},{1,17},{17,1},{2,18},{18,2},{3,19},{19,3},{4,20},{20... | collective-permute-start | bytes 589832 | tf_op jit(solution)/shard_map/ppermute | solution.py:330
  48.2 11.1 %collective-permute-start.20 = (bf16[2,192,256]{2,1,0:T(8,128)(2,1)S(1)}, bf16[2,192,256]{2,1,0:T(8,128)(2,1)S(1)}, u32[]{:S(2)}, u32[]{:S(2)}) collective-permute-start(bf16[2,192,256]{2,1,0:T(8,128)(2,1)S(1)} %add_convert_fusion.1), channel_id=1, source_target_pairs={{0,2},{2,0},{4,6},{6,4},{8,10},{10,8},{12,14},{14,12},{1,3},{3,1},... | collective-permute-start | bytes 589832 | tf_op jit(solution)/shard_map/ppermute | solution.py:327
  51.9 10.3 %collective-permute-start.14 = (bf16[2,2,64,256]{3,2,1,0:T(8,128)(2,1)S(1)}, bf16[2,2,64,256]{3,2,1,0:T(8,128)(2,1)S(1)}, u32[]{:S(2)}, u32[]{:S(2)}) collective-permute-start(bf16[2,2,64,256]{3,2,1,0:T(8,128)(2,1)S(1)} %fusion.4), channel_id=1, source_target_pairs={{0,4},{2,6},{4,0},{6,2},{8,12},{10,14},{12,8},{14,10},{1,5},{3,7},... | collective-permute-start | bytes 393224 | tf_op jit(solution)/shard_map/ppermute | solution.py:324
  55.8 10.9 %collective-permute-start.16 = (bf16[2,2,64,256]{3,2,1,0:T(8,128)(2,1)S(1)}, bf16[2,2,64,256]{3,2,1,0:T(8,128)(2,1)S(1)}, u32[]{:S(2)}, u32[]{:S(2)}) collective-permute-start(bf16[2,2,64,256]{3,2,1,0:T(8,128)(2,1)S(1)} %get-tuple-element.50), channel_id=1, source_target_pairs={{0,8},{2,10},{4,12},{6,14},{8,0},{10,2},{12,4},{14,6},{1,9},{3,11}... | collective-permute-start | bytes 393224 | tf_op jit(solution)/shard_map/ppermute | solution.py:324
  55.8 10.8 %collective-permute-start.17 = (bf16[2,2,64,256]{3,2,1,0:T(8,128)(2,1)S(1)}, bf16[2,2,64,256]{3,2,1,0:T(8,128)(2,1)S(1)}, u32[]{:S(2)}, u32[]{:S(2)}) collective-permute-start(bf16[2,2,64,256]{3,2,1,0:T(8,128)(2,1)S(1)} %get-tuple-element.51), channel_id=1, source_target_pairs={{0,12},{2,14},{4,8},{6,10},{8,4},{10,6},{12,0},{14,2},{1,13},{3,15... | collective-permute-start | bytes 393224 | tf_op jit(solution)/shard_map/ppermute | solution.py:324
  59.4 8.8 %collective-permute-start.21 = (bf16[2,48,256]{2,1,0:T(8,128)(2,1)S(1)}, bf16[2,48,256]{2,1,0:T(8,128)(2,1)S(1)}, u32[]{:S(2)}, u32[]{:S(2)}) collective-permute-start(bf16[2,48,256]{2,1,0:T(8,128)(2,1)S(1)} %get-tuple-element.52), channel_id=1, source_target_pairs={{0,4},{2,6},{4,0},{6,2},{8,12},{10,14},{12,8},{14,10},{1,5},{3,7},... | collective-permute-start | bytes 147464 | tf_op jit(solution)/shard_map/ppermute | solution.py:324
  59.5 8.7 %collective-permute-start.23 = (bf16[2,48,256]{2,1,0:T(8,128)(2,1)S(1)}, bf16[2,48,256]{2,1,0:T(8,128)(2,1)S(1)}, u32[]{:S(2)}, u32[]{:S(2)}) collective-permute-start(bf16[2,48,256]{2,1,0:T(8,128)(2,1)S(1)} %get-tuple-element.53), channel_id=1, source_target_pairs={{0,12},{2,14},{4,8},{6,10},{8,4},{10,6},{12,0},{14,2},{1,13},{3,15... | collective-permute-start | bytes 147464 | tf_op jit(solution)/shard_map/ppermute | solution.py:324
  62.2 7.0 %collective-permute-start.22 = (bf16[2,48,256]{2,1,0:T(8,128)(2,1)S(1)}, bf16[2,48,256]{2,1,0:T(8,128)(2,1)S(1)}, u32[]{:S(2)}, u32[]{:S(2)}) collective-permute-start(bf16[2,48,256]{2,1,0:T(8,128)(2,1)S(1)} %get-tuple-element.54), channel_id=1, source_target_pairs={{0,8},{2,10},{4,12},{6,14},{8,0},{10,2},{12,4},{14,6},{1,9},{3,11}... | collective-permute-start | bytes 147464 | tf_op jit(solution)/shard_map/ppermute | solution.py:324

commit v4 on v3

--- a/solution.py
+++ b/solution.py
@@ -211,48 +211,52 @@
     for b in range(batch):
 
         def combine(i, carry, b=b):
-            here = pl.ds(pl.multiple_of(b * per + i * rows, rows), rows)
-            live = live_ref[b]
-            ma = m_ref[0, here, :]
-            mb = mb_s[here, :]
-            top = jnp.maximum(ma, mb)
-            ea = jnp.exp2(ma - top)
-            eb = jnp.exp2(mb - top)
-            inverse = 1.0 / (
-                ol_ref[0, here, HEAD_DIM:] * ea + olb_s[here, HEAD_DIM:] * eb
-            )
-            ea = ea * inverse
-            eb = eb * inverse
-            attended = (ol_ref[0, here, 0:HEAD_DIM] * ea + olb_s[here, 0:HEAD_DIM] * eb) * live
-            out_ref[0, here, :] = attended.astype(bf16)
-            douts = do_ref[0, here, :].astype(f32) * live
-            da = (douts * ea).astype(bf16)
-            db = (douts * eb).astype(bf16)
-            doa_ref[0, here, :] = da
-            dob_s[here, :] = db
-            deltaa_ref[0, here, :] = jnp.broadcast_to(
-                jnp.sum(da.astype(f32) * attended, axis=1, keepdims=True), (rows, HEAD_DIM)
-            )
-            deltab_s[here, :] = jnp.broadcast_to(
-                jnp.sum(db.astype(f32) * attended, axis=1, keepdims=True), (rows, HEAD_DIM)
-            )
+            for h in range(rows // CHUNK):
+                here = pl.ds(pl.multiple_of(b * per + i * rows + h * CHUNK, CHUNK), CHUNK)
+                live = live_ref[b, h * CHUNK : (h + 1) * CHUNK]
+                ma = m_ref[0, here, :]
+                mb = mb_s[here, :]
+                top = jnp.maximum(ma, mb)
+                ea = jnp.exp2(ma - top)
+                eb = jnp.exp2(mb - top)
+                inverse = 1.0 / (
+                    ol_ref[0, here, HEAD_DIM:] * ea + olb_s[here, HEAD_DIM:] * eb
+                )
+                ea = ea * inverse
+                eb = eb * inverse
+                attended = (ol_ref[0, here, 0:HEAD_DIM] * ea + olb_s[here, 0:HEAD_DIM] * eb) * live
+                out_ref[0, here, :] = attended.astype(bf16)
+                douts = do_ref[0, here, :].astype(f32) * live
+                da = (douts * ea).astype(bf16)
+                db = (douts * eb).astype(bf16)
+                doa_ref[0, here, :] = da
+                dob_s[here, :] = db
+                deltaa_ref[0, here, :] = jnp.broadcast_to(
+                    jnp.sum(da.astype(f32) * attended, axis=1, keepdims=True), (CHUNK, HEAD_DIM)
+                )
+                deltab_s[here, :] = jnp.broadcast_to(
+                    jnp.sum(db.astype(f32) * attended, axis=1, keepdims=True), (CHUNK, HEAD_DIM)
+                )
             return carry
 
         lax.fori_loop(0, groups, combine, 0, unroll=groups)
-    for b in range(batch):
+
+    def store(t, b, term):
+        for piece in range(pieces):
+            part = slice(piece * piece_rows, (piece + 1) * piece_rows)
+            grads[4 * piece // pieces][piece % (pieces // 4), t, b, :, columns] = term[part]
+
+    for b in range(batch):
+        span = slice(b * per, (b + 1) * per)
+        store(1, b, jnp.transpose(mm_tn(dob_s[span, :], p_s[0, span, :])).astype(bf16))
         for part in blocks(per, rows, keys):
-            span = slice(b * per + part.start, b * per + part.stop)
-            dp = mm_nt(dob_s[span, :], va_s[b, :, 0:HEAD_DIM])
-            score_grads(ds_ref.at[0, span], p_s[0, span, :], dp, deltab_s[span, :])
+            some = slice(b * per + part.start, b * per + part.stop)
+            dp = mm_nt(dob_s[some, :], va_s[b, :, 0:HEAD_DIM])
+            score_grads(ds_ref.at[0, some], p_s[0, some, :], dp, deltab_s[some, :])
     for b in range(batch):
         span = slice(b * per, (b + 1) * per)
-        value_term = jnp.transpose(mm_tn(dob_s[span, :], p_s[0, span, :])).astype(bf16)
-        key_term = (jnp.transpose(mm_tn(q_ref[0, span, :], ds_ref[0, span, :])) * scale).astype(bf16)
-        for t in range(pieces):
-            part = slice(t * piece_rows, (t + 1) * piece_rows)
-            ref = grads[4 * t // pieces]
-            ref[t % (pieces // 4), 0, b, :, columns] = key_term[part]
-            ref[t % (pieces // 4), 1, b, :, columns] = value_term[part]
+        term = jnp.transpose(mm_tn(q_ref[0, span, :], ds_ref[0, span, :])) * scale
+        store(0, b, term.astype(bf16))
 
 
 def prefix_backward_body(q_ref, p_ref, doa_ref, deltaa_ref, *rest):

time: 70.2 us -> 70 us (level)
  no operation moved by 1% of the time
where the time goes in v4:
time: 70 us; the launch traced here: 69.6 us
  starting transfers between devices  31.6 us (45%)
  waiting for transfers between devices  16.5 us (24%)
  Pallas kernels  12.4 us (18%)
  local copies, waits for them, and re-layouts  5.26 us (8%)
  other arithmetic  2.98 us (4%)
  between operations  0.85 us (1%)
    ppermute x12, starting transfers between devices, swap_z(): return lax.ppermute(x, 'seq', [(i, i ^ 2 * k) for i in range(size)])  18.1 us
    ppermute x12, waiting for transfers between devices, swap_z(): return lax.ppermute(x, 'seq', [(i, i ^ 2 * k) for i in range(size)])  9.89 us
    ppermute x8, starting transfers between devices, swap_y(): return lax.ppermute(x, 'seq', [(i, i ^ 1) for i in range(size)])  8.37 us
    ppermute x8, waiting for transfers between devices, swap_y(): return lax.ppermute(x, 'seq', [(i, i ^ 1) for i in range(size)])  6.06 us
    ppermute x4, starting transfers between devices, swap_x(): return lax.ppermute(x, 'pair', [(0, 1), (1, 0)])  5.14 us
    pallas_call x1, Pallas kernels, on_device(): pl.pallas_call(lambda *refs: middle_body(pieces, *refs), grid=(kv,), in_s...  3.96 us
    unnamed x6, local copies, waits for them, and re-layouts  3.43 us
    pallas_call x1, Pallas kernels, on_device(): pl.pallas_call(lambda *refs: query_backward_body(pieces, *refs), grid=(kv...  2.91 us
  transfers between devices with their start and end apart: 24, of which 7 were waited for; matrix products, arithmetic and copies ran while one was open for 7% of the time, Pallas kernels for 9%

profile of v4, /device:TPU:0, one launch (start us, length us, event | category | flops | bytes accessed | tf_op | source)
XLA Modules:
  0.0 69.6 jit_solution(7980274920045138494)
XLA Ops:
  0.6 0.8 %fusion.11 = (bf16[1,2,48,256]{3,2,1,0:T(8,128)(2,1)S(1)}, bf16[2,48,256]{2,1,0:T(8,128)(2,1)S(1)}) fusion(bf16[1,48,256]{2,1,0:T(8,128)(2,1)} %bitcast.73, bf16[1,48,256]{2,1,0:T(8,128)(2,1)} %bitcast.74), kind=kLoop, calls=%fused_computation.48 | loop fusion | flops 24576 | bytes 147456 | tf_op jit(solution)/shard_map/stack | solution.py:338
  1.4 4.1 %collective-permute-start.1 = (bf16[2,48,256]{2,1,0:T(8,128)(2,1)S(1)}, bf16[2,48,256]{2,1,0:T(8,128)(2,1)S(1)}, u32[]{:S(2)}, u32[]{:S(2)}) collective-permute-start(bf16[2,48,256]{2,1,0:T(8,128)(2,1)S(1)} %get-tuple-element.60), channel_id=1, source_target_pairs={{0,8},{2,10},{4,12},{6,14},{8,0},{10,2},{12,4},{14,6},{1,9},{3,11}... | collective-permute-start | bytes 147464 | tf_op jit(solution)/shard_map/ppermute | solution.py:328
  5.5 1.6 %collective-permute-start = (bf16[2,48,256]{2,1,0:T(8,128)(2,1)S(1)}, bf16[2,48,256]{2,1,0:T(8,128)(2,1)S(1)}, u32[]{:S(2)}, u32[]{:S(2)}) collective-permute-start(bf16[2,48,256]{2,1,0:T(8,128)(2,1)S(1)} %get-tuple-element.60), channel_id=1, source_target_pairs={{0,4},{2,6},{4,0},{6,2},{8,12},{10,14},{12,8},{14,10},{1,5},{3,7},... | collective-permute-start | bytes 147464 | tf_op jit(solution)/shard_map/ppermute | solution.py:328
  7.1 0.9 %copy_bitcast_fusion = (bf16[1,2,64,256]{3,2,1,0:T(8,128)(2,1)S(1)}, bf16[1,2,64,256]{3,2,1,0:T(8,128)(2,1)S(1)}) fusion(bf16[1,64,2,256]{3,2,1,0:T(2,128)(2,1)} %param.10, bf16[1,64,2,256]{3,2,1,0:T(2,128)(2,1)} %param.9), kind=kLoop, calls=%fused_computation.22 | loop fusion | bytes 262144 | tf_op jit(solution)/shard_map/stack | solution.py:337
  8.0 3.9 %collective-permute-start.8 = (bf16[2,2,64,256]{3,2,1,0:T(8,128)(2,1)S(1)}, bf16[2,2,64,256]{3,2,1,0:T(8,128)(2,1)S(1)}, u32[]{:S(2)}, u32[]{:S(2)}) collective-permute-start(bf16[2,2,64,256]{3,2,1,0:T(8,128)(2,1)S(1)} %pad_maximum_fusion.1.refs_6_.refs_7_), channel_id=1, source_target_pairs={{0,12},{2,14},{4,8},{6,10},{8,4},{10,6},{12,0},{14,2},{1,13},{3,15... | collective-permute-start | bytes 393224 | tf_op jit(solution)/shard_map/ppermute | solution.py:328
  12.0 0.1 broadcast_add_fusion
  12.0 0.1 iota_add_fusion.1
  12.1 0.1 add.180
  12.3 0.1 compare_select_fusion.refs_1_
  12.4 0.1 add.190
  12.5 0.7 collective-permute-start.6
  13.2 0.3 collective-permute-done.2
  13.5 1.6 %collective-permute-start.4 = (bf16[4,2,48,256]{3,2,1,0:T(8,128)(2,1)S(1)}, bf16[4,2,48,256]{3,2,1,0:T(8,128)(2,1)S(1)}, u32[]{:S(2)}, u32[]{:S(2)}) collective-permute-start(bf16[4,2,48,256]{3,2,1,0:T(8,128)(2,1)S(1)} %pad_maximum_fusion.pa_ref.rest_0_.refs_3_), channel_id=1, source_target_pairs={{0,16},{16,0},{1,17},{17,1},{2,18},{18,2},{3,19},{19,3},{4,20},{20... | collective-permute-start | bytes 589832 | tf_op jit(solution)/shard_map/ppermute | solution.py:334
  15.1 1.5 %collective-permute-start.3 = (bf16[4,2,48,256]{3,2,1,0:T(8,128)(2,1)S(1)}, bf16[4,2,48,256]{3,2,1,0:T(8,128)(2,1)S(1)}, u32[]{:S(2)}, u32[]{:S(2)}) collective-permute-start(bf16[4,2,48,256]{3,2,1,0:T(8,128)(2,1)S(1)} %pad_maximum_fusion.pa_ref.rest_0_.refs_3_), channel_id=1, source_target_pairs={{0,2},{2,0},{4,6},{6,4},{8,10},{10,8},{12,14},{14,12},{1,3},{3,1},... | collective-permute-start | bytes 589832 | tf_op jit(solution)/shard_map/ppermute | solution.py:331
  16.6 0.7 %compare_select_fusion.1 = f32[2,768]{1,0:T(2,128)S(1)} fusion(s32[768]{0:T(1024)S(1)} %add.190, s32[2]{0:T(128)} %bitcast.76), kind=kLoop, calls=%fused_computation.30 | loop fusion | flops 3072 | bytes 9224 | tf_op jit(solution)/shard_map/jit(_where)/select_n | solution.py:355
  17.4 0.6 collective-permute-start.9
  18.0 4.8 %collective-permute-done.7.refs_8_.refs_9_ = bf16[2,2,64,256]{3,2,1,0:T(8,128)(2,1)S(1)} collective-permute-done((bf16[2,2,64,256]{3,2,1,0:T(8,128)(2,1)S(1)}, bf16[2,2,64,256]{3,2,1,0:T(8,128)(2,1)S(1)}, u32[]{:S(2)}, u32[]{:S(2)}) %collective-permute-start.7) | collective-permute-done | bytes 131104 | tf_op jit(solution)/shard_map/ppermute | solution.py:328
  22.8 1.5 %collective-permute-start.12 = (bf16[2,2,64,256]{3,2,1,0:T(8,128)(2,1)S(1)}, bf16[2,2,64,256]{3,2,1,0:T(8,128)(2,1)S(1)}, u32[]{:S(2)}, u32[]{:S(2)}) collective-permute-start(bf16[2,2,64,256]{3,2,1,0:T(8,128)(2,1)S(1)} %collective-permute-done.8.refs_9_.refs_10_), channel_id=1, source_target_pairs={{0,2},{2,0},{4,6},{6,4},{8,10},{10,8},{12,14},{14,12},{1,3},{3,1},... | collective-permute-start | bytes 393224 | tf_op jit(solution)/shard_map/ppermute | solution.py:331
  24.4 0.5 collective-permute-start.11
  24.9 1.5 %collective-permute-start.10 = (bf16[2,2,64,256]{3,2,1,0:T(8,128)(2,1)S(1)}, bf16[2,2,64,256]{3,2,1,0:T(8,128)(2,1)S(1)}, u32[]{:S(2)}, u32[]{:S(2)}) collective-permute-start(bf16[2,2,64,256]{3,2,1,0:T(8,128)(2,1)S(1)} %collective-permute-done.6.refs_7_.refs_8_), channel_id=1, source_target_pairs={{0,2},{2,0},{4,6},{6,4},{8,10},{10,8},{12,14},{14,12},{1,3},{3,1},... | collective-permute-start | bytes 393224 | tf_op jit(solution)/shard_map/ppermute | solution.py:331
  26.4 1.5 %collective-permute-start.5 = (bf16[4,2,48,256]{3,2,1,0:T(8,128)(2,1)S(1)}, bf16[4,2,48,256]{3,2,1,0:T(8,128)(2,1)S(1)}, u32[]{:S(2)}, u32[]{:S(2)}) collective-permute-start(bf16[4,2,48,256]{3,2,1,0:T(8,128)(2,1)S(1)} %collective-permute-done.3.pb_ref.rest_1_.refs_4_), channel_id=1, source_target_pairs={{0,16},{16,0},{1,17},{17,1},{2,18},{18,2},{3,19},{19,3},{4,20},{20... | collective-permute-start | bytes 589832 | tf_op jit(solution)/shard_map/ppermute | solution.py:334
  27.9 0.7 %compare_select_fusion.6 = f32[2,64]{1,0:T(2,128)S(1)} fusion(s32[64]{0:T(128)S(1)} %iota_add_fusion.2, s32[2]{0:T(128)} %bitcast.75), kind=kLoop, calls=%fused_computation.40 | loop fusion | flops 256 | bytes 776 | tf_op jit(solution)/shard_map/jit(_where)/select_n | solution.py:362
  28.6 1.0 %copy-done = bf16[1,64,2,1792]{3,2,1,0:T(2,128)(2,1)S(1)} copy-done((bf16[1,64,2,1792]{3,2,1,0:T(2,128)(2,1)S(1)}, bf16[1,64,2,1792]{3,2,1,0:T(2,128)(2,1)}, u32[]{:S(2)}) %copy-start) | copy-done | bytes 458776
  29.6 1.0 %copy-done.1 = bf16[1,64,2,1792]{3,2,1,0:T(2,128)(2,1)S(1)} copy-done((bf16[1,64,2,1792]{3,2,1,0:T(2,128)(2,1)S(1)}, bf16[1,64,2,1792]{3,2,1,0:T(2,128)(2,1)}, u32[]{:S(2)}) %copy-start.1) | copy-done | bytes 458776
  30.7 0.9 %arrange.1 = (bf16[2,896,128]{2,1,0:T(8,128)(2,1)S(1)}, bf16[2,896,128]{2,1,0:T(8,128)(2,1)S(1)}) custom-call(bf16[1,64,2,1792]{3,2,1,0:T(2,128)(2,1)S(1)} %copy-done, bf16[1,64,2,1792]{3,2,1,0:T(2,128)(2,1)S(1)} %copy-done.1), custom_call_target="tpu_custom_call" | custom-call | flops 117440512 | bytes 4194304 | tf_op jit(solution)/shard_map/arrange/pallas_call | solution.py:386
  31.5 0.6 collective-permute-done.5.pd_ref.rest_3_.refs_6_
  32.1 2.5 %prefix_forward.1 = (bf16[2,896,768]{2,1,0:T(8,128)(2,1)S(1)}, f32[2,896,256]{2,1,0:T(8,128)S(1)}, f32[2,896,128]{2,1,0:T(8,128)S(1)}) custom-call(f32[2,8,768]{2,1,0:T(8,128)S(1)} %broadcast_in_dim.52.bias_ref, bf16[2,896,128]{2,1,0:T(8,128)(2,1)S(1)} %get-tuple-element.25.q_ref.refs_2_, bf16[4,2,48,256]{3,2,1,0:T(8,128)(2,1)S(1)} %pad_maximum_fusion.pa_ref.rest_0_.refs_3_, ...), custom_call_target="tpu_custom_call" | custom-call | flops 704643072 | bytes 8388608 | tf_op jit(solution)/shard_map/prefix_forward/pallas_call | solution.py:397
  34.6 0.1 broadcast_in_dim.47.refs_0_
  34.7 4.0 %middle.1 = (bf16[2,896,128]{2,1,0:T(8,128)(2,1)S(1)}, bf16[2,896,128]{2,1,0:T(8,128)(2,1)S(1)}, f32[2,896,128]{2,1,0:T(8,128)S(1)}, bf16[2,896,512]{2,1,0:T(8,1...) custom-call(f32[2,64,128]{2,1,0:T(8,128)S(1)} %broadcast_in_dim.47.r, ...), custom_call_target="tpu_custom_call" | custom-call | flops 1174405120 | bytes 12582912 | tf_op jit(solution)/shard_map/middle/pallas_call | solution.py:417
  38.6 2.2 %prefix_backward.1 = (bf16[2,896,768]{2,1,0:T(8,128)(2,1)S(1)}, bf16[2,384,256]{2,1,0:T(8,128)(2,1)S(1)}, bf16[2,192,256]{2,1,0:T(8,128)(2,1)S(1)}, bf16[2,192,256]{2,1,0:T(8,128)(2,1)S(1)}) custom-call(bf16[2,896,128]{2,1,0:T(8,128)(2,1)S(1)} %get-tuple-element.25.q_ref.refs_2_, bf16[2,896,768]{2,1,0:T(8,128)(2,1)S(1)} %get-tuple-element.30.p_ref, ...), custom_call_target="tpu_custom_call" | custom-call | flops 1056964608 | bytes 12582912 | tf_op jit(solution)/shard_map/prefix_backward/pallas_call | solution.py:452
  40.9 1.6 %collective-permute-start.19 = (bf16[2,192,256]{2,1,0:T(8,128)(2,1)S(1)}, bf16[2,192,256]{2,1,0:T(8,128)(2,1)S(1)}, u32[]{:S(2)}, u32[]{:S(2)}) collective-permute-start(bf16[2,192,256]{2,1,0:T(8,128)(2,1)S(1)} %get-tuple-element.43), channel_id=1, source_target_pairs={{0,16},{16,0},{1,17},{17,1},{2,18},{18,2},{3,19},{19,3},{4,20},{20... | collective-permute-start | bytes 589832 | tf_op jit(solution)/shard_map/ppermute | solution.py:334
  42.5 0.5 collective-permute-start.13
  43.0 1.5 %collective-permute-start.15 = (bf16[2,2,2,64,256]{4,3,2,1,0:T(8,128)(2,1)S(1)}, bf16[2,2,2,64,256]{4,3,2,1,0:T(8,128)(2,1)S(1)}, u32[]{:S(2)}, u32[]{:S(2)}) collective-permute-start(bf16[2,2,2,64,256]{4,3,2,1,0:T(8,128)(2,1)S(1)} %get-tuple-element.40), channel_id=1, source_target_pairs={{0,2},{2,0},{4,6},{6,4},{8,10},{10,8},{12,14},{14,12},{1,3},{3,1},... | collective-permute-start | bytes 786440 | tf_op jit(solution)/shard_map/ppermute | solution.py:331
  44.5 0.5 collective-permute-start.18
  45.0 2.9 %query_backward.1 = (bf16[1,64,2,1792]{3,2,1,0:T(2,128)(2,1)}, bf16[1,64,2,1792]{3,2,1,0:T(2,128)(2,1)}) custom-call(bf16[2,896,128]{2,1,0:T(8,128)(2,1)S(1)} %get-tuple-element.29.refs_0_, bf16[2,896,768]{2,1,0:T(8,128)(2,1)S(1)} %get-tuple-element.33.refs_1_, bf16[2,896,512]{2,1,0:T(8,128)(2,1)S(1)} %get-tuple-element.34.refs_2_, ...), custom_call_target="tpu_custom_call" | custom-call | flops 587202560 | bytes 8388608 | tf_op jit(solution)/shard_map/query_backward/pallas_call | solution.py:477
  48.0 0.6 collective-permute-start.20
  48.6 3.0 %collective-permute-done.13 = bf16[2,2,2,64,256]{4,3,2,1,0:T(8,128)(2,1)S(1)} collective-permute-done((bf16[2,2,2,64,256]{4,3,2,1,0:T(8,128)(2,1)S(1)}, bf16[2,2,2,64,256]{4,3,2,1,0:T(8,128)(2,1)S(1)}, u32[]{:S(2)}, u32[]{:S(2)}) %collective-permute-start.13) | collective-permute-done | bytes 262176 | tf_op jit(solution)/shard_map/ppermute | solution.py:331
  51.7 0.7 %collective-permute-start.14 = (bf16[2,2,64,256]{3,2,1,0:T(8,128)(2,1)S(1)}, bf16[2,2,64,256]{3,2,1,0:T(8,128)(2,1)S(1)}, u32[]{:S(2)}, u32[]{:S(2)}) collective-permute-start(bf16[2,2,64,256]{3,2,1,0:T(8,128)(2,1)S(1)} %fusion.4), channel_id=1, source_target_pairs={{0,4},{2,6},{4,0},{6,2},{8,12},{10,14},{12,8},{14,10},{1,5},{3,7},... | collective-permute-start | bytes 393224 | tf_op jit(solution)/shard_map/ppermute | solution.py:328
  52.5 3.0 %collective-permute-done.15 = bf16[2,2,2,64,256]{4,3,2,1,0:T(8,128)(2,1)S(1)} collective-permute-done((bf16[2,2,2,64,256]{4,3,2,1,0:T(8,128)(2,1)S(1)}, bf16[2,2,2,64,256]{4,3,2,1,0:T(8,128)(2,1)S(1)}, u32[]{:S(2)}, u32[]{:S(2)}) %collective-permute-start.15) | collective-permute-done | bytes 262176 | tf_op jit(solution)/shard_map/ppermute | solution.py:331
  55.6 3.5 %collective-permute-start.17 = (bf16[2,2,64,256]{3,2,1,0:T(8,128)(2,1)S(1)}, bf16[2,2,64,256]{3,2,1,0:T(8,128)(2,1)S(1)}, u32[]{:S(2)}, u32[]{:S(2)}) collective-permute-start(bf16[2,2,64,256]{3,2,1,0:T(8,128)(2,1)S(1)} %get-tuple-element.51), channel_id=1, source_target_pairs={{0,12},{2,14},{4,8},{6,10},{8,4},{10,6},{12,0},{14,2},{1,13},{3,15... | collective-permute-start | bytes 393224 | tf_op jit(solution)/shard_map/ppermute | solution.py:328
  59.2 0.1 collective-permute-start.21
  59.3 2.7 %collective-permute-start.23 = (bf16[2,48,256]{2,1,0:T(8,128)(2,1)S(1)}, bf16[2,48,256]{2,1,0:T(8,128)(2,1)S(1)}, u32[]{:S(2)}, u32[]{:S(2)}) collective-permute-start(bf16[2,48,256]{2,1,0:T(8,128)(2,1)S(1)} %get-tuple-element.53), channel_id=1, source_target_pairs={{0,12},{2,14},{4,8},{6,10},{8,4},{10,6},{12,0},{14,2},{1,13},{3,15... | collective-permute-start | bytes 147464 | tf_op jit(solution)/shard_map/ppermute | solution.py:328
  62.0 0.8 %collective-permute-start.22 = (bf16[2,48,256]{2,1,0:T(8,128)(2,1)S(1)}, bf16[2,48,256]{2,1,0:T(8,128)(2,1)S(1)}, u32[]{:S(2)}, u32[]{:S(2)}) collective-permute-start(bf16[2,48,256]{2,1,0:T(8,128)(2,1)S(1)} %get-tuple-element.54), channel_id=1, source_target_pairs={{0,8},{2,10},{4,12},{6,14},{8,0},{10,2},{12,4},{14,6},{1,9},{3,11}... | collective-permute-start | bytes 147464 | tf_op jit(solution)/shard_map/ppermute | solution.py:328
  62.8 3.7 %collective-permute-done.16 = bf16[2,2,64,256]{3,2,1,0:T(8,128)(2,1)S(1)} collective-permute-done((bf16[2,2,64,256]{3,2,1,0:T(8,128)(2,1)S(1)}, bf16[2,2,64,256]{3,2,1,0:T(8,128)(2,1)S(1)}, u32[]{:S(2)}, u32[]{:S(2)}) %collective-permute-start.16) | collective-permute-done | bytes 131104 | tf_op jit(solution)/shard_map/ppermute | solution.py:328
  66.6 0.7 %copy.19 = bf16[1,64,2,256]{3,2,1,0:T(2,128)(2,1)} copy(bf16[1,64,2,256]{3,1,2,0:T(8,128)(2,1)S(1)} %get-tuple-element.55) | data formatting | bytes 131072
  67.3 0.7 %copy.18 = bf16[1,64,2,256]{3,2,1,0:T(2,128)(2,1)} copy(bf16[1,64,2,256]{3,1,2,0:T(8,128)(2,1)S(1)} %get-tuple-element.56) | data formatting | bytes 131072
  68.0 1.0 %collective-permute-done.22 = bf16[2,48,256]{2,1,0:T(8,128)(2,1)S(1)} collective-permute-done((bf16[2,48,256]{2,1,0:T(8,128)(2,1)S(1)}, bf16[2,48,256]{2,1,0:T(8,128)(2,1)S(1)}, u32[]{:S(2)}, u32[]{:S(2)}) %collective-permute-start.22) | collective-permute-done | bytes 49184 | tf_op jit(solution)/shard_map/ppermute | solution.py:328
  69.0 0.6 slice_bitcast_fusion.6
  (41 shorter events, 0.7 us)
Async XLA Ops:
  1.4 11.1 %collective-permute-start.1 = (bf16[2,48,256]{2,1,0:T(8,128)(2,1)S(1)}, bf16[2,48,256]{2,1,0:T(8,128)(2,1)S(1)}, u32[]{:S(2)}, u32[]{:S(2)}) collective-permute-start(bf16[2,48,256]{2,1,0:T(8,128)(2,1)S(1)} %get-tuple-element.60), channel_id=1, source_target_pairs={{0,8},{2,10},{4,12},{6,14},{8,0},{10,2},{12,4},{14,6},{1,9},{3,11}... | collective-permute-start | bytes 147464 | tf_op jit(solution)/shard_map/ppermute | solution.py:328
  5.5 7.7 %collective-permute-start = (bf16[2,48,256]{2,1,0:T(8,128)(2,1)S(1)}, bf16[2,48,256]{2,1,0:T(8,128)(2,1)S(1)}, u32[]{:S(2)}, u32[]{:S(2)}) collective-permute-start(bf16[2,48,256]{2,1,0:T(8,128)(2,1)S(1)} %get-tuple-element.60), channel_id=1, source_target_pairs={{0,4},{2,6},{4,0},{6,2},{8,12},{10,14},{12,8},{14,10},{1,5},{3,7},... | collective-permute-start | bytes 147464 | tf_op jit(solution)/shard_map/ppermute | solution.py:328
  7.1 6.4 %collective-permute-start.2 = (bf16[2,48,256]{2,1,0:T(8,128)(2,1)S(1)}, bf16[2,48,256]{2,1,0:T(8,128)(2,1)S(1)}, u32[]{:S(2)}, u32[]{:S(2)}) collective-permute-start(bf16[2,48,256]{2,1,0:T(8,128)(2,1)S(1)} %get-tuple-element.60), channel_id=1, source_target_pairs={{0,12},{2,14},{4,8},{6,10},{8,4},{10,6},{12,0},{14,2},{1,13},{3,15... | collective-permute-start | bytes 147464 | tf_op jit(solution)/shard_map/ppermute | solution.py:328
  8.0 9.3 %collective-permute-start.8 = (bf16[2,2,64,256]{3,2,1,0:T(8,128)(2,1)S(1)}, bf16[2,2,64,256]{3,2,1,0:T(8,128)(2,1)S(1)}, u32[]{:S(2)}, u32[]{:S(2)}) collective-permute-start(bf16[2,2,64,256]{3,2,1,0:T(8,128)(2,1)S(1)} %pad_maximum_fusion.1.refs_6_.refs_7_), channel_id=1, source_target_pairs={{0,12},{2,14},{4,8},{6,10},{8,4},{10,6},{12,0},{14,2},{1,13},{3,15... | collective-permute-start | bytes 393224 | tf_op jit(solution)/shard_map/ppermute | solution.py:328
  11.9 10.9 %collective-permute-start.7 = (bf16[2,2,64,256]{3,2,1,0:T(8,128)(2,1)S(1)}, bf16[2,2,64,256]{3,2,1,0:T(8,128)(2,1)S(1)}, u32[]{:S(2)}, u32[]{:S(2)}) collective-permute-start(bf16[2,2,64,256]{3,2,1,0:T(8,128)(2,1)S(1)} %pad_maximum_fusion.1.refs_6_.refs_7_), channel_id=1, source_target_pairs={{0,8},{2,10},{4,12},{6,14},{8,0},{10,2},{12,4},{14,6},{1,9},{3,11}... | collective-permute-start | bytes 393224 | tf_op jit(solution)/shard_map/ppermute | solution.py:328
  12.5 11.9 %collective-permute-start.6 = (bf16[2,2,64,256]{3,2,1,0:T(8,128)(2,1)S(1)}, bf16[2,2,64,256]{3,2,1,0:T(8,128)(2,1)S(1)}, u32[]{:S(2)}, u32[]{:S(2)}) collective-permute-start(bf16[2,2,64,256]{3,2,1,0:T(8,128)(2,1)S(1)} %pad_maximum_fusion.1.refs_6_.refs_7_), channel_id=1, source_target_pairs={{0,4},{2,6},{4,0},{6,2},{8,12},{10,14},{12,8},{14,10},{1,5},{3,7},... | collective-permute-start | bytes 393224 | tf_op jit(solution)/shard_map/ppermute | solution.py:328
  13.5 11.3 %collective-permute-start.4 = (bf16[4,2,48,256]{3,2,1,0:T(8,128)(2,1)S(1)}, bf16[4,2,48,256]{3,2,1,0:T(8,128)(2,1)S(1)}, u32[]{:S(2)}, u32[]{:S(2)}) collective-permute-start(bf16[4,2,48,256]{3,2,1,0:T(8,128)(2,1)S(1)} %pad_maximum_fusion.pa_ref.rest_0_.refs_3_), channel_id=1, source_target_pairs={{0,16},{16,0},{1,17},{17,1},{2,18},{18,2},{3,19},{19,3},{4,20},{20... | collective-permute-start | bytes 589832 | tf_op jit(solution)/shard_map/ppermute | solution.py:334
  15.1 11.3 %collective-permute-start.3 = (bf16[4,2,48,256]{3,2,1,0:T(8,128)(2,1)S(1)}, bf16[4,2,48,256]{3,2,1,0:T(8,128)(2,1)S(1)}, u32[]{:S(2)}, u32[]{:S(2)}) collective-permute-start(bf16[4,2,48,256]{3,2,1,0:T(8,128)(2,1)S(1)} %pad_maximum_fusion.pa_ref.rest_0_.refs_3_), channel_id=1, source_target_pairs={{0,2},{2,0},{4,6},{6,4},{8,10},{10,8},{12,14},{14,12},{1,3},{3,1},... | collective-permute-start | bytes 589832 | tf_op jit(solution)/shard_map/ppermute | solution.py:331
  17.4 17.2 %collective-permute-start.9 = (bf16[2,2,64,256]{3,2,1,0:T(8,128)(2,1)S(1)}, bf16[2,2,64,256]{3,2,1,0:T(8,128)(2,1)S(1)}, u32[]{:S(2)}, u32[]{:S(2)}) collective-permute-start(bf16[2,2,64,256]{3,2,1,0:T(8,128)(2,1)S(1)} %pad_maximum_fusion.1.refs_6_.refs_7_), channel_id=1, source_target_pairs={{0,2},{2,0},{4,6},{6,4},{8,10},{10,8},{12,14},{14,12},{1,3},{3,1},... | collective-permute-start | bytes 393224 | tf_op jit(solution)/shard_map/ppermute | solution.py:331
  22.8 11.7 %collective-permute-start.12 = (bf16[2,2,64,256]{3,2,1,0:T(8,128)(2,1)S(1)}, bf16[2,2,64,256]{3,2,1,0:T(8,128)(2,1)S(1)}, u32[]{:S(2)}, u32[]{:S(2)}) collective-permute-start(bf16[2,2,64,256]{3,2,1,0:T(8,128)(2,1)S(1)} %collective-permute-done.8.refs_9_.refs_10_), channel_id=1, source_target_pairs={{0,2},{2,0},{4,6},{6,4},{8,10},{10,8},{12,14},{14,12},{1,3},{3,1},... | collective-permute-start | bytes 393224 | tf_op jit(solution)/shard_map/ppermute | solution.py:331
  24.4 10.2 %collective-permute-start.11 = (bf16[2,2,64,256]{3,2,1,0:T(8,128)(2,1)S(1)}, bf16[2,2,64,256]{3,2,1,0:T(8,128)(2,1)S(1)}, u32[]{:S(2)}, u32[]{:S(2)}) collective-permute-start(bf16[2,2,64,256]{3,2,1,0:T(8,128)(2,1)S(1)} %collective-permute-done.7.refs_8_.refs_9_), channel_id=1, source_target_pairs={{0,2},{2,0},{4,6},{6,4},{8,10},{10,8},{12,14},{14,12},{1,3},{3,1},... | collective-permute-start | bytes 393224 | tf_op jit(solution)/shard_map/ppermute | solution.py:331
  24.9 9.7 %collective-permute-start.10 = (bf16[2,2,64,256]{3,2,1,0:T(8,128)(2,1)S(1)}, bf16[2,2,64,256]{3,2,1,0:T(8,128)(2,1)S(1)}, u32[]{:S(2)}, u32[]{:S(2)}) collective-permute-start(bf16[2,2,64,256]{3,2,1,0:T(8,128)(2,1)S(1)} %collective-permute-done.6.refs_7_.refs_8_), channel_id=1, source_target_pairs={{0,2},{2,0},{4,6},{6,4},{8,10},{10,8},{12,14},{14,12},{1,3},{3,1},... | collective-permute-start | bytes 393224 | tf_op jit(solution)/shard_map/ppermute | solution.py:331
  26.4 5.7 %collective-permute-start.5 = (bf16[4,2,48,256]{3,2,1,0:T(8,128)(2,1)S(1)}, bf16[4,2,48,256]{3,2,1,0:T(8,128)(2,1)S(1)}, u32[]{:S(2)}, u32[]{:S(2)}) collective-permute-start(bf16[4,2,48,256]{3,2,1,0:T(8,128)(2,1)S(1)} %collective-permute-done.3.pb_ref.rest_1_.refs_4_), channel_id=1, source_target_pairs={{0,16},{16,0},{1,17},{17,1},{2,18},{18,2},{3,19},{19,3},{4,20},{20... | collective-permute-start | bytes 589832 | tf_op jit(solution)/shard_map/ppermute | solution.py:334
  28.6 1.0 %copy-start = (bf16[1,64,2,1792]{3,2,1,0:T(2,128)(2,1)S(1)}, bf16[1,64,2,1792]{3,2,1,0:T(2,128)(2,1)}, u32[]{:S(2)}) copy-start(bf16[1,64,2,1792]{3,2,1,0:T(2,128)(2,1)} %raw_q_ref.1) | copy-start | bytes 1376260
  29.6 1.0 %copy-start.1 = (bf16[1,64,2,1792]{3,2,1,0:T(2,128)(2,1)S(1)}, bf16[1,64,2,1792]{3,2,1,0:T(2,128)(2,1)}, u32[]{:S(2)}) copy-start(bf16[1,64,2,1792]{3,2,1,0:T(2,128)(2,1)} %raw_do_ref.1) | copy-start | bytes 1376260
  40.9 7.0 %collective-permute-start.19 = (bf16[2,192,256]{2,1,0:T(8,128)(2,1)S(1)}, bf16[2,192,256]{2,1,0:T(8,128)(2,1)S(1)}, u32[]{:S(2)}, u32[]{:S(2)}) collective-permute-start(bf16[2,192,256]{2,1,0:T(8,128)(2,1)S(1)} %get-tuple-element.43), channel_id=1, source_target_pairs={{0,16},{16,0},{1,17},{17,1},{2,18},{18,2},{3,19},{19,3},{4,20},{20... | collective-permute-start | bytes 589832 | tf_op jit(solution)/shard_map/ppermute | solution.py:334
  42.5 9.2 %collective-permute-start.13 = (bf16[2,2,2,64,256]{4,3,2,1,0:T(8,128)(2,1)S(1)}, bf16[2,2,2,64,256]{4,3,2,1,0:T(8,128)(2,1)S(1)}, u32[]{:S(2)}, u32[]{:S(2)}) collective-permute-start(bf16[2,2,2,64,256]{4,3,2,1,0:T(8,128)(2,1)S(1)} %get-tuple-element.38), channel_id=1, source_target_pairs={{0,2},{2,0},{4,6},{6,4},{8,10},{10,8},{12,14},{14,12},{1,3},{3,1},... | collective-permute-start | bytes 786440 | tf_op jit(solution)/shard_map/ppermute | solution.py:331
  43.0 12.5 %collective-permute-start.15 = (bf16[2,2,2,64,256]{4,3,2,1,0:T(8,128)(2,1)S(1)}, bf16[2,2,2,64,256]{4,3,2,1,0:T(8,128)(2,1)S(1)}, u32[]{:S(2)}, u32[]{:S(2)}) collective-permute-start(bf16[2,2,2,64,256]{4,3,2,1,0:T(8,128)(2,1)S(1)} %get-tuple-element.40), channel_id=1, source_target_pairs={{0,2},{2,0},{4,6},{6,4},{8,10},{10,8},{12,14},{14,12},{1,3},{3,1},... | collective-permute-start | bytes 786440 | tf_op jit(solution)/shard_map/ppermute | solution.py:331
  44.5 14.6 %collective-permute-start.18 = (bf16[2,192,256]{2,1,0:T(8,128)(2,1)S(1)}, bf16[2,192,256]{2,1,0:T(8,128)(2,1)S(1)}, u32[]{:S(2)}, u32[]{:S(2)}) collective-permute-start(bf16[2,192,256]{2,1,0:T(8,128)(2,1)S(1)} %get-tuple-element.41), channel_id=1, source_target_pairs={{0,16},{16,0},{1,17},{17,1},{2,18},{18,2},{3,19},{19,3},{4,20},{20... | collective-permute-start | bytes 589832 | tf_op jit(solution)/shard_map/ppermute | solution.py:334
  48.0 11.1 %collective-permute-start.20 = (bf16[2,192,256]{2,1,0:T(8,128)(2,1)S(1)}, bf16[2,192,256]{2,1,0:T(8,128)(2,1)S(1)}, u32[]{:S(2)}, u32[]{:S(2)}) collective-permute-start(bf16[2,192,256]{2,1,0:T(8,128)(2,1)S(1)} %add_convert_fusion.1), channel_id=1, source_target_pairs={{0,2},{2,0},{4,6},{6,4},{8,10},{10,8},{12,14},{14,12},{1,3},{3,1},... | collective-permute-start | bytes 589832 | tf_op jit(solution)/shard_map/ppermute | solution.py:331
  51.7 10.2 %collective-permute-start.14 = (bf16[2,2,64,256]{3,2,1,0:T(8,128)(2,1)S(1)}, bf16[2,2,64,256]{3,2,1,0:T(8,128)(2,1)S(1)}, u32[]{:S(2)}, u32[]{:S(2)}) collective-permute-start(bf16[2,2,64,256]{3,2,1,0:T(8,128)(2,1)S(1)} %fusion.4), channel_id=1, source_target_pairs={{0,4},{2,6},{4,0},{6,2},{8,12},{10,14},{12,8},{14,10},{1,5},{3,7},... | collective-permute-start | bytes 393224 | tf_op jit(solution)/shard_map/ppermute | solution.py:328
  55.6 11.0 %collective-permute-start.16 = (bf16[2,2,64,256]{3,2,1,0:T(8,128)(2,1)S(1)}, bf16[2,2,64,256]{3,2,1,0:T(8,128)(2,1)S(1)}, u32[]{:S(2)}, u32[]{:S(2)}) collective-permute-start(bf16[2,2,64,256]{3,2,1,0:T(8,128)(2,1)S(1)} %get-tuple-element.50), channel_id=1, source_target_pairs={{0,8},{2,10},{4,12},{6,14},{8,0},{10,2},{12,4},{14,6},{1,9},{3,11}... | collective-permute-start | bytes 393224 | tf_op jit(solution)/shard_map/ppermute | solution.py:328
  55.6 10.9 %collective-permute-start.17 = (bf16[2,2,64,256]{3,2,1,0:T(8,128)(2,1)S(1)}, bf16[2,2,64,256]{3,2,1,0:T(8,128)(2,1)S(1)}, u32[]{:S(2)}, u32[]{:S(2)}) collective-permute-start(bf16[2,2,64,256]{3,2,1,0:T(8,128)(2,1)S(1)} %get-tuple-element.51), channel_id=1, source_target_pairs={{0,12},{2,14},{4,8},{6,10},{8,4},{10,6},{12,0},{14,2},{1,13},{3,15... | collective-permute-start | bytes 393224 | tf_op jit(solution)/shard_map/ppermute | solution.py:328
  59.2 8.8 %collective-permute-start.21 = (bf16[2,48,256]{2,1,0:T(8,128)(2,1)S(1)}, bf16[2,48,256]{2,1,0:T(8,128)(2,1)S(1)}, u32[]{:S(2)}, u32[]{:S(2)}) collective-permute-start(bf16[2,48,256]{2,1,0:T(8,128)(2,1)S(1)} %get-tuple-element.52), channel_id=1, source_target_pairs={{0,4},{2,6},{4,0},{6,2},{8,12},{10,14},{12,8},{14,10},{1,5},{3,7},... | collective-permute-start | bytes 147464 | tf_op jit(solution)/shard_map/ppermute | solution.py:328
  59.3 8.7 %collective-permute-start.23 = (bf16[2,48,256]{2,1,0:T(8,128)(2,1)S(1)}, bf16[2,48,256]{2,1,0:T(8,128)(2,1)S(1)}, u32[]{:S(2)}, u32[]{:S(2)}) collective-permute-start(bf16[2,48,256]{2,1,0:T(8,128)(2,1)S(1)} %get-tuple-element.53), channel_id=1, source_target_pairs={{0,12},{2,14},{4,8},{6,10},{8,4},{10,6},{12,0},{14,2},{1,13},{3,15... | collective-permute-start | bytes 147464 | tf_op jit(solution)/shard_map/ppermute | solution.py:328
  62.0 7.0 %collective-permute-start.22 = (bf16[2,48,256]{2,1,0:T(8,128)(2,1)S(1)}, bf16[2,48,256]{2,1,0:T(8,128)(2,1)S(1)}, u32[]{:S(2)}, u32[]{:S(2)}) collective-permute-start(bf16[2,48,256]{2,1,0:T(8,128)(2,1)S(1)} %get-tuple-element.54), channel_id=1, source_target_pairs={{0,8},{2,10},{4,12},{6,14},{8,0},{10,2},{12,4},{14,6},{1,9},{3,11}... | collective-permute-start | bytes 147464 | tf_op jit(solution)/shard_map/ppermute | solution.py:328
